TPU v7x, 32 devices: a whole 2x2x4 slice. The times are simulated.
32 devices in a mesh: role: 2 (over y), gx: 4 (over z), gy: 4 (over x, core).
Axes of the slice: x: 2, y: 2, z: 4, core: 2. Of those that a mesh axis runs over, the one named last changes fastest.
Arguments:
- design: float32 [64, 128, 256], P(('gx', 'gy'), None, 'role'), may hold values from 0 to 1
- force: float32 [3, 32, 64, 256], P(None, 'gx', 'gy', 'role'), may hold values from -6 to 6
- clamped_dof_mask: int32 [3, 32, 64, 256], P(None, 'gx', 'gy', 'role'), may hold values 0 or 1
- stiffness: float32 [81, 81], replicated, may hold values from -1 to 70, as said below
Outputs:
- sensitivity: float32 [64, 128, 256], P(('gx', 'gy'), None, 'role')
- displacement: float32 [3, 32, 64, 256], P(None, 'gx', 'gy', 'role')
Inputs may be any that keep to these rules, and one draw needn't show every extreme that they name: `stiffness`: symmetric, and each diagonal entry exceeds the sum of the magnitudes of the other entries of its row.
All inputs are finite; a program needn't handle non-finite values. No bound on the sum of `clamped_dof_mask` on one device may be relied on, other than what follows from the above.
Results may differ from a plain program's by a relative error of at most 0.00013.
Values sent between devices are 32-bit elements; how exact they have to be, the bound alone decides.
No kernel may reach another device: no remote copies, remote signals or barrier semaphores. Data moves between devices by JAX's collectives and lax.ppermute only.
A program may use at most 64 MiB of HBM per device.

v0:
```python
import jax
import jax.numpy as jnp
from jax import lax
from jax.sharding import PartitionSpec as P

ITERS = 3
RADIUS = 2


sharpness = 4.0
threshold = 0.5
floor_stiff = 0.001


def with_halo(block, sides, width):
    for axis, dim in sides:
        count = lax.axis_size(axis)
        forward = [(i, i + 1) for i in range(count - 1)]
        backward = [(target, source) for source, target in forward]
        low = lax.ppermute(
            lax.slice_in_dim(block, block.shape[dim] - width, None, axis=dim), axis, forward
        )
        high = lax.ppermute(lax.slice_in_dim(block, 0, width, axis=dim), axis, backward)
        block = jnp.concatenate([low, block, high], axis=dim)
    return block


def hat_list():
    return [float(RADIUS + 1 - abs(shift_idx - RADIUS)) for shift_idx in range(2 * RADIUS + 1)]


def smooth_axis(padded, axis_num, length):
    result = None
    for offset_idx, weight in enumerate(hat_list()):
        portion = weight * lax.slice_in_dim(padded, offset_idx, offset_idx + length, axis=axis_num)
        result = portion if result is None else result + portion
    return result


def axis_count(start, length, extent):
    places = start + jnp.arange(length, dtype=jnp.int32)
    counted = jnp.zeros((length,), jnp.float32)
    for offset_idx, weight in enumerate(hat_list()):
        target = places + (offset_idx - RADIUS)
        inside = jnp.logical_and(target >= 0, target < extent)
        counted = counted + weight * inside.astype(jnp.float32)
    return counted


def slab_weight(shape):
    extent_x, extent_y, extent_z = shape
    along_x = axis_count(
        lax.axis_index(("gx", "gy")) * extent_x, extent_x, extent_x * lax.axis_size(("gx", "gy"))
    )
    along_y = axis_count(0, extent_y, extent_y)
    along_z = axis_count(
        lax.axis_index("role") * extent_z, extent_z, extent_z * lax.axis_size("role")
    )
    return along_x[:, None, None] * along_y[None, :, None] * along_z[None, None, :]


def slab_smooth(field):
    extent_x, extent_y, extent_z = field.shape
    padded = with_halo(field, (("role", 2), (("gx", "gy"), 0)), RADIUS)
    padded = jnp.pad(padded, ((0, 0), (RADIUS, RADIUS), (0, 0)))
    return smooth_axis(smooth_axis(smooth_axis(padded, 2, extent_z), 1, extent_y), 0, extent_x)


def heaviside_projection(values):
    scaled = jnp.tanh(sharpness * threshold) + jnp.tanh(sharpness * (1.0 - threshold))
    return (jnp.tanh(sharpness * threshold) + jnp.tanh(sharpness * (values - threshold))) / scaled


def slope(values):
    scaled = jnp.tanh(sharpness * threshold) + jnp.tanh(sharpness * (1.0 - threshold))
    bent = jnp.tanh(sharpness * (values - threshold))
    return sharpness * (1.0 - bent * bent) / scaled


def element_mean(fine):
    count_x = fine.shape[0] // 4
    count_y = fine.shape[1] // 4
    count_z = fine.shape[2] // 2
    return fine.reshape(count_x, 4, count_y, 4, count_z, 2).mean(axis=(1, 3, 5))


def spread(elements):
    count_x, count_y, count_z = elements.shape
    widened = jnp.broadcast_to(
        elements[:, None, :, None, :, None], (count_x, 4, count_y, 4, count_z, 2)
    )
    return widened.reshape(4 * count_x, 4 * count_y, 2 * count_z)


def corner_table(node_len):
    elem_len = (node_len - 1) // 2
    nodes = jnp.arange(node_len, dtype=jnp.int32)[None, :, None]
    elems = jnp.arange(elem_len, dtype=jnp.int32)[None, None, :]
    corners = jnp.arange(3, dtype=jnp.int32)[:, None, None]
    return (nodes == 2 * elems + corners).astype(jnp.float32)


def fold_table(node_len):
    rows = jnp.arange(node_len + 2, dtype=jnp.int32)[:, None]
    cols = jnp.arange(node_len, dtype=jnp.int32)[None, :]
    target = jnp.clip(rows - 1, 0, node_len - 1)
    return (target == cols).astype(jnp.float32)


def split_axis(values, axis_num):
    half_len = (values.shape[axis_num] - 1) // 2
    pieces = [
        lax.slice_in_dim(values, corner, corner + 2 * half_len - 1, stride=2, axis=axis_num)
        for corner in range(3)
    ]
    return jnp.stack(pieces, axis=0)


def split_nodes(values):
    stacked = split_axis(values, 1)
    stacked = split_axis(stacked, 3)
    table = corner_table(values.shape[3])
    stacked = jnp.einsum(
        "baqxyk,ckg->cbaqxyg",
        stacked,
        table,
        precision=lax.Precision.HIGHEST,
        preferred_element_type=jnp.float32,
    )
    return stacked.reshape(81, -1)


def merge_axis(parts, axis_num):
    opening = parts[0]
    middle = parts[1]
    closing = parts[2]
    length = opening.shape[axis_num]
    before = [(0, 0)] * opening.ndim
    before[axis_num] = (0, 1)
    behind = [(0, 0)] * opening.ndim
    behind[axis_num] = (1, 0)
    evens = jnp.pad(opening, before) + jnp.pad(closing, behind)
    leading = lax.slice_in_dim(evens, 0, length, axis=axis_num)
    ending = lax.slice_in_dim(evens, length, length + 1, axis=axis_num)
    braided = jnp.stack([leading, middle], axis=axis_num + 1)
    new_shape = list(leading.shape)
    new_shape[axis_num] = 2 * length
    return jnp.concatenate([braided.reshape(new_shape), ending], axis=axis_num)


def merge_nodes(stiffness_product, element_shape):
    reshaped = stiffness_product.reshape((3, 3, 3, 3) + tuple(element_shape))
    table = corner_table(2 * element_shape[2] + 1)
    merged = jnp.einsum(
        "cbaqxyg,ckg->baqxyk",
        reshaped,
        table,
        precision=lax.Precision.HIGHEST,
        preferred_element_type=jnp.float32,
    )
    merged = merge_axis(merged, 3)
    return merge_axis(merged, 1)


def fold_axis(padded, axis_num):
    inner_len = padded.shape[axis_num] - 2
    below = lax.slice_in_dim(padded, 0, 1, axis=axis_num)
    above = lax.slice_in_dim(padded, inner_len + 1, inner_len + 2, axis=axis_num)
    lowest = lax.slice_in_dim(padded, 1, 2, axis=axis_num) + below
    highest = lax.slice_in_dim(padded, inner_len, inner_len + 1, axis=axis_num) + above
    centre = lax.slice_in_dim(padded, 2, inner_len, axis=axis_num)
    return jnp.concatenate([lowest, centre, highest], axis=axis_num)


def shared_sum(values):
    padded = with_halo(values, (("role", 3), ("gx", 1), ("gy", 2)), 1)
    folded = fold_axis(fold_axis(padded, 1), 2)
    table = fold_table(values.shape[3])
    return jnp.einsum(
        "qxyk,kn->qxyn",
        folded,
        table,
        precision=lax.Precision.HIGHEST,
        preferred_element_type=jnp.float32,
    )


def inner_sum(left, right):
    local_part = jnp.sum((left * right)[:, :-1, :-1, :-1])
    return lax.psum(local_part, ("role", "gx", "gy"))


def conjugate_gradient_solve(operate, rhs):
    solution = jnp.zeros_like(rhs)
    residual = rhs
    direction = rhs
    current = inner_sum(residual, residual)
    for sweep in range(ITERS):
        applied = operate(direction)
        step_len = current / inner_sum(direction, applied)
        solution = solution + step_len * direction
        residual = residual - step_len * applied
        updated = inner_sum(residual, residual)
        direction = residual + updated / current * direction
        current = updated
    return solution


def on_device(design, force, clamped_dof_mask, stiffness):
    filter_weight_grid = slab_weight(design.shape)
    filtered = slab_smooth(design) / filter_weight_grid
    density_slab = element_mean(heaviside_projection(filtered))
    density = lax.all_to_all(density_slab, "gy", split_axis=1, concat_axis=0, tiled=True)
    factor = floor_stiff + (1.0 - floor_stiff) * density**3
    behind = ((0, 0), (0, 1), (0, 1), (0, 1))
    owned = jnp.concatenate([force, (1 - clamped_dof_mask).astype(jnp.float32)], axis=0)
    shared = shared_sum(jnp.pad(owned, behind))
    free = shared[3:]
    rhs = free * shared[:3]
    scales = factor.reshape(-1)

    def operate(values):
        columns = split_nodes(free * values)
        stiffness_product = (
            jnp.dot(
                stiffness,
                columns,
                precision=lax.Precision.HIGHEST,
                preferred_element_type=jnp.float32,
            )
            * scales[None, :]
        )
        return free * shared_sum(merge_nodes(stiffness_product, factor.shape))

    solution = conjugate_gradient_solve(operate, rhs)
    columns = split_nodes(solution)
    energy = jnp.sum(
        columns
        * jnp.dot(
            stiffness, columns, precision=lax.Precision.HIGHEST, preferred_element_type=jnp.float32
        ),
        axis=0,
    ).reshape(factor.shape)
    element_grad = -3.0 * density**2 * (1.0 - floor_stiff) * energy / 32.0
    slab_grad = lax.all_to_all(element_grad, "gy", split_axis=0, concat_axis=1, tiled=True)
    voxel_grad = spread(slab_grad) * slope(filtered)
    sensitivity = slab_smooth(voxel_grad / filter_weight_grid)
    return (sensitivity, solution[:, :-1, :-1, :-1])


def solution(mesh):
    placed = (
        P(("gx", "gy"), None, "role"),
        P(None, "gx", "gy", "role"),
        P(None, "gx", "gy", "role"),
        P(),
    )
    return jax.shard_map(
        on_device,
        mesh=mesh,
        in_specs=placed,
        out_specs=(P(("gx", "gy"), None, "role"), P(None, "gx", "gy", "role")),
        check_vma=False,
    )
```

profile of v0, /device:TPU:3, one launch (start us, length us, event | category | flops | bytes accessed | tf_op | source)
XLA Modules:
  0.0 500.0 jit_solution(17376885833993922380)
XLA Ops:
  0.7 3.3 collective-permute-start.4
  11.9 4.9 collective-permute-done.5
  17.4 3.2 collective-permute-start.6
  22.7 3.8 collective-permute-done.7
  28.2 5.8 %collective-permute-start.9 = (f32[6,11,1,131]{3,2,1,0:T(1,128)S(1)}, f32[6,11,1,131]{3,2,1,0:T(1,128)S(1)}, u32[]{:S(2)}, u32[]{:S(2)}) collective-permute-start(f32[6,11,1,131]{3,2,1,0:T(1,128)S(1)} %get-tuple-element.15), channel_id=1, source_target_pairs={{1,0},{2,1},{3,2},{5,4},{6,5},{7,6},{9,8},{10,9},{11,10},{13,12},{... | collective-permute-start | bytes 103760 | tf_op jit(solution)/shard_map/ppermute | solution.py:23
  36.8 3.6 collective-permute-start.3
  44.1 5.5 %slice.538 = f32[3,3,4,8,129]{4,3,2,1,0:T(8,128)} slice(f32[3,3,4,17,129]{4,3,2,1,0:T(8,128)} %pad_maximum_fusion.2), slice={[0:3:1], [0:3:1], [0:4:1], [2:17:2], [0:129:1]} | slice | bytes 297216 | tf_op jit(solution)/shard_map/slice | solution.py:113
  49.6 5.2 %slice.537 = f32[3,3,4,8,129]{4,3,2,1,0:T(8,128)} slice(f32[3,3,4,17,129]{4,3,2,1,0:T(8,128)} %pad_maximum_fusion.2), slice={[0:3:1], [0:3:1], [0:4:1], [1:16:2], [0:129:1]} | slice | bytes 297216 | tf_op jit(solution)/shard_map/slice | solution.py:113
  54.9 5.3 %slice.536 = f32[3,3,4,8,129]{4,3,2,1,0:T(8,128)} slice(f32[3,3,4,17,129]{4,3,2,1,0:T(8,128)} %pad_maximum_fusion.2), slice={[0:3:1], [0:3:1], [0:4:1], [0:15:2], [0:129:1]} | slice | bytes 297216 | tf_op jit(solution)/shard_map/slice | solution.py:113
  63.3 3.5 reduce_sum.80
  70.6 4.9 all-to-all-start
  81.0 2.8 fusion
  89.9 5.5 %collective-permute-done.10 = f32[3,9,17,1]{3,2,1,0:T(8,128)S(1)} collective-permute-done((f32[3,9,17,1]{3,2,1,0:T(8,128)S(1)}, f32[3,9,17,1]{3,2,1,0:T(8,128)S(1)}, u32[]{:S(2)}, u32[]{:S(2)}) %collective-permute-start.10) | collective-permute-done | bytes 1868 | tf_op jit(solution)/shard_map/ppermute | solution.py:20
  95.4 3.9 collective-permute-done.11
  99.4 3.2 collective-permute-start.12
  104.0 3.7 collective-permute-done.13
  109.2 5.4 %collective-permute-start.15 = (f32[3,11,1,131]{3,2,1,0:T(1,128)S(1)}, f32[3,11,1,131]{3,2,1,0:T(1,128)S(1)}, u32[]{:S(2)}, u32[]{:S(2)}) collective-permute-start(f32[3,11,1,131]{3,2,1,0:T(1,128)S(1)} %get-tuple-element.23), channel_id=1, source_target_pairs={{1,0},{2,1},{3,2},{5,4},{6,5},{7,6},{9,8},{10,9},{11,10},{13,12},{... | collective-permute-start | bytes 51884 | tf_op jit(solution)/shard_map/ppermute | solution.py:23
  117.4 41.7 %all-reduce.15 = (f32[]{:T(128)}, f32[]{:T(128)}) all-reduce(f32[]{:T(128)} %get-tuple-element.3, f32[]{:T(128)} %get-tuple-element.2), channel_id=1, replica_groups=mesh['role'=2,'gx'=4,'gy'=4] {'role','gx','gy'}, use_global_device_ids=true, to_apply=%region_3.4 | all-reduce | flops 2 | bytes 16 | tf_op jit(solution)/shard_map/psum | solution.py:190
  161.2 39.4 %psum.44 = f32[]{:T(128)} all-reduce(f32[]{:T(128)} %fusion.89), channel_id=1, replica_groups=mesh['role'=2,'gx'=4,'gy'=4] {'role','gx','gy'}, use_global_device_ids=true, to_apply=%region_7.8 | all-reduce | flops 1 | bytes 8 | tf_op jit(solution)/shard_map/psum | solution.py:190
  204.2 5.5 %slice.572 = f32[3,3,4,8,129]{4,3,2,1,0:T(8,128)} slice(f32[3,3,4,17,129]{4,3,2,1,0:T(8,128)} %pad_maximum_fusion.3), slice={[0:3:1], [0:3:1], [0:4:1], [2:17:2], [0:129:1]} | slice | bytes 297216 | tf_op jit(solution)/shard_map/slice | solution.py:113
  209.7 5.3 %slice.571 = f32[3,3,4,8,129]{4,3,2,1,0:T(8,128)} slice(f32[3,3,4,17,129]{4,3,2,1,0:T(8,128)} %pad_maximum_fusion.3), slice={[0:3:1], [0:3:1], [0:4:1], [1:16:2], [0:129:1]} | slice | bytes 297216 | tf_op jit(solution)/shard_map/slice | solution.py:113
  214.9 5.2 %slice.570 = f32[3,3,4,8,129]{4,3,2,1,0:T(8,128)} slice(f32[3,3,4,17,129]{4,3,2,1,0:T(8,128)} %pad_maximum_fusion.3), slice={[0:3:1], [0:3:1], [0:4:1], [0:15:2], [0:129:1]} | slice | bytes 297216 | tf_op jit(solution)/shard_map/slice | solution.py:113
  220.2 3.1 convolution_bitcast_fusion.3
  225.9 2.8 fusion.1
  228.7 2.7 reshape.257
  238.3 3.5 collective-permute-start.16
  243.2 4.8 collective-permute-done.16
  247.9 3.9 collective-permute-done.17
  251.9 3.4 collective-permute-start.18
  256.7 3.7 collective-permute-done.19
  261.9 6.1 %collective-permute-start.21 = (f32[3,11,1,131]{3,2,1,0:T(1,128)S(1)}, f32[3,11,1,131]{3,2,1,0:T(1,128)S(1)}, u32[]{:S(2)}, u32[]{:S(2)}) collective-permute-start(f32[3,11,1,131]{3,2,1,0:T(1,128)S(1)} %get-tuple-element.21), channel_id=1, source_target_pairs={{1,0},{2,1},{3,2},{5,4},{6,5},{7,6},{9,8},{10,9},{11,10},{13,12},{... | collective-permute-start | bytes 51884 | tf_op jit(solution)/shard_map/ppermute | solution.py:23
  271.7 40.7 %psum.45 = f32[]{:T(128)} all-reduce(f32[]{:T(128)} %fusion.88), channel_id=1, replica_groups=mesh['role'=2,'gx'=4,'gy'=4] {'role','gx','gy'}, use_global_device_ids=true, to_apply=%region_9.10 | all-reduce | flops 1 | bytes 8 | tf_op jit(solution)/shard_map/psum | solution.py:190
  316.6 40.1 %psum.46 = f32[]{:T(128)} all-reduce(f32[]{:T(128)} %fusion.87), channel_id=1, replica_groups=mesh['role'=2,'gx'=4,'gy'=4] {'role','gx','gy'}, use_global_device_ids=true, to_apply=%region_11.12 | all-reduce | flops 1 | bytes 8 | tf_op jit(solution)/shard_map/psum | solution.py:190
  359.5 3.2 slice.606
  362.7 3.1 slice.605
  365.8 3.1 slice.604
  382.6 3.5 collective-permute-start.22
  387.4 4.8 collective-permute-done.22
  392.2 3.9 collective-permute-done.23
  399.8 3.7 collective-permute-done.25
  405.1 6.1 %collective-permute-start.27 = (f32[3,11,1,131]{3,2,1,0:T(1,128)S(1)}, f32[3,11,1,131]{3,2,1,0:T(1,128)S(1)}, u32[]{:S(2)}, u32[]{:S(2)}) collective-permute-start(f32[3,11,1,131]{3,2,1,0:T(1,128)S(1)} %get-tuple-element.19), channel_id=1, source_target_pairs={{1,0},{2,1},{3,2},{5,4},{6,5},{7,6},{9,8},{10,9},{11,10},{13,12},{... | collective-permute-start | bytes 51884 | tf_op jit(solution)/shard_map/ppermute | solution.py:23
  414.9 40.7 %psum.47 = f32[]{:T(128)} all-reduce(f32[]{:T(128)} %fusion.86), channel_id=1, replica_groups=mesh['role'=2,'gx'=4,'gy'=4] {'role','gx','gy'}, use_global_device_ids=true, to_apply=%region_13.14 | all-reduce | flops 1 | bytes 8 | tf_op jit(solution)/shard_map/psum | solution.py:190
  461.9 5.2 %all_to_all.21 = f32[4,1,512]{2,1,0:T(1,128)S(1)} all-to-all(f32[4,1,512]{2,1,0:T(1,128)S(1)} %reshape.286), channel_id=1, replica_groups=mesh['role'=2,'gx'=4,'gy'=4] {'gy'}, dimensions={0} | all-to-all | bytes 16384 | tf_op jit(solution)/shard_map/all_to_all | solution.py:245
  470.3 3.8 collective-permute-start.28
  475.4 3.7 collective-permute-done.28
  479.1 3.8 collective-permute-done.29
  483.3 5.9 %collective-permute-start.30 = (f32[2,128,132]{2,1,0:T(8,128)S(1)}, f32[2,128,132]{2,1,0:T(8,128)S(1)}, u32[]{:S(2)}, u32[]{:S(2)}) collective-permute-start(f32[2,128,132]{2,1,0:T(8,128)S(1)} %get-tuple-element.78), channel_id=1, source_target_pairs={{0,1},{1,2},{2,3},{3,4},{4,5},{5,6},{6,7},{7,8},{8,9},{9,10},{10,1... | collective-permute-start | bytes 405512 | tf_op jit(solution)/shard_map/ppermute | solution.py:20
  492.5 5.3 %collective-permute-done.31 = f32[2,128,132]{2,1,0:T(8,128)S(1)} collective-permute-done((f32[2,128,132]{2,1,0:T(8,128)S(1)}, f32[2,128,132]{2,1,0:T(8,128)S(1)}, u32[]{:S(2)}, u32[]{:S(2)}) %collective-permute-start.31) | collective-permute-done | bytes 135200 | tf_op jit(solution)/shard_map/ppermute | solution.py:23
  (231 shorter events, 105.7 us)
Async XLA Ops:
  0.6 80.3 %copy-start = (f32[81,81]{1,0:T(8,128)S(1)}, f32[81,81]{1,0:T(8,128)}, u32[]{:S(2)}) copy-start(f32[81,81]{1,0:T(8,128)} %param.7) | copy-start | bytes 78736
  0.6 8.8 %copy-start.6 = (f32[3,8,16,128]{3,2,1,0:T(8,128)S(1)}, f32[3,8,16,128]{3,2,1,0:T(8,128)}, u32[]{:S(2)}) copy-start(f32[3,8,16,128]{3,2,1,0:T(8,128)} %param.5) | copy-start | bytes 589828
  0.7 10.8 %collective-permute-start.4 = (f32[6,9,17,1]{2,3,1,0:T(1,128)S(1)}, f32[6,9,17,1]{2,3,1,0:T(1,128)S(1)}, u32[]{:S(2)}, u32[]{:S(2)}) collective-permute-start(f32[6,9,17,1]{2,3,1,0:T(1,128)S(1)} %slice.514), channel_id=1, source_target_pairs={{0,16},{1,17},{2,18},{3,19},{4,20},{5,21},{6,22},{7,23},{8,24},{9,... | collective-permute-start | bytes 11024 | tf_op jit(solution)/shard_map/ppermute | solution.py:20
  5.9 16.1 %collective-permute-start = (f32[4,128,2]{2,1,0:T(8,128)}, f32[4,128,2]{2,1,0:T(8,128)S(1)}, u32[]{:S(2)}, u32[]{:S(2)}) collective-permute-start(f32[4,128,2]{2,1,0:T(8,128)} %get-tuple-element.84), channel_id=1, source_target_pairs={{0,16},{1,17},{2,18},{3,19},{4,20},{5,21},{6,22},{7,23},{8,24},{9,... | collective-permute-start | bytes 12296 | tf_op jit(solution)/shard_map/ppermute | solution.py:20
  7.2 14.8 %collective-permute-start.1 = (f32[4,128,2]{2,1,0:T(8,128)}, f32[4,128,2]{2,1,0:T(8,128)S(1)}, u32[]{:S(2)}, u32[]{:S(2)}) collective-permute-start(f32[4,128,2]{2,1,0:T(8,128)} %get-tuple-element.85), channel_id=1, source_target_pairs={{16,0},{17,1},{18,2},{19,3},{20,4},{21,5},{22,6},{23,7},{24,8},{25... | collective-permute-start | bytes 12296 | tf_op jit(solution)/shard_map/ppermute | solution.py:23
  10.0 6.8 %collective-permute-start.5 = (f32[6,9,17,1]{2,3,1,0:T(1,128)S(1)}, f32[6,9,17,1]{2,3,1,0:T(1,128)S(1)}, u32[]{:S(2)}, u32[]{:S(2)}) collective-permute-start(f32[6,9,17,1]{2,3,1,0:T(1,128)S(1)} %copy.52), channel_id=1, source_target_pairs={{16,0},{17,1},{18,2},{19,3},{20,4},{21,5},{22,6},{23,7},{24,8},{25... | collective-permute-start | bytes 11024 | tf_op jit(solution)/shard_map/ppermute | solution.py:23
  17.2 4.7 copy-start.1
  17.4 5.3 %collective-permute-start.6 = (f32[6,1,17,131]{3,2,1,0:T(8,128)S(1)}, f32[6,1,17,131]{3,2,1,0:T(8,128)S(1)}, u32[]{:S(2)}, u32[]{:S(2)}) collective-permute-start(f32[6,1,17,131]{3,2,1,0:T(8,128)S(1)} %get-tuple-element.16), channel_id=1, source_target_pairs={{0,4},{4,8},{8,12},{1,5},{5,9},{9,13},{2,6},{6,10},{10,14},{3,7},{... | collective-permute-start | bytes 160352 | tf_op jit(solution)/shard_map/ppermute | solution.py:20
  20.6 5.9 %collective-permute-start.7 = (f32[6,1,17,131]{3,2,1,0:T(8,128)S(1)}, f32[6,1,17,131]{3,2,1,0:T(8,128)S(1)}, u32[]{:S(2)}, u32[]{:S(2)}) collective-permute-start(f32[6,1,17,131]{3,2,1,0:T(8,128)S(1)} %get-tuple-element.17), channel_id=1, source_target_pairs={{4,0},{8,4},{12,8},{5,1},{9,5},{13,9},{6,2},{10,6},{14,10},{7,3},{... | collective-permute-start | bytes 160352 | tf_op jit(solution)/shard_map/ppermute | solution.py:23
  26.9 13.5 %collective-permute-start.8 = (f32[6,11,1,131]{3,2,1,0:T(1,128)S(1)}, f32[6,11,1,131]{3,2,1,0:T(1,128)S(1)}, u32[]{:S(2)}, u32[]{:S(2)}) collective-permute-start(f32[6,11,1,131]{3,2,1,0:T(1,128)S(1)} %get-tuple-element.14), channel_id=1, source_target_pairs={{0,1},{1,2},{2,3},{4,5},{5,6},{6,7},{8,9},{9,10},{10,11},{12,13},{... | collective-permute-start | bytes 103760 | tf_op jit(solution)/shard_map/ppermute | solution.py:20
  28.2 12.2 %collective-permute-start.9 = (f32[6,11,1,131]{3,2,1,0:T(1,128)S(1)}, f32[6,11,1,131]{3,2,1,0:T(1,128)S(1)}, u32[]{:S(2)}, u32[]{:S(2)}) collective-permute-start(f32[6,11,1,131]{3,2,1,0:T(1,128)S(1)} %get-tuple-element.15), channel_id=1, source_target_pairs={{1,0},{2,1},{3,2},{5,4},{6,5},{7,6},{9,8},{10,9},{11,10},{13,12},{... | collective-permute-start | bytes 103760 | tf_op jit(solution)/shard_map/ppermute | solution.py:23
  34.9 25.3 %collective-permute-start.2 = (f32[2,128,132]{2,1,0:T(8,128)}, f32[2,128,132]{2,1,0:T(8,128)}, u32[]{:S(2)}, u32[]{:S(2)}) collective-permute-start(f32[2,128,132]{2,1,0:T(8,128)} %get-tuple-element.80), channel_id=1, source_target_pairs={{0,1},{1,2},{2,3},{3,4},{4,5},{5,6},{6,7},{7,8},{8,9},{9,10},{10,1... | collective-permute-start | bytes 405512 | tf_op jit(solution)/shard_map/ppermute | solution.py:20
  36.8 23.3 %collective-permute-start.3 = (f32[2,128,132]{2,1,0:T(8,128)}, f32[2,128,132]{2,1,0:T(8,128)}, u32[]{:S(2)}, u32[]{:S(2)}) collective-permute-start(f32[2,128,132]{2,1,0:T(8,128)} %get-tuple-element.81), channel_id=1, source_target_pairs={{1,0},{2,1},{3,2},{4,3},{5,4},{6,5},{7,6},{8,7},{9,8},{10,9},{11,1... | collective-permute-start | bytes 405512 | tf_op jit(solution)/shard_map/ppermute | solution.py:23
  70.6 8.3 %all-to-all-start = ((f32[4,1,512]{2,1,0:T(1,128)}), f32[4,1,512]{2,1,0:T(1,128)S(1)}, u32[]{:S(2)}, u32[]{:S(2)}) async-start(f32[4,1,512]{2,1,0:T(1,128)} %reshape.284), calls=%async_computation | async-start | bytes 16384 | tf_op jit(solution)/shard_map/all_to_all | solution.py:213
  87.2 8.2 %collective-permute-start.10 = (f32[3,9,17,1]{3,2,1,0:T(8,128)S(1)}, f32[3,9,17,1]{3,2,1,0:T(8,128)S(1)}, u32[]{:S(2)}, u32[]{:S(2)}) collective-permute-start(f32[3,9,17,1]{3,2,1,0:T(8,128)S(1)} %get-tuple-element.73), channel_id=1, source_target_pairs={{0,16},{1,17},{2,18},{3,19},{4,20},{5,21},{6,22},{7,23},{8,24},{9,... | collective-permute-start | bytes 5516 | tf_op jit(solution)/shard_map/ppermute | solution.py:20
  88.6 10.7 %collective-permute-start.11 = (f32[3,9,17,1]{3,2,1,0:T(8,128)S(1)}, f32[3,9,17,1]{3,2,1,0:T(8,128)S(1)}, u32[]{:S(2)}, u32[]{:S(2)}) collective-permute-start(f32[3,9,17,1]{3,2,1,0:T(8,128)S(1)} %get-tuple-element.74), channel_id=1, source_target_pairs={{16,0},{17,1},{18,2},{19,3},{20,4},{21,5},{22,6},{23,7},{24,8},{25... | collective-permute-start | bytes 5516 | tf_op jit(solution)/shard_map/ppermute | solution.py:23
  99.4 4.6 collective-permute-start.12
  102.6 5.1 %collective-permute-start.13 = (f32[3,1,17,131]{3,2,1,0:T(8,128)S(1)}, f32[3,1,17,131]{3,2,1,0:T(8,128)S(1)}, u32[]{:S(2)}, u32[]{:S(2)}) collective-permute-start(f32[3,1,17,131]{3,2,1,0:T(8,128)S(1)} %get-tuple-element.30), channel_id=1, source_target_pairs={{4,0},{8,4},{12,8},{5,1},{9,5},{13,9},{6,2},{10,6},{14,10},{7,3},{... | collective-permute-start | bytes 80180 | tf_op jit(solution)/shard_map/ppermute | solution.py:23
  107.9 6.7 %collective-permute-start.14 = (f32[3,11,1,131]{3,2,1,0:T(1,128)S(1)}, f32[3,11,1,131]{3,2,1,0:T(1,128)S(1)}, u32[]{:S(2)}, u32[]{:S(2)}) collective-permute-start(f32[3,11,1,131]{3,2,1,0:T(1,128)S(1)} %get-tuple-element.22), channel_id=1, source_target_pairs={{0,1},{1,2},{2,3},{4,5},{5,6},{6,7},{8,9},{9,10},{10,11},{12,13},{... | collective-permute-start | bytes 51884 | tf_op jit(solution)/shard_map/ppermute | solution.py:20
  109.2 6.2 %collective-permute-start.15 = (f32[3,11,1,131]{3,2,1,0:T(1,128)S(1)}, f32[3,11,1,131]{3,2,1,0:T(1,128)S(1)}, u32[]{:S(2)}, u32[]{:S(2)}) collective-permute-start(f32[3,11,1,131]{3,2,1,0:T(1,128)S(1)} %get-tuple-element.23), channel_id=1, source_target_pairs={{1,0},{2,1},{3,2},{5,4},{6,5},{7,6},{9,8},{10,9},{11,10},{13,12},{... | collective-permute-start | bytes 51884 | tf_op jit(solution)/shard_map/ppermute | solution.py:23
  238.3 9.6 %collective-permute-start.16 = (f32[3,9,17,1]{3,2,1,0:T(8,128)S(1)}, f32[3,9,17,1]{3,2,1,0:T(8,128)S(1)}, u32[]{:S(2)}, u32[]{:S(2)}) collective-permute-start(f32[3,9,17,1]{3,2,1,0:T(8,128)S(1)} %get-tuple-element.66), channel_id=1, source_target_pairs={{0,16},{1,17},{2,18},{3,19},{4,20},{5,21},{6,22},{7,23},{8,24},{9,... | collective-permute-start | bytes 5516 | tf_op jit(solution)/shard_map/ppermute | solution.py:20
  241.9 9.9 %collective-permute-start.17 = (f32[3,9,17,1]{3,2,1,0:T(8,128)S(1)}, f32[3,9,17,1]{3,2,1,0:T(8,128)S(1)}, u32[]{:S(2)}, u32[]{:S(2)}) collective-permute-start(f32[3,9,17,1]{3,2,1,0:T(8,128)S(1)} %get-tuple-element.67), channel_id=1, source_target_pairs={{16,0},{17,1},{18,2},{19,3},{20,4},{21,5},{22,6},{23,7},{24,8},{25... | collective-permute-start | bytes 5516 | tf_op jit(solution)/shard_map/ppermute | solution.py:23
  251.9 4.8 collective-permute-start.18
  255.3 5.1 %collective-permute-start.19 = (f32[3,1,17,131]{3,2,1,0:T(8,128)S(1)}, f32[3,1,17,131]{3,2,1,0:T(8,128)S(1)}, u32[]{:S(2)}, u32[]{:S(2)}) collective-permute-start(f32[3,1,17,131]{3,2,1,0:T(8,128)S(1)} %get-tuple-element.28), channel_id=1, source_target_pairs={{4,0},{8,4},{12,8},{5,1},{9,5},{13,9},{6,2},{10,6},{14,10},{7,3},{... | collective-permute-start | bytes 80180 | tf_op jit(solution)/shard_map/ppermute | solution.py:23
  260.6 7.4 %collective-permute-start.20 = (f32[3,11,1,131]{3,2,1,0:T(1,128)S(1)}, f32[3,11,1,131]{3,2,1,0:T(1,128)S(1)}, u32[]{:S(2)}, u32[]{:S(2)}) collective-permute-start(f32[3,11,1,131]{3,2,1,0:T(1,128)S(1)} %get-tuple-element.20), channel_id=1, source_target_pairs={{0,1},{1,2},{2,3},{4,5},{5,6},{6,7},{8,9},{9,10},{10,11},{12,13},{... | collective-permute-start | bytes 51884 | tf_op jit(solution)/shard_map/ppermute | solution.py:20
  261.9 6.9 %collective-permute-start.21 = (f32[3,11,1,131]{3,2,1,0:T(1,128)S(1)}, f32[3,11,1,131]{3,2,1,0:T(1,128)S(1)}, u32[]{:S(2)}, u32[]{:S(2)}) collective-permute-start(f32[3,11,1,131]{3,2,1,0:T(1,128)S(1)} %get-tuple-element.21), channel_id=1, source_target_pairs={{1,0},{2,1},{3,2},{5,4},{6,5},{7,6},{9,8},{10,9},{11,10},{13,12},{... | collective-permute-start | bytes 51884 | tf_op jit(solution)/shard_map/ppermute | solution.py:23
  270.1 0.9 copy-start.4
  315.0 0.9 copy-start.3
  359.3 54.0 %copy-start.2 = (f32[3,9,17,129]{3,2,1,0:T(8,128)}, f32[3,9,17,129]{3,2,1,0:T(8,128)S(1)}, u32[]{:S(2)}) copy-start(f32[3,9,17,129]{3,2,1,0:T(8,128)S(1)} %get-tuple-element.7) | copy-start | bytes 710536
  382.6 9.6 %collective-permute-start.22 = (f32[3,9,17,1]{3,2,1,0:T(8,128)S(1)}, f32[3,9,17,1]{3,2,1,0:T(8,128)S(1)}, u32[]{:S(2)}, u32[]{:S(2)}) collective-permute-start(f32[3,9,17,1]{3,2,1,0:T(8,128)S(1)} %get-tuple-element.59), channel_id=1, source_target_pairs={{0,16},{1,17},{2,18},{3,19},{4,20},{5,21},{6,22},{7,23},{8,24},{9,... | collective-permute-start | bytes 5516 | tf_op jit(solution)/shard_map/ppermute | solution.py:20
  386.1 9.9 %collective-permute-start.23 = (f32[3,9,17,1]{3,2,1,0:T(8,128)S(1)}, f32[3,9,17,1]{3,2,1,0:T(8,128)S(1)}, u32[]{:S(2)}, u32[]{:S(2)}) collective-permute-start(f32[3,9,17,1]{3,2,1,0:T(8,128)S(1)} %get-tuple-element.60), channel_id=1, source_target_pairs={{16,0},{17,1},{18,2},{19,3},{20,4},{21,5},{22,6},{23,7},{24,8},{25... | collective-permute-start | bytes 5516 | tf_op jit(solution)/shard_map/ppermute | solution.py:23
  396.2 3.6 collective-permute-start.24
  398.4 5.1 %collective-permute-start.25 = (f32[3,1,17,131]{3,2,1,0:T(8,128)S(1)}, f32[3,1,17,131]{3,2,1,0:T(8,128)S(1)}, u32[]{:S(2)}, u32[]{:S(2)}) collective-permute-start(f32[3,1,17,131]{3,2,1,0:T(8,128)S(1)} %get-tuple-element.26), channel_id=1, source_target_pairs={{4,0},{8,4},{12,8},{5,1},{9,5},{13,9},{6,2},{10,6},{14,10},{7,3},{... | collective-permute-start | bytes 80180 | tf_op jit(solution)/shard_map/ppermute | solution.py:23
  403.8 7.5 %collective-permute-start.26 = (f32[3,11,1,131]{3,2,1,0:T(1,128)S(1)}, f32[3,11,1,131]{3,2,1,0:T(1,128)S(1)}, u32[]{:S(2)}, u32[]{:S(2)}) collective-permute-start(f32[3,11,1,131]{3,2,1,0:T(1,128)S(1)} %get-tuple-element.18), channel_id=1, source_target_pairs={{0,1},{1,2},{2,3},{4,5},{5,6},{6,7},{8,9},{9,10},{10,11},{12,13},{... | collective-permute-start | bytes 51884 | tf_op jit(solution)/shard_map/ppermute | solution.py:20
  405.1 7.0 %collective-permute-start.27 = (f32[3,11,1,131]{3,2,1,0:T(1,128)S(1)}, f32[3,11,1,131]{3,2,1,0:T(1,128)S(1)}, u32[]{:S(2)}, u32[]{:S(2)}) collective-permute-start(f32[3,11,1,131]{3,2,1,0:T(1,128)S(1)} %get-tuple-element.19), channel_id=1, source_target_pairs={{1,0},{2,1},{3,2},{5,4},{6,5},{7,6},{9,8},{10,9},{11,10},{13,12},{... | collective-permute-start | bytes 51884 | tf_op jit(solution)/shard_map/ppermute | solution.py:23
  468.2 1.8 copy-start.5
  470.3 8.9 %collective-permute-start.28 = (f32[4,128,2]{2,1,0:T(8,128)S(1)}, f32[4,128,2]{2,1,0:T(8,128)S(1)}, u32[]{:S(2)}, u32[]{:S(2)}) collective-permute-start(f32[4,128,2]{2,1,0:T(8,128)S(1)} %get-tuple-element.82), channel_id=1, source_target_pairs={{0,16},{1,17},{2,18},{3,19},{4,20},{5,21},{6,22},{7,23},{8,24},{9,... | collective-permute-start | bytes 12296 | tf_op jit(solution)/shard_map/ppermute | solution.py:20
  474.1 8.9 %collective-permute-start.29 = (f32[4,128,2]{2,1,0:T(8,128)S(1)}, f32[4,128,2]{2,1,0:T(8,128)S(1)}, u32[]{:S(2)}, u32[]{:S(2)}) collective-permute-start(f32[4,128,2]{2,1,0:T(8,128)S(1)} %get-tuple-element.83), channel_id=1, source_target_pairs={{16,0},{17,1},{18,2},{19,3},{20,4},{21,5},{22,6},{23,7},{24,8},{25... | collective-permute-start | bytes 12296 | tf_op jit(solution)/shard_map/ppermute | solution.py:23
  483.3 9.2 %collective-permute-start.30 = (f32[2,128,132]{2,1,0:T(8,128)S(1)}, f32[2,128,132]{2,1,0:T(8,128)S(1)}, u32[]{:S(2)}, u32[]{:S(2)}) collective-permute-start(f32[2,128,132]{2,1,0:T(8,128)S(1)} %get-tuple-element.78), channel_id=1, source_target_pairs={{0,1},{1,2},{2,3},{3,4},{4,5},{5,6},{6,7},{7,8},{8,9},{9,10},{10,1... | collective-permute-start | bytes 405512 | tf_op jit(solution)/shard_map/ppermute | solution.py:20
  489.2 8.6 %collective-permute-start.31 = (f32[2,128,132]{2,1,0:T(8,128)S(1)}, f32[2,128,132]{2,1,0:T(8,128)S(1)}, u32[]{:S(2)}, u32[]{:S(2)}) collective-permute-start(f32[2,128,132]{2,1,0:T(8,128)S(1)} %get-tuple-element.79), channel_id=1, source_target_pairs={{1,0},{2,1},{3,2},{4,3},{5,4},{6,5},{7,6},{8,7},{9,8},{10,9},{11,1... | collective-permute-start | bytes 405512 | tf_op jit(solution)/shard_map/ppermute | solution.py:23
where the time goes:
time: 510 us; the launch traced here: 500 us
  blocking collectives  208 us (41%)
  starting transfers between devices  88.6 us (17%)
  local copies, waits for them, and re-layouts  80 us (16%)
  waiting for transfers between devices  63.2 us (12%)
  other arithmetic  27.6 us (5%)
  matrix products  23.6 us (5%)
  between operations  9.15 us (2%)
    psum x5, blocking collectives, inner_sum(): return lax.psum(local_part, ('role', 'gx', 'gy'))  203 us
    ppermute x16, waiting for transfers between devices, with_halo(): lax.ppermute(lax.slice_in_dim(block, 0, width, axis=dim), axis, backward)  43 us
    slice x12, local copies, waits for them, and re-layouts, split_axis(): lax.slice_in_dim(values, corner, corner + 2 * half_len - 1, stride=2, axi...  42.4 us
    ppermute x16, starting transfers between devices, with_halo(): lax.ppermute(lax.slice_in_dim(block, block.shape[dim] - width, None, axis...  41.8 us
    ppermute x16, starting transfers between devices, with_halo(): lax.ppermute(lax.slice_in_dim(block, 0, width, axis=dim), axis, backward)  41.8 us
    ppermute x16, waiting for transfers between devices, with_halo(): lax.ppermute(lax.slice_in_dim(block, block.shape[dim] - width, None, axis...  20.2 us
  transfers between devices with their start and end apart: 33, of which 22 were waited for; matrix products, arithmetic and copies ran while one was open for 6% of the time, Pallas kernels for 0%

commit v1 on v0

v1 whole, which is shorter than its diff:
```python
import jax
import jax.numpy as jnp
import numpy as np
from jax import lax
from jax.experimental import pallas as pl
from jax.experimental.pallas import tpu as pltpu
from jax.sharding import PartitionSpec as P

SHARPNESS = 4.0
THRESHOLD = 0.5
FLOOR_STIFF = 0.001
TANH2 = float(np.tanh(2.0))
LANES = 128
HALO = 3
STRIP = 8
ROWS = 120
LINE = ("gx", "gy")
F32 = jnp.float32
BF16 = jnp.bfloat16


def iota(shape, dim):
    return lax.broadcasted_iota(jnp.int32, shape, dim)


def place_table():
    table = np.zeros((ROWS, 81), np.float32)
    for c in range(3):
        for b in range(3):
            for a in range(3):
                for q in range(3):
                    dof = ((c * 3 + b) * 3 + a) * 3 + q
                    if c < 2:
                        row = 8 * (3 * a + b) + 4 * c + q
                    else:
                        row = 72 + 8 * (2 * b + (a == 2)) + 4 * (a == 1) + q
                    table[row, dof] = 1.0
    return table


def split2(x):
    hi = x.astype(BF16)
    return hi, (x - hi.astype(F32)).astype(BF16)


def split3(x):
    hi = x.astype(BF16)
    rest = x - hi.astype(F32)
    mid = rest.astype(BF16)
    return hi, mid, (rest - mid.astype(F32)).astype(BF16)


def dot(a, b):
    return jnp.dot(a, b, preferred_element_type=F32)


def pick_right(x, table):
    hi, mid, lo = split3(x)
    return (dot(hi, table) + dot(mid, table)) + dot(lo, table)


def pick_left(table, x):
    hi, mid, lo = split3(x)
    return (dot(table, hi) + dot(table, mid)) + dot(table, lo)


def where_am_i():
    role = lax.axis_index("role")
    slab = lax.axis_index("gx") * lax.axis_size("gy") + lax.axis_index("gy")
    return role, slab


def element_lanes(shape, role, half):
    lane = iota(shape, len(shape) - 1)
    above = jnp.logical_and(lane >= half, lane < half + HALO)
    below = lane >= LANES - HALO
    roles = lax.axis_size("role")
    return (lane < half) | (above & (role < roles - 1)) | (below & (role > 0))


def hat_count(place, extent):
    low = jnp.where(place == 0, 3.0, jnp.where(place == 1, 1.0, 0.0))
    high = jnp.where(place == extent - 1, 3.0, jnp.where(place == extent - 2, 1.0, 0.0))
    return 9.0 - low - high


def smooth_z(x):
    width = x.shape[1]
    for _ in range(2):
        x = x + pltpu.roll(x, 1, 1) + pltpu.roll(x, width - 1, 1)
    return x


def smooth_y(x):
    rows = x.shape[0]
    x = jnp.concatenate([x, jnp.zeros((8, x.shape[1]), F32)], axis=0)
    for _ in range(2):
        x = x + pltpu.roll(x, 1, 0) + pltpu.roll(x, rows + 7, 0)
    return x[:rows]


def prep_kernel(force_ref, mask_ref, next_ref, stiff_ref, place_ref, pack_ref, table_ref):
    parts = pack_ref.shape[0]
    for q in range(3):
        free = 1.0 - mask_ref[q].astype(F32)
        rhs = free * force_ref[q]
        for row, val in ((q, rhs), (q + 3, free)):
            for j in range(parts):
                for a in range(3):
                    x = 2 * j + a
                    pack_ref[j, row, a] = val[x] if x < 2 * parts else next_ref[row]
    place = place_ref[...]
    half_way = jnp.dot(place, stiff_ref[...], precision=lax.Precision.HIGHEST, preferred_element_type=F32)
    spread = lax.dot_general(
        half_way, place, (((1,), (1,)), ((), ())), precision=lax.Precision.HIGHEST, preferred_element_type=F32
    )
    hi, lo = split2(spread)
    row = iota((ROWS, 2 * ROWS), 0)
    col = iota((ROWS, 2 * ROWS), 1)
    twice = jnp.where(row == 8 * (col // 16) + col % 8, 1.0, 0.0).astype(BF16)
    table_ref[:ROWS] = dot(hi, twice).astype(BF16)
    table_ref[ROWS:] = dot(lo, twice).astype(BF16)


def plane_rows(tiles):
    return tiles * 8


def shifted_tiles(nodes_ref, tiles, s):
    count = plane_rows(tiles)
    upper = (iota((count, LANES), 0) & 4) == 0
    if s == 0:
        first = nodes_ref[0:count]
        second = nodes_ref[count : 2 * count]
        x = jnp.where(upper, first, pltpu.roll(second, 4, 0))
    else:
        x = jnp.where(upper, nodes_ref[2 * count : 3 * count], 0.0)
    return pltpu.roll(x, LANES - 1, 1)


def pair_tiles(x):
    tiles = x.shape[0] // 8
    hi = x.astype(BF16).astype(F32)
    lo = x - hi
    both = jnp.concatenate([hi.reshape(tiles, 8, LANES), lo.reshape(tiles, 8, LANES)], axis=1)
    return both.astype(BF16)


def make_tiles(nodes_ref, main_ref, shift_ref, shift32_ref):
    tiles = main_ref.shape[1]
    count = plane_rows(tiles)
    for a in range(3):
        main_ref[a] = pair_tiles(nodes_ref[a * count : (a + 1) * count])
    for s in range(2):
        x = shifted_tiles(nodes_ref, tiles, s)
        if shift32_ref is not None:
            shift32_ref[s] = x
        shift_ref[s] = pair_tiles(x)


def sweep(table_ref, main_ref, shift_ref, factor_ref, out_ref, energies):
    tiles = main_ref.shape[1]
    columns = factor_ref.shape[0]
    upper = iota((8, LANES), 0) < 4

    def finish(node, parts):
        t0, t1, t2, s0, s1 = parts
        r0 = pltpu.roll(s0, 1, 1)
        r1 = pltpu.roll(s1, 1, 1)
        done = (
            t0 + jnp.where(upper, r0, 0.0),
            t1 + jnp.where(upper, pltpu.roll(r0, 4, 0), 0.0),
            t2 + jnp.where(upper, r1, 0.0),
        )
        for a in range(3):
            out_ref[pl.ds(pl.multiple_of((a * tiles + node) * 8, 8), 8), :] = done[a]

    def body(i, carry):
        cols = []
        for k in range(2):
            base = 4 * i + 2 * k
            pieces = [main_ref[a, base + b] for a in range(3) for b in range(3)]
            pieces += [shift_ref[s, base + b] for b in range(3) for s in range(2)]
            cols.append(jnp.concatenate(pieces, axis=0))
        product = dot(table_ref[...], jnp.concatenate(cols, axis=1))
        product = product[:ROWS] + product[ROWS:]
        parts = []
        for k in range(2):
            y = product[:, k * LANES : (k + 1) * LANES]
            base = 4 * i + 2 * k
            for nodes_ref, shift32_ref, e_ref in energies:
                total = None
                for a in range(3):
                    for b in range(3):
                        at = pl.multiple_of((a * tiles + base + b) * 8, 8)
                        term = nodes_ref[pl.ds(at, 8), :] * y[8 * (3 * a + b) : 8 * (3 * a + b) + 8]
                        total = term if total is None else total + term
                for b in range(3):
                    for s in range(2):
                        at = pl.multiple_of((base + b) * 8, 8)
                        lo = 72 + 8 * (2 * b + s)
                        total = total + shift32_ref[s, pl.ds(at, 8), :] * y[lo : lo + 8]
                e_ref[pl.ds(2 * i + k, 1), :] = jnp.sum(total, axis=0, keepdims=True)
            if out_ref is not None:
                z = y * factor_ref[pl.ds(2 * i + k, 1), :]
                parts.append(
                    [
                        [z[8 * (3 * a + b) : 8 * (3 * a + b) + 8] for a in range(3)]
                        + [z[72 + 8 * (2 * b + s) : 80 + 8 * (2 * b + s)] for s in range(2)]
                        for b in range(3)
                    ]
                )
        if out_ref is None:
            return carry
        left, right = parts
        finish(4 * i, [c + v for c, v in zip(carry, left[0])])
        finish(4 * i + 1, left[1])
        finish(4 * i + 2, [c + v for c, v in zip(left[2], right[0])])
        finish(4 * i + 3, right[1])
        return tuple(right[2])

    if out_ref is None:
        lax.fori_loop(0, columns // 2, lambda i, c: body(i, c), 0)
    else:
        zero = jnp.zeros((8, LANES), F32)
        lax.fori_loop(0, columns // 2, body, (zero,) * 5)
        for a in range(3):
            for node in range(2 * columns, tiles):
                at = (a * tiles + node) * 8
                out_ref[at : at + 8, :] = zero


def send_planes(local_ref, tiles, slab, to_a, to_b):
    count = plane_rows(tiles)
    low = local_ref[0:count]
    high = local_ref[2 * count : 3 * count]
    even = slab % 2 == 0
    to_a[...] = jnp.where(even, high, low)
    to_b[...] = jnp.where(even, low, high)


def gather_nodes(local_ref, from_a, from_b, free_ref, tiles, slab, nodes_ref):
    count = plane_rows(tiles)
    even = slab % 2 == 0
    a = from_a[...]
    b = from_b[...]
    nodes_ref[0:count] = free_ref[0:count] * (local_ref[0:count] + jnp.where(even, b, a))
    nodes_ref[count : 2 * count] = free_ref[count : 2 * count] * local_ref[count : 2 * count]
    nodes_ref[2 * count :] = free_ref[2 * count :] * (local_ref[2 * count :] + jnp.where(even, a, b))


def first_kernel(
    design_ref, da_ref, db_ref, strip_ref, rf_ref, table_ref,
    sw_ref, factor_ref, density_ref, nodes_ref, free_ref, local_ref, to_a, to_b, e00_ref,
    fine_ref, sum_ref, main_ref, shift_ref, shift32_ref,
):
    planes, fy, fz = design_ref.shape
    tiles = main_ref.shape[1]
    count = plane_rows(tiles)
    role, slab = where_am_i()
    slabs = lax.axis_size("gx") * lax.axis_size("gy")
    roles = lax.axis_size("role")
    half = fz // 2
    even = slab % 2 == 0

    at_lane = jnp.where(role == 0, 0, LANES - STRIP)
    put = jnp.where(iota((STRIP, LANES), 1) == iota((STRIP, LANES), 0) + at_lane, 1.0, 0.0).astype(BF16)
    for p in range(planes):
        a = da_ref[p]
        b = db_ref[p]
        fine_ref[p, :, :fz] = jnp.where(even, b, a)
        fine_ref[planes + p, :, :fz] = design_ref[p]
        fine_ref[2 * planes + p, :, :fz] = jnp.where(even, a, b)
    for p in range(planes):
        own = pick_right(strip_ref[p * fy : (p + 1) * fy], put)
        a = pick_right(strip_ref[(planes + p) * fy : (planes + p + 1) * fy], put)
        b = pick_right(strip_ref[(2 * planes + p) * fy : (2 * planes + p + 1) * fy], put)
        fine_ref[p, :, fz:] = jnp.where(even, b, a)
        fine_ref[planes + p, :, fz:] = own
        fine_ref[2 * planes + p, :, fz:] = jnp.where(even, a, b)

    width = 2 * fz
    lane = iota((1, width), 1)
    z_place = role * fz + jnp.where(lane < fz + fz // 2, lane, lane - width)
    inv_z = 1.0 / hat_count(z_place, roles * fz)
    inv_y = 1.0 / hat_count(iota((fy, 1), 0), fy)
    inv_yz = inv_y * inv_z
    sum_ref[...] = jnp.zeros((fy, width), F32)

    def filter_plane(p, _):
        x = fine_ref[p] + fine_ref[p + 4] + 2.0 * (fine_ref[p + 1] + fine_ref[p + 3]) + 3.0 * fine_ref[p + 2]
        x = smooth_y(smooth_z(x))
        place = jnp.full((1, 1), slab * planes + p - 2, jnp.int32)
        inv = inv_yz * (1.0 / hat_count(place, slabs * planes))
        bent = jnp.tanh(SHARPNESS * (x * inv - THRESHOLD))
        sw_ref[p] = (SHARPNESS / (2.0 * TANH2)) * (1.0 - bent * bent) * inv
        mine = jnp.logical_and(p >= 2, p < 2 + planes)
        sum_ref[...] += jnp.where(mine, (TANH2 + bent) * (1.0 / (2.0 * TANH2)), 0.0)
        return 0

    lax.fori_loop(0, planes + 4, filter_plane, 0)

    rows = factor_ref.shape[0]
    pool_y = jnp.where(iota((rows, fy), 1) // 4 == iota((rows, fy), 0), 1.0, 0.0).astype(BF16)
    pool_z = jnp.where(iota((width, LANES), 0) // 2 == iota((width, LANES), 1), 1.0, 0.0).astype(BF16)
    density = pick_right(pick_left(pool_y, sum_ref[...]), pool_z) * (1.0 / 32.0)
    inside = element_lanes((rows, LANES), role, half)
    density = jnp.where(inside, density, 0.0)
    density_ref[...] = density
    factor_ref[...] = jnp.where(inside, FLOOR_STIFF + (1.0 - FLOOR_STIFF) * density * density * density, 0.0)

    nodes_ref[...] = jnp.zeros(nodes_ref.shape, F32)
    free_ref[...] = jnp.zeros(free_ref.shape, F32)
    zi = iota((LANES, width), 0)
    ci = iota((LANES, width), 1)
    lane_of = ci & (LANES - 1)
    odd = ci // LANES
    own_table = jnp.where(zi == 2 * lane_of + odd, 1.0, 0.0).astype(BF16)
    si = iota((STRIP, width), 0)
    ci = iota((STRIP, width), 1)
    lane_of = ci & (LANES - 1)
    odd = ci // LANES
    first_lane = jnp.where(role == 0, half, LANES - STRIP // 2)
    strip_table = jnp.where(si == 2 * (lane_of - first_lane) + odd, 1.0, 0.0).astype(BF16)
    parts = rf_ref.shape[0]
    deep = rf_ref.shape[3]
    base = 3 * planes * fy
    for row in range(6):
        for a in range(3):
            x = jnp.concatenate([rf_ref[j, row, a] for j in range(parts)], axis=0)
            st = jnp.concatenate(
                [
                    strip_ref[base + ((j * 6 + row) * 3 + a) * deep : base + ((j * 6 + row) * 3 + a + 1) * deep]
                    for j in range(parts)
                ],
                axis=0,
            )
            if row < 3:
                y = pick_right(x, own_table) + pick_right(st, strip_table)
                dest = nodes_ref
            else:
                y = dot(x.astype(BF16), own_table) + dot(st.astype(BF16), strip_table)
                dest = free_ref
            q = row % 3
            dest[pl.ds(a * count + q, parts * deep, stride=8), :] = y[:, :LANES]
            dest[pl.ds(a * count + 4 + q, parts * deep, stride=8), :] = y[:, LANES:]

    make_tiles(nodes_ref, main_ref, shift_ref, shift32_ref)
    sweep(table_ref, main_ref, shift_ref, factor_ref, local_ref, [(nodes_ref, shift32_ref, e00_ref)])
    send_planes(local_ref, tiles, slab, to_a, to_b)


def second_kernel(
    prev_ref, free_ref, last_ref, from_a, from_b, factor_ref, table_ref,
    nodes_ref, local_ref, to_a, to_b, e01_ref, e11_ref,
    main_ref, shift_ref, shift32_ref, prev32_ref,
):
    tiles = main_ref.shape[1]
    role, slab = where_am_i()
    gather_nodes(last_ref, from_a, from_b, free_ref, tiles, slab, nodes_ref)
    for s in range(2):
        prev32_ref[s] = shifted_tiles(prev_ref, tiles, s)
    make_tiles(nodes_ref, main_ref, shift_ref, shift32_ref)
    sweep(
        table_ref, main_ref, shift_ref, factor_ref, local_ref,
        [(prev_ref, prev32_ref, e01_ref), (nodes_ref, shift32_ref, e11_ref)],
    )
    send_planes(local_ref, tiles, slab, to_a, to_b)


def third_kernel(
    v0_ref, v1_ref, free_ref, last_ref, from_a, from_b, factor_ref, table_ref, e00_ref, e01_ref, e11_ref,
    nodes_ref, e02_ref, e12_ref, e22_ref, moment_ref,
    main_ref, shift_ref, shift32_ref, s0_ref, s1_ref,
):
    tiles = main_ref.shape[1]
    count = plane_rows(tiles)
    role, slab = where_am_i()
    gather_nodes(last_ref, from_a, from_b, free_ref, tiles, slab, nodes_ref)
    for s in range(2):
        s0_ref[s] = shifted_tiles(v0_ref, tiles, s)
        s1_ref[s] = shifted_tiles(v1_ref, tiles, s)
    make_tiles(nodes_ref, main_ref, shift_ref, shift32_ref)
    sweep(
        table_ref, main_ref, shift_ref, factor_ref, None,
        [(v0_ref, s0_ref, e02_ref), (v1_ref, s1_ref, e12_ref), (nodes_ref, shift32_ref, e22_ref)],
    )
    half = LANES // 2
    own = iota((1, LANES), 1) < half
    v0 = v0_ref[0 : 2 * count]
    sums = [jnp.sum(v0 * v0, axis=0, keepdims=True)]
    for e_ref in (e00_ref, e01_ref, e11_ref, e12_ref, e22_ref):
        sums.append(jnp.sum(factor_ref[...] * e_ref[...], axis=0, keepdims=True))
    lane = iota((1, LANES), 1)
    out = jnp.zeros((1, LANES), F32)
    for k, s in enumerate(sums):
        total = jnp.sum(jnp.where(own, s, 0.0), axis=1, keepdims=True)
        out = jnp.where(lane == k, total, out)
    moment_ref[...] = jnp.broadcast_to(out, moment_ref.shape)


def combine_kernel(
    moment_ref, v0_ref, v1_ref, v2_ref, e00_ref, e01_ref, e11_ref, e02_ref, e12_ref, e22_ref, density_ref,
    grad_ref, u_ref, nodes_ref,
):
    role, slab = where_am_i()
    parts, _, _, deep, fz = u_ref.shape
    half = fz // 2
    count = v0_ref.shape[0] // 3
    total = jnp.sum(moment_ref[...], axis=0, keepdims=True)
    lane = iota((1, LANES), 1)
    m = [jnp.sum(jnp.where(lane == k, total, 0.0), axis=1, keepdims=True) for k in range(6)]
    s = m[1] / m[0]
    inv = 1.0 / s
    mu = [jnp.ones_like(s)]
    power = 1.0 / m[0]
    for k in range(1, 6):
        power = power * inv
        mu.append(m[k] * power)
    nu = list(mu)
    for depth in range(1, 6):
        for k in range(5, depth - 1, -1):
            nu[k] = nu[k] - nu[k - 1]
    g = [nu[k] + nu[k + 1] for k in range(5)]
    l10 = g[1] / g[0]
    l20 = g[2] / g[0]
    d1 = g[2] - l10 * g[1]
    x12 = g[3] - l10 * g[2]
    r1 = nu[1] - l10 * nu[0]
    r2 = nu[2] - l20 * nu[0]
    l21 = x12 / d1
    d2 = (g[4] - l20 * g[2]) - l21 * x12
    c2 = (r2 - l21 * r1) / d2
    c1 = (r1 - x12 * c2) / d1
    c0 = (nu[0] - g[1] * c1 - g[2] * c2) / g[0]
    w0 = (c0 - c1 + c2) * inv
    w1 = (c1 - 2.0 * c2) * inv * inv
    w2 = c2 * inv * inv * inv
    energy = (
        w0 * (w0 * e00_ref[...] + 2.0 * (w1 * e01_ref[...] + w2 * e02_ref[...]))
        + w1 * (w1 * e11_ref[...] + 2.0 * w2 * e12_ref[...])
        + w2 * w2 * e22_ref[...]
    )
    density = density_ref[...]
    grad = (-3.0 * (1.0 - FLOOR_STIFF) / 32.0) * density * density * energy
    grad_ref[...] = jnp.where(element_lanes(grad.shape, role, half), grad, 0.0)
    nodes_ref[...] = w0 * v0_ref[0 : 2 * count] + w1 * v1_ref[0 : 2 * count] + w2 * v2_ref[0 : 2 * count]
    gi = iota((LANES, fz), 0)
    zi = iota((LANES, fz), 1)
    even_table = jnp.where(zi == 2 * gi, 1.0, 0.0).astype(BF16)
    odd_table = jnp.where(zi == 2 * gi + 1, 1.0, 0.0).astype(BF16)
    for a in range(2):
        for q in range(3):
            even = nodes_ref[pl.ds(a * count + q, parts * deep, stride=8), :]
            odd = nodes_ref[pl.ds(a * count + 4 + q, parts * deep, stride=8), :]
            x = pick_right(even, even_table) + pick_right(odd, odd_table)
            for j in range(parts):
                u_ref[j, q, a] = x[j * deep : (j + 1) * deep]


def last_kernel(grad_ref, ga_ref, gb_ref, sw_ref, out_ref, work_ref):
    planes, fy, fz = out_ref.shape
    width = 2 * fz
    role, slab = where_am_i()
    even = slab % 2 == 0
    rows = grad_ref.shape[0]
    pool_y = jnp.where(iota((fy, rows), 0) // 4 == iota((fy, rows), 1), 1.0, 0.0).astype(BF16)
    pool_z = jnp.where(iota((LANES, width), 1) // 2 == iota((LANES, width), 0), 1.0, 0.0).astype(BF16)
    a = ga_ref[...]
    b = gb_ref[...]
    low = jnp.where(even, b, a)
    high = jnp.where(even, a, b)
    for grad, first, last in ((low, 0, 2), (grad_ref[...], 2, 2 + planes), (high, 2 + planes, 4 + planes)):
        wide = pick_right(pick_left(pool_y, grad), pool_z)
        for p in range(first, last):
            work_ref[p] = wide * sw_ref[p]

    def body(p, _):
        x = work_ref[p] + work_ref[p + 4] + 2.0 * (work_ref[p + 1] + work_ref[p + 3]) + 3.0 * work_ref[p + 2]
        out_ref[p] = smooth_y(smooth_z(x))[:, :fz]
        return 0

    lax.fori_loop(0, planes, body, 0)


def shape(*dims, dtype=F32):
    return jax.ShapeDtypeStruct(dims, dtype)


def on_device(design, force, clamped_dof_mask, stiffness):
    planes, fy, fz = design.shape
    _, bx, by, _ = force.shape
    gx = lax.axis_size("gx")
    gy = lax.axis_size("gy")
    roles = lax.axis_size("role")
    devices = gx * gy * roles
    slabs = gx * gy
    assert roles == 2 and planes == 4 and fz == LANES and bx == 2 * gy and slabs % 2 == 0
    columns = fy // 4
    nodes = fy // 2
    tiles = nodes + 2
    count = tiles * 8
    pairs_a = [(i, i ^ 1) for i in range(slabs)]
    pairs_b = [(i, i + 1 if i % 2 else i - 1) for i in range(1, slabs - 1)]

    def beside(to_a, to_b):
        return lax.ppermute(to_a, LINE, pairs_a), lax.ppermute(to_b, LINE, pairs_b)

    free0 = (1 - clamped_dof_mask[:, 0]).astype(F32)
    next_plane = lax.ppermute(
        jnp.concatenate([free0 * force[:, 0], free0], axis=0), "gx", [(i + 1, i) for i in range(gx - 1)]
    )
    design_a, design_b = beside(design, design)
    pack, table = pl.pallas_call(
        prep_kernel,
        out_shape=(shape(gy, 6, 3, by, fz), shape(2 * ROWS, 2 * ROWS, dtype=BF16)),
        name="prep",
    )(force, clamped_dof_mask, next_plane, stiffness, jnp.asarray(place_table()))
    rf = lax.all_to_all(pack, "gy", 0, 0)

    role = lax.axis_index("role")

    def strip(x):
        return jnp.where(role == 0, x[..., fz - STRIP :], x[..., :STRIP]).reshape(-1, STRIP)

    strips = jnp.concatenate([strip(design), strip(design_a), strip(design_b), strip(rf)], axis=0)
    strips = lax.ppermute(strips, "role", [(0, 1), (1, 0)])

    node_set = shape(3 * count, LANES)
    plane = shape(count, LANES)
    element = shape(columns, LANES)
    tile_scratch = [
        pltpu.VMEM((3, tiles, 16, LANES), BF16),
        pltpu.VMEM((2, tiles, 16, LANES), BF16),
        pltpu.VMEM((2, count, LANES), F32),
    ]
    shift32 = pltpu.VMEM((2, count, LANES), F32)
    sw, factor, density, v0, free, local, to_a, to_b, e00 = pl.pallas_call(
        first_kernel,
        out_shape=(shape(planes + 4, fy, 2 * fz), element, element, node_set, node_set, node_set, plane, plane, element),
        scratch_shapes=[pltpu.VMEM((3 * planes, fy, 2 * fz), F32), pltpu.VMEM((fy, 2 * fz), F32)] + tile_scratch,
        name="first",
    )(design, design_a, design_b, strips, rf, table)
    from_a, from_b = beside(to_a, to_b)
    v1, local, to_a, to_b, e01, e11 = pl.pallas_call(
        second_kernel,
        out_shape=(node_set, node_set, plane, plane, element, element),
        scratch_shapes=tile_scratch + [shift32],
        name="second",
    )(v0, free, local, from_a, from_b, factor, table)
    from_a, from_b = beside(to_a, to_b)
    v2, e02, e12, e22, moments = pl.pallas_call(
        third_kernel,
        out_shape=(node_set, element, element, element, shape(devices, LANES)),
        scratch_shapes=tile_scratch + [shift32, shift32],
        name="third",
    )(v0, v1, free, local, from_a, from_b, factor, table, e00, e01, e11)
    moments = lax.all_to_all(moments, ("role", "gx", "gy"), 0, 0, tiled=True)
    grad, u = pl.pallas_call(
        combine_kernel,
        out_shape=(element, shape(gy, 3, 2, by, fz)),
        scratch_shapes=[pltpu.VMEM((2 * count, LANES), F32)],
        name="combine",
    )(moments, v0, v1, v2, e00, e01, e11, e02, e12, e22, density)
    grad_a, grad_b = beside(grad, grad)
    sensitivity = pl.pallas_call(
        last_kernel,
        out_shape=shape(planes, fy, fz),
        scratch_shapes=[pltpu.VMEM((planes + 4, fy, 2 * fz), F32)],
        name="last",
    )(grad, grad_a, grad_b, sw)
    u = lax.all_to_all(u, "gy", 0, 0)
    displacement = jnp.transpose(u, (1, 0, 2, 3, 4)).reshape(3, bx, by, fz)
    return sensitivity, displacement


def solution(mesh):
    placed = (
        P(("gx", "gy"), None, "role"),
        P(None, "gx", "gy", "role"),
        P(None, "gx", "gy", "role"),
        P(),
    )
    return jax.shard_map(
        on_device,
        mesh=mesh,
        in_specs=placed,
        out_specs=(P(("gx", "gy"), None, "role"), P(None, "gx", "gy", "role")),
        check_vma=False,
    )
```

time: 510 us -> 115 us (0.23); the launches traced: 500 us -> 114 us
  blocking collectives: 208 us -> 12.4 us
  local copies, waits for them, and re-layouts: 80 us -> 5.35 us
  starting transfers between devices: 88.6 us -> 31.5 us
  waiting for transfers between devices: 63.2 us -> 24.7 us
  Pallas kernels: 0 us -> 35.9 us
  other arithmetic: 27.6 us -> 3.17 us
  matrix products: 23.6 us -> 0 us
  between operations: 9.15 us -> 0.78 us
    psum x5 -> x0, blocking collectives: 203 us -> none  [inner_sum(): return lax.psum(local_part, ('role', 'gx', 'gy'))]
    ppermute x32 -> x10, starting transfers between devices: 83.7 us -> 21.4 us  [the longest x4 14.4 us: beside(): lax.ppermute(to_b, LINE, pairs_b)]
    slice x34 -> x0, local copies, waits for them, and re-layouts: 47.1 us -> none  [the longest x12 42.4 us: split_axis(): lax.slice_in_dim(values, corner, corner + 2 * half_len - 1, stride=2, axi...]
    ppermute x32 -> x10, waiting for transfers between devices: 63.2 us -> 17.6 us  [the longest x4 12.9 us: beside(): lax.ppermute(to_b, LINE, pairs_b)]
    pallas_call x0 -> x6, Pallas kernels: none -> 35.9 us  [the longest x1 12.2 us: on_device(): pl.pallas_call(first_kernel, out_shape=(shape(planes + 4, fy, 2 * fz), el...]
    dot_general x15 -> x0, matrix products: 23.6 us -> none  [the longest x4 8.2 us: split_nodes(): jnp.einsum('baqxyk,ckg->cbaqxyg', stacked, table, precision=lax.Precision...]
    reshape x11 -> x4, local copies, waits for them, and re-layouts: 11.9 us -> 0.45 us  [strip(): jnp.where(role == 0, x[..., fz - STRIP:], x[..., :STRIP]).reshape(-1, STRIP)]
    reduce_sum x7 -> x0, other arithmetic: 7.24 us -> none  [the longest x5 4.43 us: inner_sum(): local_part = jnp.sum((left * right)[:, :-1, :-1, :-1])]
  transfers between devices with their start and end apart: 33 -> 12, of which waited for: 22 -> 6; matrix products, arithmetic and copies ran while one was open for 6% -> 3% of each run, Pallas kernels for 0% -> 6%
where the time goes in v1:
time: 115 us; the launch traced here: 114 us
  Pallas kernels  35.9 us (31%)
  starting transfers between devices  31.5 us (27%)
  waiting for transfers between devices  24.7 us (21%)
  blocking collectives  12.4 us (11%)
  local copies, waits for them, and re-layouts  5.35 us (5%)
  other arithmetic  3.17 us (3%)
    ppermute x4, starting transfers between devices, beside(): lax.ppermute(to_b, LINE, pairs_b)  14.4 us
    ppermute x4, waiting for transfers between devices, beside(): lax.ppermute(to_b, LINE, pairs_b)  12.9 us
    all_to_all x1, blocking collectives, on_device(): moments = lax.all_to_all(moments, ('role', 'gx', 'gy'), 0, 0, tiled=True)  12.4 us
    pallas_call x1, Pallas kernels, on_device(): pl.pallas_call(first_kernel, out_shape=(shape(planes + 4, fy, 2 * fz), el...  12.2 us
    pallas_call x1, Pallas kernels, on_device(): pl.pallas_call(second_kernel, out_shape=(node_set, node_set, plane, plane...  7.44 us
    all_to_all x1, waiting for transfers between devices, on_device(): rf = lax.all_to_all(pack, 'gy', 0, 0)  7.19 us
    pallas_call x1, Pallas kernels, on_device(): pl.pallas_call(third_kernel, out_shape=(node_set, element, element, eleme...  6.9 us
    all_to_all x1, starting transfers between devices, on_device(): u = lax.all_to_all(u, 'gy', 0, 0)  5.22 us
  transfers between devices with their start and end apart: 12, of which 6 were waited for; matrix products, arithmetic and copies ran while one was open for 3% of the time, Pallas kernels for 6%

profile of v1, /device:TPU:3, one launch (start us, length us, event | category | flops | bytes accessed | tf_op | source)
XLA Modules:
  0.0 113.8 jit_solution(14876680404898671069)
XLA Ops:
  0.6 3.7 %collective-permute-start.1 = (f32[4,128,128]{2,1,0:T(8,128)}, f32[4,128,128]{2,1,0:T(8,128)S(1)}, u32[]{:S(2)}, u32[]{:S(2)}) collective-permute-start(f32[4,128,128]{2,1,0:T(8,128)} %design_ref.1), channel_id=1, source_target_pairs={{1,2},{2,1},{3,4},{4,3},{5,6},{6,5},{7,8},{8,7},{9,10},{10,9},{11,... | collective-permute-start | bytes 786440 | tf_op jit(solution)/shard_map/ppermute | solution.py:507
  4.4 0.1 collective-permute-start
  4.5 0.7 fusion.1
  5.2 0.8 bitcast_multiply_fusion
  6.0 1.3 %collective-permute-start.2 = (f32[6,16,128]{2,1,0:T(8,128)S(1)}, f32[6,16,128]{2,1,0:T(8,128)S(1)}, u32[]{:S(2)}, u32[]{:S(2)}) collective-permute-start(f32[6,16,128]{2,1,0:T(8,128)S(1)} %pad_maximum_fusion.1), channel_id=1, source_target_pairs={{4,0},{8,4},{12,8},{5,1},{9,5},{13,9},{6,2},{10,6},{14,10},{7,3},{... | collective-permute-start | bytes 147464 | tf_op jit(solution)/shard_map/ppermute | solution.py:510
  7.3 1.2 %slice_select_fusion.3 = f32[4,128,8]{2,1,0:T(8,128)S(1)} fusion(f32[4,128,128]{2,1,0:T(8,128)} %design_ref.1, pred[]{:T(512)S(6)} %eq.2), kind=kLoop, calls=%fused_computation.3 | loop fusion | flops 4096 | bytes 49153 | tf_op jit(solution)/shard_map/jit(_where)/select_n | solution.py:524
  8.4 0.1 copy.14
  8.5 2.6 %collective-permute-done.2.next_ref = f32[6,16,128]{2,1,0:T(8,128)S(1)} collective-permute-done((f32[6,16,128]{2,1,0:T(8,128)S(1)}, f32[6,16,128]{2,1,0:T(8,128)S(1)}, u32[]{:S(2)}, u32[]{:S(2)}) %collective-permute-start.2) | collective-permute-done | bytes 49184 | tf_op jit(solution)/shard_map/ppermute | solution.py:510
  11.1 0.6 copy-done.7
  11.7 2.6 %prep.1 = (f32[4,6,3,16,128]{4,3,2,1,0:T(8,128)}, bf16[240,240]{1,0:T(8,128)(2,1)}) custom-call(f32[3,8,16,128]{3,2,1,0:T(8,128)} %force_ref.1, s32[3,8,16,128]{3,2,1,0:T(8,128)} %mask_ref.1, f32[6,16,128]{2,1,0:T(8,128)} %copy-done.7, f32[81,81]{1,0:T(8,128)} %stiff_ref.1, f32[120,81]{1,0:T(8,128)} %constant.12.clone.place_ref), custom_call_target="tpu_custom_call" | custom-call | tf_op jit(solution)/shard_map/prep/pallas_call | solution.py:514
  14.3 4.9 %all-to-all-start = ((f32[4,6,3,16,128]{4,3,2,1,0:T(8,128)}), f32[4,6,3,16,128]{4,3,2,1,0:T(8,128)S(1)}, u32[]{:S(2)}, u32[]{:S(2)}) async-start(f32[4,6,3,16,128]{4,3,2,1,0:T(8,128)} %get-tuple-element.26), calls=%async_computation | async-start | bytes 1179648 | tf_op jit(solution)/shard_map/all_to_all | solution.py:519
  19.2 0.0 collective-permute-done.1.db_ref
  19.2 0.1 slice_select_fusion.1
  19.3 0.1 copy.16
  19.4 0.0 collective-permute-done.da_ref
  19.4 0.1 slice_select_fusion.2
  19.5 0.1 copy.15
  19.6 7.2 %all-to-all-done.rf_ref = f32[4,6,3,16,128]{4,3,2,1,0:T(8,128)S(1)} async-done(((f32[4,6,3,16,128]{4,3,2,1,0:T(8,128)}), f32[4,6,3,16,128]{4,3,2,1,0:T(8,128)S(1)}, u32[]{:S(2)}, u32[]{:S(2)}) %all-to-all-start) | async-done | bytes 589856 | tf_op jit(solution)/shard_map/all_to_all | solution.py:519
  26.8 0.2 slice_select_fusion
  27.1 0.2 copy.17
  27.3 1.3 %collective-permute-start.3 = (f32[2688,8]{0,1:T(8,128)S(1)}, f32[2688,8]{0,1:T(8,128)S(1)}, u32[]{:S(2)}, u32[]{:S(2)}) collective-permute-start(f32[2688,8]{0,1:T(8,128)S(1)} %pad_maximum_fusion), channel_id=1, source_target_pairs={{0,16},{16,0},{1,17},{17,1},{2,18},{18,2},{3,19},{19,3},{4,20},{20... | collective-permute-start | bytes 258056 | tf_op jit(solution)/shard_map/ppermute | solution.py:527
  28.6 2.1 %collective-permute-done.3 = f32[2688,8]{0,1:T(8,128)S(1)} collective-permute-done((f32[2688,8]{0,1:T(8,128)S(1)}, f32[2688,8]{0,1:T(8,128)S(1)}, u32[]{:S(2)}, u32[]{:S(2)}) %collective-permute-start.3) | collective-permute-done | bytes 86048 | tf_op jit(solution)/shard_map/ppermute | solution.py:527
  30.7 1.6 %copy.18.strip_ref = f32[2688,8]{1,0:T(8,128)} copy(f32[2688,8]{0,1:T(8,128)S(1)} %collective-permute-done.3) | data formatting | bytes 172032 | tf_op jit(solution)/shard_map/ppermute | solution.py:527
  32.2 12.2 %first.1 = (f32[8,128,256]{2,1,0:T(8,128)}, f32[32,128]{1,0:T(8,128)}, f32[32,128]{1,0:T(8,128)}, f32[1584,128]{1,0:T(8,128)}, f32[1584,128]{1,0:T(8,128)}, /*in...) custom-call(f32[4,128,128]{2,1,0:T(8,128)} %design_ref.1, ...), custom_call_target="tpu_custom_call" | custom-call | tf_op jit(solution)/shard_map/first/pallas_call | solution.py:538
  44.4 1.7 %collective-permute-start.4 = (f32[528,128]{1,0:T(8,128)}, f32[528,128]{1,0:T(8,128)S(1)}, u32[]{:S(2)}, u32[]{:S(2)}) collective-permute-start(f32[528,128]{1,0:T(8,128)} %get-tuple-element.31), channel_id=1, source_target_pairs={{0,1},{1,0},{2,3},{3,2},{4,5},{5,4},{6,7},{7,6},{8,9},{9,8},{10,11... | collective-permute-start | bytes 811016 | tf_op jit(solution)/shard_map/ppermute | solution.py:507
  46.2 4.2 %collective-permute-start.5 = (f32[528,128]{1,0:T(8,128)}, f32[528,128]{1,0:T(8,128)S(1)}, u32[]{:S(2)}, u32[]{:S(2)}) collective-permute-start(f32[528,128]{1,0:T(8,128)} %get-tuple-element.32), channel_id=1, source_target_pairs={{1,2},{2,1},{3,4},{4,3},{5,6},{6,5},{7,8},{8,7},{9,10},{10,9},{11,... | collective-permute-start | bytes 811016 | tf_op jit(solution)/shard_map/ppermute | solution.py:507
  50.3 0.0 collective-permute-done.4.from_a
  50.3 4.8 %collective-permute-done.5.from_b = f32[528,128]{1,0:T(8,128)S(1)} collective-permute-done((f32[528,128]{1,0:T(8,128)}, f32[528,128]{1,0:T(8,128)S(1)}, u32[]{:S(2)}, u32[]{:S(2)}) %collective-permute-start.5) | collective-permute-done | bytes 270368 | tf_op jit(solution)/shard_map/ppermute | solution.py:507
  55.1 0.7 copy-done.4
  55.8 7.4 %second.1 = (f32[1584,128]{1,0:T(8,128)}, f32[1584,128]{1,0:T(8,128)}, f32[528,128]{1,0:T(8,128)}, f32[528,128]{1,0:T(8,128)}, f32[32,128]{1,0:T(8,128)}, /*index=5*/f32[32,128]{1,0:T(8,128)}) custom-call(f32[1584,128]{1,0:T(8,128)} %get-tuple-element.28.prev_ref.v0_ref, f32[1584,128]{1,0:T(8,128)} %get-tuple-element.29.free_ref, ...), custom_call_target="tpu_custom_call" | custom-call | tf_op jit(solution)/shard_map/second/pallas_call | solution.py:545
  63.3 1.9 %collective-permute-start.6 = (f32[528,128]{1,0:T(8,128)}, f32[528,128]{1,0:T(8,128)S(1)}, u32[]{:S(2)}, u32[]{:S(2)}) collective-permute-start(f32[528,128]{1,0:T(8,128)} %get-tuple-element.36), channel_id=1, source_target_pairs={{0,1},{1,0},{2,3},{3,2},{4,5},{5,4},{6,7},{7,6},{8,9},{9,8},{10,11... | collective-permute-start | bytes 811016 | tf_op jit(solution)/shard_map/ppermute | solution.py:507
  65.2 4.6 %collective-permute-start.7 = (f32[528,128]{1,0:T(8,128)}, f32[528,128]{1,0:T(8,128)S(1)}, u32[]{:S(2)}, u32[]{:S(2)}) collective-permute-start(f32[528,128]{1,0:T(8,128)} %get-tuple-element.37), channel_id=1, source_target_pairs={{1,2},{2,1},{3,4},{4,3},{5,6},{6,5},{7,8},{8,7},{9,10},{10,9},{11,... | collective-permute-start | bytes 811016 | tf_op jit(solution)/shard_map/ppermute | solution.py:507
  69.9 0.0 collective-permute-done.6.from_a
  69.9 4.4 %collective-permute-done.7.from_b = f32[528,128]{1,0:T(8,128)S(1)} collective-permute-done((f32[528,128]{1,0:T(8,128)}, f32[528,128]{1,0:T(8,128)S(1)}, u32[]{:S(2)}, u32[]{:S(2)}) %collective-permute-start.7) | collective-permute-done | bytes 270368 | tf_op jit(solution)/shard_map/ppermute | solution.py:507
  74.3 0.7 copy-done.6
  75.0 6.9 %third.1 = (f32[1584,128]{1,0:T(8,128)}, f32[32,128]{1,0:T(8,128)}, f32[32,128]{1,0:T(8,128)}, f32[32,128]{1,0:T(8,128)}, f32[32,128]{1,0:T(8,128)}) custom-call(f32[1584,128]{1,0:T(8,128)} %get-tuple-element.28.prev_ref.v0_ref, f32[1584,128]{1,0:T(8,128)} %get-tuple-element.34.v1_ref, f32[1584,128]{1,0:T(8,128)} %get-tuple-element.29.free_ref, ...), custom_call_target="tpu_custom_call" | custom-call | tf_op jit(solution)/shard_map/third/pallas_call | solution.py:552
  81.9 12.4 %all_to_all.21 = f32[32,1,128]{2,1,0:T(1,128)} all-to-all(f32[32,1,128]{2,1,0:T(1,128)} %bitcast.33), channel_id=1, replica_groups=mesh['role'=2,'gx'=4,'gy'=4] {'role','gx','gy'}, dimensions={0} | all-to-all | bytes 32768 | tf_op jit(solution)/shard_map/all_to_all | solution.py:558
  94.3 3.0 %combine.1 = (f32[32,128]{1,0:T(8,128)}, f32[4,3,2,16,128]{4,3,2,1,0:T(8,128)}) custom-call(f32[32,128]{1,0:T(8,128)} %bitcast.32, f32[1584,128]{1,0:T(8,128)} %get-tuple-element.28.prev_ref.v0_ref, f32[1584,128]{1,0:T(8,128)} %get-tuple-element.34.v1_ref, f32[1584,128]{1,0:T(8,128)} %get-tuple-element.42.v2_ref, f32[32,128]{1,0:T(8,128)} %get-tuple-element.38.e00_ref, ...), custom_call_target="tpu_custom_call" | custom-call | tf_op jit(solution)/shard_map/combine/pallas_call | solution.py:559
  97.4 5.2 %all-to-all-start.2 = ((f32[4,3,2,16,128]{4,3,2,1,0:T(8,128)}), f32[4,3,2,16,128]{4,3,2,1,0:T(8,128)S(1)}, u32[]{:S(2)}, u32[]{:S(2)}) async-start(f32[4,3,2,16,128]{4,3,2,1,0:T(8,128)} %get-tuple-element.49), calls=%async_computation.2 | async-start | bytes 393216 | tf_op jit(solution)/shard_map/all_to_all | solution.py:572
  102.6 1.9 %collective-permute-start.9 = (f32[32,128]{1,0:T(8,128)}, f32[32,128]{1,0:T(8,128)S(1)}, u32[]{:S(2)}, u32[]{:S(2)}) collective-permute-start(f32[32,128]{1,0:T(8,128)} %get-tuple-element.47.grad_ref), channel_id=1, source_target_pairs={{1,2},{2,1},{3,4},{4,3},{5,6},{6,5},{7,8},{8,7},{9,10},{10,9},{11,... | collective-permute-start | bytes 49160 | tf_op jit(solution)/shard_map/ppermute | solution.py:507
  104.5 0.6 collective-permute-start.8
  105.1 3.7 %collective-permute-done.9.gb_ref = f32[32,128]{1,0:T(8,128)S(1)} collective-permute-done((f32[32,128]{1,0:T(8,128)}, f32[32,128]{1,0:T(8,128)S(1)}, u32[]{:S(2)}, u32[]{:S(2)}) %collective-permute-start.9) | collective-permute-done | bytes 16416 | tf_op jit(solution)/shard_map/ppermute | solution.py:507
  108.8 0.0 collective-permute-done.8.ga_ref
  108.8 0.6 copy-done.8
  109.4 0.0 copy-done.9
  109.4 3.8 %last.1 = f32[4,128,128]{2,1,0:T(8,128)} custom-call(f32[32,128]{1,0:T(8,128)} %get-tuple-element.47.grad_ref, f32[32,128]{1,0:T(8,128)} %copy-done.9, f32[32,128]{1,0:T(8,128)} %copy-done.8, f32[8,128,256]{2,1,0:T(8,128)} %get-tuple-element.48.sw_ref), custom_call_target="tpu_custom_call" | custom-call | tf_op jit(solution)/shard_map/last/pallas_call | solution.py:566
  113.1 0.0 all-to-all-done.2
  113.1 0.7 copy.20
  (17 shorter events, 0.0 us)
Async XLA Ops:
  0.6 18.5 %collective-permute-start.1 = (f32[4,128,128]{2,1,0:T(8,128)}, f32[4,128,128]{2,1,0:T(8,128)S(1)}, u32[]{:S(2)}, u32[]{:S(2)}) collective-permute-start(f32[4,128,128]{2,1,0:T(8,128)} %design_ref.1), channel_id=1, source_target_pairs={{1,2},{2,1},{3,4},{4,3},{5,6},{6,5},{7,8},{8,7},{9,10},{10,9},{11,... | collective-permute-start | bytes 786440 | tf_op jit(solution)/shard_map/ppermute | solution.py:507
  4.4 15.0 %collective-permute-start = (f32[4,128,128]{2,1,0:T(8,128)}, f32[4,128,128]{2,1,0:T(8,128)S(1)}, u32[]{:S(2)}, u32[]{:S(2)}) collective-permute-start(f32[4,128,128]{2,1,0:T(8,128)} %design_ref.1), channel_id=1, source_target_pairs={{0,1},{1,0},{2,3},{3,2},{4,5},{5,4},{6,7},{7,6},{8,9},{9,8},{10,11... | collective-permute-start | bytes 786440 | tf_op jit(solution)/shard_map/ppermute | solution.py:507
  6.0 5.1 %collective-permute-start.2 = (f32[6,16,128]{2,1,0:T(8,128)S(1)}, f32[6,16,128]{2,1,0:T(8,128)S(1)}, u32[]{:S(2)}, u32[]{:S(2)}) collective-permute-start(f32[6,16,128]{2,1,0:T(8,128)S(1)} %pad_maximum_fusion.1), channel_id=1, source_target_pairs={{4,0},{8,4},{12,8},{5,1},{9,5},{13,9},{6,2},{10,6},{14,10},{7,3},{... | collective-permute-start | bytes 147464 | tf_op jit(solution)/shard_map/ppermute | solution.py:510
  11.1 0.6 copy-start.7
  14.3 12.6 %all-to-all-start = ((f32[4,6,3,16,128]{4,3,2,1,0:T(8,128)}), f32[4,6,3,16,128]{4,3,2,1,0:T(8,128)S(1)}, u32[]{:S(2)}, u32[]{:S(2)}) async-start(f32[4,6,3,16,128]{4,3,2,1,0:T(8,128)} %get-tuple-element.26), calls=%async_computation | async-start | bytes 1179648 | tf_op jit(solution)/shard_map/all_to_all | solution.py:519
  19.2 7.9 %copy-start.1 = (f32[4,128,128]{2,1,0:T(8,128)}, f32[4,128,128]{2,1,0:T(8,128)S(1)}, u32[]{:S(2)}) copy-start(f32[4,128,128]{2,1,0:T(8,128)S(1)} %collective-permute-done.1.db_ref) | copy-start | bytes 786436
  19.4 7.7 %copy-start.2 = (f32[4,128,128]{2,1,0:T(8,128)}, f32[4,128,128]{2,1,0:T(8,128)S(1)}, u32[]{:S(2)}) copy-start(f32[4,128,128]{2,1,0:T(8,128)S(1)} %collective-permute-done.da_ref) | copy-start | bytes 786436
  26.8 5.4 %copy-start = (f32[4,6,3,16,128]{4,3,2,1,0:T(8,128)}, f32[4,6,3,16,128]{4,3,2,1,0:T(8,128)S(1)}, u32[]{:S(2)}) copy-start(f32[4,6,3,16,128]{4,3,2,1,0:T(8,128)S(1)} %all-to-all-done.rf_ref) | copy-start | bytes 1769476
  27.3 3.4 %collective-permute-start.3 = (f32[2688,8]{0,1:T(8,128)S(1)}, f32[2688,8]{0,1:T(8,128)S(1)}, u32[]{:S(2)}, u32[]{:S(2)}) collective-permute-start(f32[2688,8]{0,1:T(8,128)S(1)} %pad_maximum_fusion), channel_id=1, source_target_pairs={{0,16},{16,0},{1,17},{17,1},{2,18},{18,2},{3,19},{19,3},{4,20},{20... | collective-permute-start | bytes 258056 | tf_op jit(solution)/shard_map/ppermute | solution.py:527
  44.4 5.9 %collective-permute-start.4 = (f32[528,128]{1,0:T(8,128)}, f32[528,128]{1,0:T(8,128)S(1)}, u32[]{:S(2)}, u32[]{:S(2)}) collective-permute-start(f32[528,128]{1,0:T(8,128)} %get-tuple-element.31), channel_id=1, source_target_pairs={{0,1},{1,0},{2,3},{3,2},{4,5},{5,4},{6,7},{7,6},{8,9},{9,8},{10,11... | collective-permute-start | bytes 811016 | tf_op jit(solution)/shard_map/ppermute | solution.py:507
  46.2 9.0 %collective-permute-start.5 = (f32[528,128]{1,0:T(8,128)}, f32[528,128]{1,0:T(8,128)S(1)}, u32[]{:S(2)}, u32[]{:S(2)}) collective-permute-start(f32[528,128]{1,0:T(8,128)} %get-tuple-element.32), channel_id=1, source_target_pairs={{1,2},{2,1},{3,4},{4,3},{5,6},{6,5},{7,8},{8,7},{9,10},{10,9},{11,... | collective-permute-start | bytes 811016 | tf_op jit(solution)/shard_map/ppermute | solution.py:507
  50.3 4.8 %copy-start.3 = (f32[528,128]{1,0:T(8,128)}, f32[528,128]{1,0:T(8,128)S(1)}, u32[]{:S(2)}) copy-start(f32[528,128]{1,0:T(8,128)S(1)} %collective-permute-done.4.from_a) | copy-start | bytes 811012
  55.1 0.7 copy-start.4
  63.3 6.6 %collective-permute-start.6 = (f32[528,128]{1,0:T(8,128)}, f32[528,128]{1,0:T(8,128)S(1)}, u32[]{:S(2)}, u32[]{:S(2)}) collective-permute-start(f32[528,128]{1,0:T(8,128)} %get-tuple-element.36), channel_id=1, source_target_pairs={{0,1},{1,0},{2,3},{3,2},{4,5},{5,4},{6,7},{7,6},{8,9},{9,8},{10,11... | collective-permute-start | bytes 811016 | tf_op jit(solution)/shard_map/ppermute | solution.py:507
  65.2 9.1 %collective-permute-start.7 = (f32[528,128]{1,0:T(8,128)}, f32[528,128]{1,0:T(8,128)S(1)}, u32[]{:S(2)}, u32[]{:S(2)}) collective-permute-start(f32[528,128]{1,0:T(8,128)} %get-tuple-element.37), channel_id=1, source_target_pairs={{1,2},{2,1},{3,4},{4,3},{5,6},{6,5},{7,8},{8,7},{9,10},{10,9},{11,... | collective-permute-start | bytes 811016 | tf_op jit(solution)/shard_map/ppermute | solution.py:507
  69.9 4.4 %copy-start.5 = (f32[528,128]{1,0:T(8,128)}, f32[528,128]{1,0:T(8,128)S(1)}, u32[]{:S(2)}) copy-start(f32[528,128]{1,0:T(8,128)S(1)} %collective-permute-done.6.from_a) | copy-start | bytes 811012
  74.3 0.7 copy-start.6
  97.4 15.7 %all-to-all-start.2 = ((f32[4,3,2,16,128]{4,3,2,1,0:T(8,128)}), f32[4,3,2,16,128]{4,3,2,1,0:T(8,128)S(1)}, u32[]{:S(2)}, u32[]{:S(2)}) async-start(f32[4,3,2,16,128]{4,3,2,1,0:T(8,128)} %get-tuple-element.49), calls=%async_computation.2 | async-start | bytes 393216 | tf_op jit(solution)/shard_map/all_to_all | solution.py:572
  102.6 6.2 %collective-permute-start.9 = (f32[32,128]{1,0:T(8,128)}, f32[32,128]{1,0:T(8,128)S(1)}, u32[]{:S(2)}, u32[]{:S(2)}) collective-permute-start(f32[32,128]{1,0:T(8,128)} %get-tuple-element.47.grad_ref), channel_id=1, source_target_pairs={{1,2},{2,1},{3,4},{4,3},{5,6},{6,5},{7,8},{8,7},{9,10},{10,9},{11,... | collective-permute-start | bytes 49160 | tf_op jit(solution)/shard_map/ppermute | solution.py:507
  104.5 4.2 %collective-permute-start.8 = (f32[32,128]{1,0:T(8,128)}, f32[32,128]{1,0:T(8,128)S(1)}, u32[]{:S(2)}, u32[]{:S(2)}) collective-permute-start(f32[32,128]{1,0:T(8,128)} %get-tuple-element.47.grad_ref), channel_id=1, source_target_pairs={{0,1},{1,0},{2,3},{3,2},{4,5},{5,4},{6,7},{7,6},{8,9},{9,8},{10,11... | collective-permute-start | bytes 49160 | tf_op jit(solution)/shard_map/ppermute | solution.py:507
  108.8 0.6 copy-start.8
  108.8 0.6 copy-start.9

commit v2 on v1

--- a/solution.py
+++ b/solution.py
@@ -15,6 +15,7 @@
 STRIP = 8
 ROWS = 120
 LINE = ("gx", "gy")
+KEEP = pltpu.CompilerParams(vmem_limit_bytes=20 << 20)
 F32 = jnp.float32
 BF16 = jnp.bfloat16
 
@@ -515,6 +516,7 @@
         prep_kernel,
         out_shape=(shape(gy, 6, 3, by, fz), shape(2 * ROWS, 2 * ROWS, dtype=BF16)),
         name="prep",
+        compiler_params=KEEP,
     )(force, clamped_dof_mask, next_plane, stiffness, jnp.asarray(place_table()))
     rf = lax.all_to_all(pack, "gy", 0, 0)
 
@@ -540,6 +542,7 @@
         out_shape=(shape(planes + 4, fy, 2 * fz), element, element, node_set, node_set, node_set, plane, plane, element),
         scratch_shapes=[pltpu.VMEM((3 * planes, fy, 2 * fz), F32), pltpu.VMEM((fy, 2 * fz), F32)] + tile_scratch,
         name="first",
+        compiler_params=KEEP,
     )(design, design_a, design_b, strips, rf, table)
     from_a, from_b = beside(to_a, to_b)
     v1, local, to_a, to_b, e01, e11 = pl.pallas_call(
@@ -547,6 +550,7 @@
         out_shape=(node_set, node_set, plane, plane, element, element),
         scratch_shapes=tile_scratch + [shift32],
         name="second",
+        compiler_params=KEEP,
     )(v0, free, local, from_a, from_b, factor, table)
     from_a, from_b = beside(to_a, to_b)
     v2, e02, e12, e22, moments = pl.pallas_call(
@@ -554,6 +558,7 @@
         out_shape=(node_set, element, element, element, shape(devices, LANES)),
         scratch_shapes=tile_scratch + [shift32, shift32],
         name="third",
+        compiler_params=KEEP,
     )(v0, v1, free, local, from_a, from_b, factor, table, e00, e01, e11)
     moments = lax.all_to_all(moments, ("role", "gx", "gy"), 0, 0, tiled=True)
     grad, u = pl.pallas_call(
@@ -561,6 +566,7 @@
         out_shape=(element, shape(gy, 3, 2, by, fz)),
         scratch_shapes=[pltpu.VMEM((2 * count, LANES), F32)],
         name="combine",
+        compiler_params=KEEP,
     )(moments, v0, v1, v2, e00, e01, e11, e02, e12, e22, density)
     grad_a, grad_b = beside(grad, grad)
     sensitivity = pl.pallas_call(
@@ -568,6 +574,7 @@
         out_shape=shape(planes, fy, fz),
         scratch_shapes=[pltpu.VMEM((planes + 4, fy, 2 * fz), F32)],
         name="last",
+        compiler_params=KEEP,
     )(grad, grad_a, grad_b, sw)
     u = lax.all_to_all(u, "gy", 0, 0)
     displacement = jnp.transpose(u, (1, 0, 2, 3, 4)).reshape(3, bx, by, fz)

time: 115 us -> 99.7 us (0.87)
  Pallas kernels: 35.9 us -> 23 us
    pallas_call x1, Pallas kernels: 12.2 us -> 8.81 us  [on_device(): pl.pallas_call(first_kernel, out_shape=(shape(planes + 4, fy, 2 * fz), el...]
    pallas_call x1, Pallas kernels: 7.44 us -> 4.6 us  [on_device(): pl.pallas_call(second_kernel, out_shape=(node_set, node_set, plane, plane...]
    pallas_call x1, Pallas kernels: 6.9 us -> 4.23 us  [on_device(): pl.pallas_call(third_kernel, out_shape=(node_set, element, element, eleme...]
    pallas_call x1, Pallas kernels: 3.04 us -> 1.36 us  [on_device(): pl.pallas_call(combine_kernel, out_shape=(element, shape(gy, 3, 2, by, fz...]
    pallas_call x1, Pallas kernels: 3.76 us -> 2.48 us  [on_device(): pl.pallas_call(last_kernel, out_shape=shape(planes, fy, fz), scratch_shap...]
    unnamed x20 -> x14, local copies, waits for them, and re-layouts: 2.65 us -> 2.64 us
  transfers between devices with their start and end apart: 12 -> 12, of which waited for: 6 -> 6; matrix products, arithmetic and copies ran while one was open for 3% -> 3% of each run, Pallas kernels for 6% -> 4%
where the time goes in v2:
time: 99.7 us; the launch traced here: 99.1 us
  starting transfers between devices  31.5 us (32%)
  waiting for transfers between devices  24.2 us (24%)
  Pallas kernels  23 us (23%)
  blocking collectives  12.3 us (12%)
  local copies, waits for them, and re-layouts  4.21 us (4%)
  other arithmetic  3.17 us (3%)
    ppermute x4, starting transfers between devices, beside(): lax.ppermute(to_b, LINE, pairs_b)  14.6 us
    all_to_all x1, blocking collectives, on_device(): moments = lax.all_to_all(moments, ('role', 'gx', 'gy'), 0, 0, tiled=True)  12.3 us
    ppermute x4, waiting for transfers between devices, beside(): lax.ppermute(to_b, LINE, pairs_b)  12.3 us
    pallas_call x1, Pallas kernels, on_device(): pl.pallas_call(first_kernel, out_shape=(shape(planes + 4, fy, 2 * fz), el...  8.81 us
    all_to_all x1, waiting for transfers between devices, on_device(): rf = lax.all_to_all(pack, 'gy', 0, 0)  7.19 us
    all_to_all x1, starting transfers between devices, on_device(): u = lax.all_to_all(u, 'gy', 0, 0)  5.07 us
    all_to_all x1, starting transfers between devices, on_device(): rf = lax.all_to_all(pack, 'gy', 0, 0)  4.88 us
    pallas_call x1, Pallas kernels, on_device(): pl.pallas_call(second_kernel, out_shape=(node_set, node_set, plane, plane...  4.6 us
  transfers between devices with their start and end apart: 12, of which 6 were waited for; matrix products, arithmetic and copies ran while one was open for 3% of the time, Pallas kernels for 4%

profile of v2, /device:TPU:3, one launch (start us, length us, event | category | flops | bytes accessed | tf_op | source)
XLA Modules:
  0.0 99.1 jit_solution(5954028971649650725)
XLA Ops:
  0.6 0.0 copy-start.3
  0.6 0.0 copy-start.4
  0.7 3.9 %collective-permute-start.1 = (f32[4,128,128]{2,1,0:T(8,128)}, f32[4,128,128]{2,1,0:T(8,128)S(1)}, u32[]{:S(2)}, u32[]{:S(2)}) collective-permute-start(f32[4,128,128]{2,1,0:T(8,128)} %design_ref.1), channel_id=1, source_target_pairs={{1,2},{2,1},{3,4},{4,3},{5,6},{6,5},{7,8},{8,7},{9,10},{10,9},{11,... | collective-permute-start | bytes 786440 | tf_op jit(solution)/shard_map/ppermute | solution.py:508
  4.5 0.1 collective-permute-start
  4.6 0.7 fusion.1
  5.4 0.8 bitcast_multiply_fusion
  6.1 1.3 %collective-permute-start.2 = (f32[6,16,128]{2,1,0:T(8,128)S(1)}, f32[6,16,128]{2,1,0:T(8,128)S(1)}, u32[]{:S(2)}, u32[]{:S(2)}) collective-permute-start(f32[6,16,128]{2,1,0:T(8,128)S(1)} %pad_maximum_fusion.1), channel_id=1, source_target_pairs={{4,0},{8,4},{12,8},{5,1},{9,5},{13,9},{6,2},{10,6},{14,10},{7,3},{... | collective-permute-start | bytes 147464 | tf_op jit(solution)/shard_map/ppermute | solution.py:511
  7.4 1.2 %slice_select_fusion.3 = f32[4,128,8]{2,1,0:T(8,128)S(1)} fusion(f32[4,128,128]{2,1,0:T(8,128)} %design_ref.1, pred[]{:T(512)S(6)} %eq.2), kind=kLoop, calls=%fused_computation.3 | loop fusion | flops 4096 | bytes 49153 | tf_op jit(solution)/shard_map/jit(_where)/select_n | solution.py:526
  8.6 0.1 copy.14
  8.7 2.6 %collective-permute-done.2.next_ref = f32[6,16,128]{2,1,0:T(8,128)S(1)} collective-permute-done((f32[6,16,128]{2,1,0:T(8,128)S(1)}, f32[6,16,128]{2,1,0:T(8,128)S(1)}, u32[]{:S(2)}, u32[]{:S(2)}) %collective-permute-start.2) | collective-permute-done | bytes 49184 | tf_op jit(solution)/shard_map/ppermute | solution.py:511
  11.3 0.8 copy-done.5
  12.1 0.8 copy-done.6
  12.9 1.5 %prep.1 = (f32[4,6,3,16,128]{4,3,2,1,0:T(8,128)}, bf16[240,240]{1,0:T(8,128)(2,1)S(1)}) custom-call(f32[3,8,16,128]{3,2,1,0:T(8,128)S(1)} %copy-done.4, s32[3,8,16,128]{3,2,1,0:T(8,128)S(1)} %copy-done.3, f32[6,16,128]{2,1,0:T(8,128)S(1)} %collective-permute-done.2.next_ref, f32[81,81]{1,0:T(8,128)S(1)} %copy-done.6, f32[120,81]{1,0:T(8,128)S(1)} %copy-done.5), custom_call_target="tpu_custom_call" | custom-call | tf_op jit(solution)/shard_map/prep/pallas_call | solution.py:515
  14.4 4.9 %all-to-all-start = ((f32[4,6,3,16,128]{4,3,2,1,0:T(8,128)}), f32[4,6,3,16,128]{4,3,2,1,0:T(8,128)S(1)}, u32[]{:S(2)}, u32[]{:S(2)}) async-start(f32[4,6,3,16,128]{4,3,2,1,0:T(8,128)} %get-tuple-element.26), calls=%async_computation | async-start | bytes 1179648 | tf_op jit(solution)/shard_map/all_to_all | solution.py:521
  19.2 0.0 collective-permute-done.1.db_ref
  19.2 0.1 slice_select_fusion.1
  19.4 0.1 copy.16
  19.5 0.0 collective-permute-done.da_ref
  19.5 0.1 slice_select_fusion.2
  19.6 0.1 copy.15
  19.7 7.2 %all-to-all-done.rf_ref = f32[4,6,3,16,128]{4,3,2,1,0:T(8,128)S(1)} async-done(((f32[4,6,3,16,128]{4,3,2,1,0:T(8,128)}), f32[4,6,3,16,128]{4,3,2,1,0:T(8,128)S(1)}, u32[]{:S(2)}, u32[]{:S(2)}) %all-to-all-start) | async-done | bytes 589856 | tf_op jit(solution)/shard_map/all_to_all | solution.py:521
  26.9 0.2 slice_select_fusion
  27.1 0.0 copy-start
  27.1 0.2 copy.17
  27.3 1.3 %collective-permute-start.3 = (f32[2688,8]{0,1:T(8,128)S(1)}, f32[2688,8]{0,1:T(8,128)S(1)}, u32[]{:S(2)}, u32[]{:S(2)}) collective-permute-start(f32[2688,8]{0,1:T(8,128)S(1)} %pad_maximum_fusion), channel_id=1, source_target_pairs={{0,16},{16,0},{1,17},{17,1},{2,18},{18,2},{3,19},{19,3},{4,20},{20... | collective-permute-start | bytes 258056 | tf_op jit(solution)/shard_map/ppermute | solution.py:529
  28.6 2.1 %collective-permute-done.3 = f32[2688,8]{0,1:T(8,128)S(1)} collective-permute-done((f32[2688,8]{0,1:T(8,128)S(1)}, f32[2688,8]{0,1:T(8,128)S(1)}, u32[]{:S(2)}, u32[]{:S(2)}) %collective-permute-start.3) | collective-permute-done | bytes 86048 | tf_op jit(solution)/shard_map/ppermute | solution.py:529
  30.7 0.4 copy.18.strip_ref
  31.2 8.8 %first.1 = (f32[8,128,256]{2,1,0:T(8,128)S(1)}, f32[32,128]{1,0:T(8,128)S(1)}, f32[32,128]{1,0:T(8,128)S(1)}, f32[1584,128]{1,0:T(8,128)S(1)}, f32[1584,128]{1,0...) custom-call(f32[4,128,128]{2,1,0:T(8,128)S(1)} %copy-done, ...), custom_call_target="tpu_custom_call" | custom-call | tf_op jit(solution)/shard_map/first/pallas_call | solution.py:540
  40.0 1.0 %copy-done.1 = f32[8,128,256]{2,1,0:T(8,128)} copy-done((f32[8,128,256]{2,1,0:T(8,128)}, f32[8,128,256]{2,1,0:T(8,128)S(1)}, u32[]{:S(2)}) %copy-start.1) | copy-done | bytes 1048600
  41.0 1.8 %collective-permute-start.4 = (f32[528,128]{1,0:T(8,128)S(1)}, f32[528,128]{1,0:T(8,128)S(1)}, u32[]{:S(2)}, u32[]{:S(2)}) collective-permute-start(f32[528,128]{1,0:T(8,128)S(1)} %get-tuple-element.31), channel_id=1, source_target_pairs={{0,1},{1,0},{2,3},{3,2},{4,5},{5,4},{6,7},{7,6},{8,9},{9,8},{10,11... | collective-permute-start | bytes 811016 | tf_op jit(solution)/shard_map/ppermute | solution.py:508
  42.8 4.1 %collective-permute-start.5 = (f32[528,128]{1,0:T(8,128)S(1)}, f32[528,128]{1,0:T(8,128)S(1)}, u32[]{:S(2)}, u32[]{:S(2)}) collective-permute-start(f32[528,128]{1,0:T(8,128)S(1)} %get-tuple-element.32), channel_id=1, source_target_pairs={{1,2},{2,1},{3,4},{4,3},{5,6},{6,5},{7,8},{8,7},{9,10},{10,9},{11,... | collective-permute-start | bytes 811016 | tf_op jit(solution)/shard_map/ppermute | solution.py:508
  46.9 0.0 collective-permute-done.4.from_a
  46.9 4.6 %collective-permute-done.5.from_b = f32[528,128]{1,0:T(8,128)S(1)} collective-permute-done((f32[528,128]{1,0:T(8,128)S(1)}, f32[528,128]{1,0:T(8,128)S(1)}, u32[]{:S(2)}, u32[]{:S(2)}) %collective-permute-start.5) | collective-permute-done | bytes 270368 | tf_op jit(solution)/shard_map/ppermute | solution.py:508
  51.5 4.6 %second.1 = (f32[1584,128]{1,0:T(8,128)S(1)}, f32[1584,128]{1,0:T(8,128)S(1)}, f32[528,128]{1,0:T(8,128)S(1)}, f32[528,128]{1,0:T(8,128)S(1)}, f32[32,128]{1,0:T(8,128)S(1)}, /*index=5*/f32[32,128]{1,0:T(8,128)S(1)}) custom-call(f32[1584,128]{1,0:T(8,128)S(1)} %get-tuple-element.28.prev_ref.v0_ref, f32[1584,128]{1,0:T(8,128)S(1)} %get-tuple-element.29.free_ref, ...), custom_call_target="tpu_custom_call" | custom-call | tf_op jit(solution)/shard_map/second/pallas_call | solution.py:548
  56.1 2.0 %collective-permute-start.6 = (f32[528,128]{1,0:T(8,128)S(1)}, f32[528,128]{1,0:T(8,128)S(1)}, u32[]{:S(2)}, u32[]{:S(2)}) collective-permute-start(f32[528,128]{1,0:T(8,128)S(1)} %get-tuple-element.36), channel_id=1, source_target_pairs={{0,1},{1,0},{2,3},{3,2},{4,5},{5,4},{6,7},{7,6},{8,9},{9,8},{10,11... | collective-permute-start | bytes 811016 | tf_op jit(solution)/shard_map/ppermute | solution.py:508
  58.1 4.6 %collective-permute-start.7 = (f32[528,128]{1,0:T(8,128)S(1)}, f32[528,128]{1,0:T(8,128)S(1)}, u32[]{:S(2)}, u32[]{:S(2)}) collective-permute-start(f32[528,128]{1,0:T(8,128)S(1)} %get-tuple-element.37), channel_id=1, source_target_pairs={{1,2},{2,1},{3,4},{4,3},{5,6},{6,5},{7,8},{8,7},{9,10},{10,9},{11,... | collective-permute-start | bytes 811016 | tf_op jit(solution)/shard_map/ppermute | solution.py:508
  62.8 0.0 collective-permute-done.6.from_a
  62.8 4.2 %collective-permute-done.7.from_b = f32[528,128]{1,0:T(8,128)S(1)} collective-permute-done((f32[528,128]{1,0:T(8,128)S(1)}, f32[528,128]{1,0:T(8,128)S(1)}, u32[]{:S(2)}, u32[]{:S(2)}) %collective-permute-start.7) | collective-permute-done | bytes 270368 | tf_op jit(solution)/shard_map/ppermute | solution.py:508
  67.0 4.2 %third.1 = (f32[1584,128]{1,0:T(8,128)S(1)}, f32[32,128]{1,0:T(8,128)S(1)}, f32[32,128]{1,0:T(8,128)S(1)}, f32[32,128]{1,0:T(8,128)S(1)}, f32[32,128]{1,0:T(8,128)S(1)}) custom-call(f32[1584,128]{1,0:T(8,128)S(1)} %get-tuple-element.28.prev_ref.v0_ref, f32[1584,128]{1,0:T(8,128)S(1)} %get-tuple-element.34.v1_ref, ...), custom_call_target="tpu_custom_call" | custom-call | tf_op jit(solution)/shard_map/third/pallas_call | solution.py:556
  71.2 12.3 %all_to_all.21 = f32[32,1,128]{2,1,0:T(1,128)S(1)} all-to-all(f32[32,1,128]{2,1,0:T(1,128)S(1)} %bitcast.27), channel_id=1, replica_groups=mesh['role'=2,'gx'=4,'gy'=4] {'role','gx','gy'}, dimensions={0} | all-to-all | bytes 32768 | tf_op jit(solution)/shard_map/all_to_all | solution.py:563
  83.5 1.4 %combine.1 = (f32[32,128]{1,0:T(8,128)S(1)}, f32[4,3,2,16,128]{4,3,2,1,0:T(8,128)}) custom-call(f32[32,128]{1,0:T(8,128)S(1)} %bitcast.26, f32[1584,128]{1,0:T(8,128)S(1)} %get-tuple-element.28.prev_ref.v0_ref, f32[1584,128]{1,0:T(8,128)S(1)} %get-tuple-element.34.v1_ref, f32[1584,128]{1,0:T(8,128)S(1)} %get-tuple-element.42.v2_ref, ...), custom_call_target="tpu_custom_call" | custom-call | tf_op jit(solution)/shard_map/combine/pallas_call | solution.py:564
  84.9 5.1 %all-to-all-start.2 = ((f32[4,3,2,16,128]{4,3,2,1,0:T(8,128)}), f32[4,3,2,16,128]{4,3,2,1,0:T(8,128)S(1)}, u32[]{:S(2)}, u32[]{:S(2)}) async-start(f32[4,3,2,16,128]{4,3,2,1,0:T(8,128)} %get-tuple-element.49), calls=%async_computation.2 | async-start | bytes 393216 | tf_op jit(solution)/shard_map/all_to_all | solution.py:579
  90.0 1.9 %collective-permute-start.9 = (f32[32,128]{1,0:T(8,128)S(1)}, f32[32,128]{1,0:T(8,128)S(1)}, u32[]{:S(2)}, u32[]{:S(2)}) collective-permute-start(f32[32,128]{1,0:T(8,128)S(1)} %get-tuple-element.47.grad_ref), channel_id=1, source_target_pairs={{1,2},{2,1},{3,4},{4,3},{5,6},{6,5},{7,8},{8,7},{9,10},{10,9},{11,... | collective-permute-start | bytes 49160 | tf_op jit(solution)/shard_map/ppermute | solution.py:508
  91.9 0.6 collective-permute-start.8
  92.4 3.5 %collective-permute-done.9.gb_ref = f32[32,128]{1,0:T(8,128)S(1)} collective-permute-done((f32[32,128]{1,0:T(8,128)S(1)}, f32[32,128]{1,0:T(8,128)S(1)}, u32[]{:S(2)}, u32[]{:S(2)}) %collective-permute-start.9) | collective-permute-done | bytes 16416 | tf_op jit(solution)/shard_map/ppermute | solution.py:508
  95.9 2.5 %last.1 = f32[4,128,128]{2,1,0:T(8,128)} custom-call(f32[32,128]{1,0:T(8,128)S(1)} %get-tuple-element.47.grad_ref, f32[32,128]{1,0:T(8,128)S(1)} %collective-permute-done.8.ga_ref, f32[32,128]{1,0:T(8,128)S(1)} %collective-permute-done.9.gb_ref, f32[8,128,256]{2,1,0:T(8,128)S(1)} %copy-done.2), custom_call_target="tpu_custom_call" | custom-call | tf_op jit(solution)/shard_map/last/pallas_call | solution.py:572
  98.4 0.0 all-to-all-done.2
  98.4 0.7 copy.20
  (11 shorter events, 0.0 us)
Async XLA Ops:
  0.6 10.6 %copy-start.3 = (s32[3,8,16,128]{3,2,1,0:T(8,128)S(1)}, s32[3,8,16,128]{3,2,1,0:T(8,128)}, u32[]{:S(2)}) copy-start(s32[3,8,16,128]{3,2,1,0:T(8,128)} %mask_ref.1) | copy-start | bytes 589828
  0.6 10.6 %copy-start.4 = (f32[3,8,16,128]{3,2,1,0:T(8,128)S(1)}, f32[3,8,16,128]{3,2,1,0:T(8,128)}, u32[]{:S(2)}) copy-start(f32[3,8,16,128]{3,2,1,0:T(8,128)} %force_ref.1) | copy-start | bytes 589828
  0.7 18.6 %collective-permute-start.1 = (f32[4,128,128]{2,1,0:T(8,128)}, f32[4,128,128]{2,1,0:T(8,128)S(1)}, u32[]{:S(2)}, u32[]{:S(2)}) collective-permute-start(f32[4,128,128]{2,1,0:T(8,128)} %design_ref.1), channel_id=1, source_target_pairs={{1,2},{2,1},{3,4},{4,3},{5,6},{6,5},{7,8},{8,7},{9,10},{10,9},{11,... | collective-permute-start | bytes 786440 | tf_op jit(solution)/shard_map/ppermute | solution.py:508
  4.5 14.9 %collective-permute-start = (f32[4,128,128]{2,1,0:T(8,128)}, f32[4,128,128]{2,1,0:T(8,128)S(1)}, u32[]{:S(2)}, u32[]{:S(2)}) collective-permute-start(f32[4,128,128]{2,1,0:T(8,128)} %design_ref.1), channel_id=1, source_target_pairs={{0,1},{1,0},{2,3},{3,2},{4,5},{5,4},{6,7},{7,6},{8,9},{9,8},{10,11... | collective-permute-start | bytes 786440 | tf_op jit(solution)/shard_map/ppermute | solution.py:508
  6.1 5.1 %collective-permute-start.2 = (f32[6,16,128]{2,1,0:T(8,128)S(1)}, f32[6,16,128]{2,1,0:T(8,128)S(1)}, u32[]{:S(2)}, u32[]{:S(2)}) collective-permute-start(f32[6,16,128]{2,1,0:T(8,128)S(1)} %pad_maximum_fusion.1), channel_id=1, source_target_pairs={{4,0},{8,4},{12,8},{5,1},{9,5},{13,9},{6,2},{10,6},{14,10},{7,3},{... | collective-permute-start | bytes 147464 | tf_op jit(solution)/shard_map/ppermute | solution.py:511
  11.3 0.8 copy-start.5
  12.1 0.8 copy-start.6
  14.4 12.5 %all-to-all-start = ((f32[4,6,3,16,128]{4,3,2,1,0:T(8,128)}), f32[4,6,3,16,128]{4,3,2,1,0:T(8,128)S(1)}, u32[]{:S(2)}, u32[]{:S(2)}) async-start(f32[4,6,3,16,128]{4,3,2,1,0:T(8,128)} %get-tuple-element.26), calls=%async_computation | async-start | bytes 1179648 | tf_op jit(solution)/shard_map/all_to_all | solution.py:521
  27.1 4.0 %copy-start = (f32[4,128,128]{2,1,0:T(8,128)S(1)}, f32[4,128,128]{2,1,0:T(8,128)}, u32[]{:S(2)}) copy-start(f32[4,128,128]{2,1,0:T(8,128)} %design_ref.1) | copy-start | bytes 786436
  27.3 3.4 %collective-permute-start.3 = (f32[2688,8]{0,1:T(8,128)S(1)}, f32[2688,8]{0,1:T(8,128)S(1)}, u32[]{:S(2)}, u32[]{:S(2)}) collective-permute-start(f32[2688,8]{0,1:T(8,128)S(1)} %pad_maximum_fusion), channel_id=1, source_target_pairs={{0,16},{16,0},{1,17},{17,1},{2,18},{18,2},{3,19},{19,3},{4,20},{20... | collective-permute-start | bytes 258056 | tf_op jit(solution)/shard_map/ppermute | solution.py:529
  40.0 1.0 %copy-start.1 = (f32[8,128,256]{2,1,0:T(8,128)}, f32[8,128,256]{2,1,0:T(8,128)S(1)}, u32[]{:S(2)}) copy-start(f32[8,128,256]{2,1,0:T(8,128)S(1)} %get-tuple-element.48.sw_ref) | copy-start | bytes 3145732
  41.0 5.9 %collective-permute-start.4 = (f32[528,128]{1,0:T(8,128)S(1)}, f32[528,128]{1,0:T(8,128)S(1)}, u32[]{:S(2)}, u32[]{:S(2)}) collective-permute-start(f32[528,128]{1,0:T(8,128)S(1)} %get-tuple-element.31), channel_id=1, source_target_pairs={{0,1},{1,0},{2,3},{3,2},{4,5},{5,4},{6,7},{7,6},{8,9},{9,8},{10,11... | collective-permute-start | bytes 811016 | tf_op jit(solution)/shard_map/ppermute | solution.py:508
  42.8 8.8 %collective-permute-start.5 = (f32[528,128]{1,0:T(8,128)S(1)}, f32[528,128]{1,0:T(8,128)S(1)}, u32[]{:S(2)}, u32[]{:S(2)}) collective-permute-start(f32[528,128]{1,0:T(8,128)S(1)} %get-tuple-element.32), channel_id=1, source_target_pairs={{1,2},{2,1},{3,4},{4,3},{5,6},{6,5},{7,8},{8,7},{9,10},{10,9},{11,... | collective-permute-start | bytes 811016 | tf_op jit(solution)/shard_map/ppermute | solution.py:508
  56.1 6.6 %collective-permute-start.6 = (f32[528,128]{1,0:T(8,128)S(1)}, f32[528,128]{1,0:T(8,128)S(1)}, u32[]{:S(2)}, u32[]{:S(2)}) collective-permute-start(f32[528,128]{1,0:T(8,128)S(1)} %get-tuple-element.36), channel_id=1, source_target_pairs={{0,1},{1,0},{2,3},{3,2},{4,5},{5,4},{6,7},{7,6},{8,9},{9,8},{10,11... | collective-permute-start | bytes 811016 | tf_op jit(solution)/shard_map/ppermute | solution.py:508
  58.1 8.9 %collective-permute-start.7 = (f32[528,128]{1,0:T(8,128)S(1)}, f32[528,128]{1,0:T(8,128)S(1)}, u32[]{:S(2)}, u32[]{:S(2)}) collective-permute-start(f32[528,128]{1,0:T(8,128)S(1)} %get-tuple-element.37), channel_id=1, source_target_pairs={{1,2},{2,1},{3,4},{4,3},{5,6},{6,5},{7,8},{8,7},{9,10},{10,9},{11,... | collective-permute-start | bytes 811016 | tf_op jit(solution)/shard_map/ppermute | solution.py:508
  83.5 12.4 %copy-start.2 = (f32[8,128,256]{2,1,0:T(8,128)S(1)}, f32[8,128,256]{2,1,0:T(8,128)}, u32[]{:S(2)}) copy-start(f32[8,128,256]{2,1,0:T(8,128)} %copy-done.1) | copy-start | bytes 3145732
  84.9 13.5 %all-to-all-start.2 = ((f32[4,3,2,16,128]{4,3,2,1,0:T(8,128)}), f32[4,3,2,16,128]{4,3,2,1,0:T(8,128)S(1)}, u32[]{:S(2)}, u32[]{:S(2)}) async-start(f32[4,3,2,16,128]{4,3,2,1,0:T(8,128)} %get-tuple-element.49), calls=%async_computation.2 | async-start | bytes 393216 | tf_op jit(solution)/shard_map/all_to_all | solution.py:579
  90.0 5.9 %collective-permute-start.9 = (f32[32,128]{1,0:T(8,128)S(1)}, f32[32,128]{1,0:T(8,128)S(1)}, u32[]{:S(2)}, u32[]{:S(2)}) collective-permute-start(f32[32,128]{1,0:T(8,128)S(1)} %get-tuple-element.47.grad_ref), channel_id=1, source_target_pairs={{1,2},{2,1},{3,4},{4,3},{5,6},{6,5},{7,8},{8,7},{9,10},{10,9},{11,... | collective-permute-start | bytes 49160 | tf_op jit(solution)/shard_map/ppermute | solution.py:508
  91.9 4.0 %collective-permute-start.8 = (f32[32,128]{1,0:T(8,128)S(1)}, f32[32,128]{1,0:T(8,128)S(1)}, u32[]{:S(2)}, u32[]{:S(2)}) collective-permute-start(f32[32,128]{1,0:T(8,128)S(1)} %get-tuple-element.47.grad_ref), channel_id=1, source_target_pairs={{0,1},{1,0},{2,3},{3,2},{4,5},{5,4},{6,7},{7,6},{8,9},{9,8},{10,11... | collective-permute-start | bytes 49160 | tf_op jit(solution)/shard_map/ppermute | solution.py:508

commit v3 on v2

--- a/solution.py
+++ b/solution.py
@@ -15,7 +15,7 @@
 STRIP = 8
 ROWS = 120
 LINE = ("gx", "gy")
-KEEP = pltpu.CompilerParams(vmem_limit_bytes=20 << 20)
+KEEP = pltpu.CompilerParams(vmem_limit_bytes=12 << 20)
 F32 = jnp.float32
 BF16 = jnp.bfloat16
 
@@ -100,8 +100,31 @@
     return x[:rows]
 
 
-def prep_kernel(force_ref, mask_ref, next_ref, stiff_ref, place_ref, pack_ref, table_ref):
+def strip_rows_kernel(force_ref, mask_ref, plane_ref, strip_ref, corner_ref):
+    _, bx, by, fz = force_ref.shape
+    role, _ = where_am_i()
+    first = jnp.where(role == 0, fz - STRIP, 0)
+    take = jnp.where(iota((fz, LANES), 0) == first + (iota((fz, LANES), 1) & (STRIP - 1)), 1.0, 0.0).astype(BF16)
+    own_y = (iota((bx, by, LANES), 2) // STRIP) == iota((bx, by, LANES), 1)
+    corner_ref[...] = jnp.zeros(corner_ref.shape, F32)
+    for q in range(3):
+        free = 1.0 - mask_ref[q].astype(F32)
+        rhs = free * force_ref[q]
+        plane_ref[q * by : (q + 1) * by] = rhs[0]
+        plane_ref[(q + 3) * by : (q + 4) * by] = free[0]
+        edge = pick_right(rhs.reshape(bx * by, fz), take), dot(free.reshape(bx * by, fz).astype(BF16), take)
+        for row, x in ((q, edge[0]), (q + 3, edge[1])):
+            x = jnp.sum(jnp.where(own_y, x.reshape(bx, by, LANES), 0.0), axis=1)
+            strip_ref[row * bx : (row + 1) * bx] = x
+            corner_ref[row : row + 1] = x[0:1]
+
+
+def pack_kernel(force_ref, mask_ref, plane_ref, strip_ref, corner_ref, stiff_ref, place_ref, pack_ref, table_ref):
+    _, bx, by, _ = force_ref.shape
     parts = pack_ref.shape[0]
+    tail = 18 * by
+    for j in range(parts):
+        pack_ref[j, tail + 18 :] = jnp.zeros((pack_ref.shape[1] - tail - 18, LANES), F32)
     for q in range(3):
         free = 1.0 - mask_ref[q].astype(F32)
         rhs = free * force_ref[q]
@@ -109,7 +132,11 @@
             for j in range(parts):
                 for a in range(3):
                     x = 2 * j + a
-                    pack_ref[j, row, a] = val[x] if x < 2 * parts else next_ref[row]
+                    at = row * 3 + a
+                    inner = x < bx
+                    pack_ref[j, at * by : (at + 1) * by] = val[x] if inner else plane_ref[row * by : (row + 1) * by]
+                    edge = strip_ref[row * bx + x : row * bx + x + 1] if inner else corner_ref[row : row + 1]
+                    pack_ref[j, tail + at : tail + at + 1] = edge
     place = place_ref[...]
     half_way = jnp.dot(place, stiff_ref[...], precision=lax.Precision.HIGHEST, preferred_element_type=F32)
     spread = lax.dot_general(
@@ -250,14 +277,8 @@
     nodes_ref[2 * count :] = free_ref[2 * count :] * (local_ref[2 * count :] + jnp.where(even, a, b))
 
 
-def first_kernel(
-    design_ref, da_ref, db_ref, strip_ref, rf_ref, table_ref,
-    sw_ref, factor_ref, density_ref, nodes_ref, free_ref, local_ref, to_a, to_b, e00_ref,
-    fine_ref, sum_ref, main_ref, shift_ref, shift32_ref,
-):
+def filter_kernel(design_ref, da_ref, db_ref, strip_ref, sw_ref, factor_ref, density_ref, fine_ref, sum_ref):
     planes, fy, fz = design_ref.shape
-    tiles = main_ref.shape[1]
-    count = plane_rows(tiles)
     role, slab = where_am_i()
     slabs = lax.axis_size("gx") * lax.axis_size("gy")
     roles = lax.axis_size("role")
@@ -310,37 +331,44 @@
     density_ref[...] = density
     factor_ref[...] = jnp.where(inside, FLOOR_STIFF + (1.0 - FLOOR_STIFF) * density * density * density, 0.0)
 
+
+def first_kernel(
+    rf_ref, factor_ref, table_ref,
+    nodes_ref, free_ref, local_ref, to_a, to_b, e00_ref,
+    main_ref, shift_ref, shift32_ref,
+):
+    tiles = main_ref.shape[1]
+    count = plane_rows(tiles)
+    role, slab = where_am_i()
+    half = LANES // 2
+    parts = rf_ref.shape[0]
+    deep = (2 * factor_ref.shape[0]) // parts
+    tail = 18 * deep
+
     nodes_ref[...] = jnp.zeros(nodes_ref.shape, F32)
     free_ref[...] = jnp.zeros(free_ref.shape, F32)
-    zi = iota((LANES, width), 0)
-    ci = iota((LANES, width), 1)
-    lane_of = ci & (LANES - 1)
-    odd = ci // LANES
-    own_table = jnp.where(zi == 2 * lane_of + odd, 1.0, 0.0).astype(BF16)
-    si = iota((STRIP, width), 0)
-    ci = iota((STRIP, width), 1)
+    zi = iota((2 * LANES, 2 * LANES), 0)
+    ci = iota((2 * LANES, 2 * LANES), 1)
     lane_of = ci & (LANES - 1)
     odd = ci // LANES
     first_lane = jnp.where(role == 0, half, LANES - STRIP // 2)
-    strip_table = jnp.where(si == 2 * (lane_of - first_lane) + odd, 1.0, 0.0).astype(BF16)
-    parts = rf_ref.shape[0]
-    deep = rf_ref.shape[3]
-    base = 3 * planes * fy
+    own = zi == 2 * lane_of + odd
+    edge = (zi & (STRIP - 1)) == 2 * (lane_of - first_lane) + odd
+    table = jnp.where(zi < LANES, jnp.where(own, 1.0, 0.0), jnp.where(edge, 1.0, 0.0)).astype(BF16)
+    own_y = (iota((deep, LANES), 1) // STRIP) == iota((deep, LANES), 0)
     for row in range(6):
         for a in range(3):
-            x = jnp.concatenate([rf_ref[j, row, a] for j in range(parts)], axis=0)
+            at = row * 3 + a
+            x = jnp.concatenate([rf_ref[j, at * deep : (at + 1) * deep] for j in range(parts)], axis=0)
             st = jnp.concatenate(
-                [
-                    strip_ref[base + ((j * 6 + row) * 3 + a) * deep : base + ((j * 6 + row) * 3 + a + 1) * deep]
-                    for j in range(parts)
-                ],
-                axis=0,
+                [jnp.where(own_y, rf_ref[j, tail + at : tail + at + 1], 0.0) for j in range(parts)], axis=0
             )
+            x = jnp.concatenate([x, st], axis=1)
             if row < 3:
-                y = pick_right(x, own_table) + pick_right(st, strip_table)
+                y = pick_right(x, table)
                 dest = nodes_ref
             else:
-                y = dot(x.astype(BF16), own_table) + dot(st.astype(BF16), strip_table)
+                y = dot(x.astype(BF16), table)
                 dest = free_ref
             q = row % 3
             dest[pl.ds(a * count + q, parts * deep, stride=8), :] = y[:, :LANES]
@@ -507,17 +535,25 @@
     def beside(to_a, to_b):
         return lax.ppermute(to_a, LINE, pairs_a), lax.ppermute(to_b, LINE, pairs_b)
 
-    free0 = (1 - clamped_dof_mask[:, 0]).astype(F32)
-    next_plane = lax.ppermute(
-        jnp.concatenate([free0 * force[:, 0], free0], axis=0), "gx", [(i + 1, i) for i in range(gx - 1)]
+    plane0, strips, corner = pl.pallas_call(
+        strip_rows_kernel,
+        out_shape=(shape(6 * by, fz), shape(6 * bx, LANES), shape(8, LANES)),
+        name="rows",
+        compiler_params=KEEP,
+    )(force, clamped_dof_mask)
+    plane0, strips, corner, design = lax.optimization_barrier((plane0, strips, corner, design))
+    next_plane = lax.ppermute(plane0, "gx", [(i + 1, i) for i in range(gx - 1)])
+    strips = lax.ppermute(strips, "role", [(0, 1), (1, 0)])
+    corner = lax.ppermute(
+        corner, ("role", "gx"), [((1 - r) * gx + i + 1, r * gx + i) for r in range(2) for i in range(gx - 1)]
     )
     design_a, design_b = beside(design, design)
     pack, table = pl.pallas_call(
-        prep_kernel,
-        out_shape=(shape(gy, 6, 3, by, fz), shape(2 * ROWS, 2 * ROWS, dtype=BF16)),
-        name="prep",
-        compiler_params=KEEP,
-    )(force, clamped_dof_mask, next_plane, stiffness, jnp.asarray(place_table()))
+        pack_kernel,
+        out_shape=(shape(gy, 18 * by + 24, fz), shape(2 * ROWS, 2 * ROWS, dtype=BF16)),
+        name="pack",
+        compiler_params=KEEP,
+    )(force, clamped_dof_mask, next_plane, strips, corner, stiffness, jnp.asarray(place_table()))
     rf = lax.all_to_all(pack, "gy", 0, 0)
 
     role = lax.axis_index("role")
@@ -525,8 +561,8 @@
     def strip(x):
         return jnp.where(role == 0, x[..., fz - STRIP :], x[..., :STRIP]).reshape(-1, STRIP)
 
-    strips = jnp.concatenate([strip(design), strip(design_a), strip(design_b), strip(rf)], axis=0)
-    strips = lax.ppermute(strips, "role", [(0, 1), (1, 0)])
+    fine_strips = jnp.concatenate([strip(design), strip(design_a), strip(design_b)], axis=0)
+    fine_strips = lax.ppermute(fine_strips, "role", [(0, 1), (1, 0)])
 
     node_set = shape(3 * count, LANES)
     plane = shape(count, LANES)
@@ -537,13 +573,21 @@
         pltpu.VMEM((2, count, LANES), F32),
     ]
     shift32 = pltpu.VMEM((2, count, LANES), F32)
-    sw, factor, density, v0, free, local, to_a, to_b, e00 = pl.pallas_call(
+    sw, factor, density = pl.pallas_call(
+        filter_kernel,
+        out_shape=(shape(planes + 4, fy, 2 * fz), element, element),
+        scratch_shapes=[pltpu.VMEM((3 * planes, fy, 2 * fz), F32), pltpu.VMEM((fy, 2 * fz), F32)],
+        name="filter",
+        compiler_params=KEEP,
+        cost_estimate=pl.CostEstimate(flops=30_000_000, transcendentals=0, bytes_accessed=4_000_000),
+    )(design, design_a, design_b, fine_strips)
+    v0, free, local, to_a, to_b, e00 = pl.pallas_call(
         first_kernel,
-        out_shape=(shape(planes + 4, fy, 2 * fz), element, element, node_set, node_set, node_set, plane, plane, element),
-        scratch_shapes=[pltpu.VMEM((3 * planes, fy, 2 * fz), F32), pltpu.VMEM((fy, 2 * fz), F32)] + tile_scratch,
+        out_shape=(node_set, node_set, node_set, plane, plane, element),
+        scratch_shapes=tile_scratch,
         name="first",
         compiler_params=KEEP,
-    )(design, design_a, design_b, strips, rf, table)
+    )(rf, factor, table)
     from_a, from_b = beside(to_a, to_b)
     v1, local, to_a, to_b, e01, e11 = pl.pallas_call(
         second_kernel,

time: 99.7 us -> 93.2 us (0.935)
  waiting for transfers between devices: 24.2 us -> 18.3 us
  other arithmetic: 3.17 us -> 0.41 us
  starting transfers between devices: 31.5 us -> 33.9 us
  local copies, waits for them, and re-layouts: 4.21 us -> 3.15 us
    all_to_all x1, waiting for transfers between devices: 7.19 us -> 0.3 us  [on_device(): rf = lax.all_to_all(pack, 'gy', 0, 0)]
    ppermute x1 -> x3, waiting for transfers between devices: 2.56 us -> 5.81 us  [the longest x1 2.74 us: on_device(): next_plane = lax.ppermute(plane0, 'gx', [(i + 1, i) for i in range(gx - 1)])]
    ppermute x1 -> x3, starting transfers between devices: 1.29 us -> 3.86 us  [the longest x1 1.29 us: on_device(): lax.ppermute(corner, ('role', 'gx'), [((1 - r) * gx + i + 1, r * gx + i)...]
    ppermute x1, waiting for transfers between devices: 2.1 us -> 0.01 us  [on_device(): strips = lax.ppermute(strips, 'role', [(0, 1), (1, 0)])]
    select_n x4 -> x3, other arithmetic: 1.65 us -> 0.4 us  [strip(): jnp.where(role == 0, x[..., fz - STRIP:], x[..., :STRIP]).reshape(-1, STRIP)]
    pallas_call x2 -> x4, Pallas kernels: 10.3 us -> 11 us  [the longest x1 5.34 us: on_device(): pl.pallas_call(first_kernel, out_shape=(node_set, node_set, node_set, pla...]
  transfers between devices with their start and end apart: 12 -> 14, of which waited for: 6 -> 7; matrix products, arithmetic and copies ran while one was open for 3% -> 1% of each run, Pallas kernels for 4% -> 8%
where the time goes in v3:
time: 93.2 us; the launch traced here: 92.7 us
  starting transfers between devices  33.9 us (36%)
  Pallas kernels  23.7 us (25%)
  waiting for transfers between devices  18.3 us (20%)
  blocking collectives  12.4 us (13%)
  local copies, waits for them, and re-layouts  3.15 us (3%)
    ppermute x4, starting transfers between devices, beside(): lax.ppermute(to_b, LINE, pairs_b)  14.6 us
    all_to_all x1, blocking collectives, on_device(): moments = lax.all_to_all(moments, ('role', 'gx', 'gy'), 0, 0, tiled=True)  12.4 us
    ppermute x4, waiting for transfers between devices, beside(): lax.ppermute(to_b, LINE, pairs_b)  12.2 us
    all_to_all x1, starting transfers between devices, on_device(): rf = lax.all_to_all(pack, 'gy', 0, 0)  5.45 us
    pallas_call x1, Pallas kernels, on_device(): pl.pallas_call(first_kernel, out_shape=(node_set, node_set, node_set, pla...  5.34 us
    all_to_all x1, starting transfers between devices, on_device(): u = lax.all_to_all(u, 'gy', 0, 0)  5.07 us
    pallas_call x1, Pallas kernels, on_device(): pl.pallas_call(second_kernel, out_shape=(node_set, node_set, plane, plane...  4.61 us
    pallas_call x1, Pallas kernels, on_device(): pl.pallas_call(third_kernel, out_shape=(node_set, element, element, eleme...  4.23 us
  transfers between devices with their start and end apart: 14, of which 7 were waited for; matrix products, arithmetic and copies ran while one was open for 1% of the time, Pallas kernels for 8%

profile of v3, /device:TPU:3, one launch (start us, length us, event | category | flops | bytes accessed | tf_op | source)
XLA Modules:
  0.0 92.7 jit_solution(14888296578499616742)
XLA Ops:
  0.6 0.0 copy-start.1
  0.7 1.0 %copy-done.1 = f32[3,8,16,128]{3,2,1,0:T(8,128)S(1)} copy-done((f32[3,8,16,128]{3,2,1,0:T(8,128)S(1)}, f32[3,8,16,128]{3,2,1,0:T(8,128)}, u32[]{:S(2)}) %copy-start.1) | copy-done | bytes 196632
  1.6 0.9 copy-done.3
  2.5 0.3 rows.1
  2.8 3.7 %collective-permute-start.4 = (f32[4,128,128]{2,1,0:T(8,128)S(1)}, f32[4,128,128]{2,1,0:T(8,128)S(1)}, u32[]{:S(2)}, u32[]{:S(2)}) collective-permute-start(f32[4,128,128]{2,1,0:T(8,128)S(1)} %copy-done), channel_id=1, source_target_pairs={{1,2},{2,1},{3,4},{4,3},{5,6},{6,5},{7,8},{8,7},{9,10},{10,9},{11,... | collective-permute-start | bytes 786440 | tf_op jit(solution)/shard_map/ppermute | solution.py:536
  6.6 0.1 collective-permute-start.3
  6.7 1.3 %collective-permute-start.2 = (f32[8,128]{1,0:T(8,128)S(1)}, f32[8,128]{1,0:T(8,128)S(1)}, u32[]{:S(2)}, u32[]{:S(2)}) collective-permute-start(f32[8,128]{1,0:T(8,128)S(1)} %get-tuple-element.38), channel_id=1, source_target_pairs={{20,0},{24,4},{28,8},{4,16},{8,20},{12,24},{21,1},{25,5},{29,9},{5... | collective-permute-start | bytes 12296 | tf_op jit(solution)/shard_map/ppermute | solution.py:547
  8.0 1.3 %collective-permute-start.1 = (f32[48,128]{1,0:T(8,128)S(1)}, f32[48,128]{1,0:T(8,128)S(1)}, u32[]{:S(2)}, u32[]{:S(2)}) collective-permute-start(f32[48,128]{1,0:T(8,128)S(1)} %get-tuple-element.37), channel_id=1, source_target_pairs={{0,16},{16,0},{1,17},{17,1},{2,18},{18,2},{3,19},{19,3},{4,20},{20... | collective-permute-start | bytes 73736 | tf_op jit(solution)/shard_map/ppermute | solution.py:546
  9.3 1.3 %collective-permute-start = (f32[96,128]{1,0:T(8,128)S(1)}, f32[96,128]{1,0:T(8,128)S(1)}, u32[]{:S(2)}, u32[]{:S(2)}) collective-permute-start(f32[96,128]{1,0:T(8,128)S(1)} %get-tuple-element.36), channel_id=1, source_target_pairs={{4,0},{8,4},{12,8},{5,1},{9,5},{13,9},{6,2},{10,6},{14,10},{7,3},{... | collective-permute-start | bytes 147464 | tf_op jit(solution)/shard_map/ppermute | solution.py:545
  10.6 0.0 copy-start.4
  10.6 0.0 copy-start.6
  10.6 0.1 slice_select_fusion.2
  10.7 0.0 copy-start.2
  10.7 0.0 copy-start.5
  10.8 0.1 copy.8
  10.8 1.1 %collective-permute-done.2.corner_ref = f32[8,128]{1,0:T(8,128)S(1)} collective-permute-done((f32[8,128]{1,0:T(8,128)S(1)}, f32[8,128]{1,0:T(8,128)S(1)}, u32[]{:S(2)}, u32[]{:S(2)}) %collective-permute-start.2) | collective-permute-done | bytes 4128 | tf_op jit(solution)/shard_map/ppermute | solution.py:547
  11.9 0.0 collective-permute-done.1.strip_ref
  11.9 2.7 %collective-permute-done.plane_ref = f32[96,128]{1,0:T(8,128)S(1)} collective-permute-done((f32[96,128]{1,0:T(8,128)S(1)}, f32[96,128]{1,0:T(8,128)S(1)}, u32[]{:S(2)}, u32[]{:S(2)}) %collective-permute-start) | collective-permute-done | bytes 49184 | tf_op jit(solution)/shard_map/ppermute | solution.py:545
  14.7 1.5 %pack.1 = (f32[4,312,128]{2,1,0:T(8,128)}, bf16[240,240]{1,0:T(8,128)(2,1)S(1)}) custom-call(f32[3,8,16,128]{3,2,1,0:T(8,128)S(1)} %copy-done.2, s32[3,8,16,128]{3,2,1,0:T(8,128)S(1)} %copy-done.4, f32[96,128]{1,0:T(8,128)S(1)} %collective-permute-done.plane_ref, f32[48,128]{1,0:T(8,128)S(1)} %collective-permute-done.1.strip_ref, ...), custom_call_target="tpu_custom_call" | custom-call | tf_op jit(solution)/shard_map/pack/pallas_call | solution.py:551
  16.2 5.4 %all-to-all-start = ((f32[4,312,128]{2,1,0:T(8,128)}), f32[4,312,128]{2,1,0:T(8,128)S(1)}, u32[]{:S(2)}, u32[]{:S(2)}) async-start(f32[4,312,128]{2,1,0:T(8,128)} %get-tuple-element.39), calls=%async_computation | async-start | bytes 1277952 | tf_op jit(solution)/shard_map/all_to_all | solution.py:557
  21.6 0.0 collective-permute-done.4.db_ref
  21.6 0.1 slice_select_fusion
  21.8 0.1 copy.10
  21.9 0.1 slice_select_fusion.1
  22.0 0.1 copy.9
  22.1 1.3 %collective-permute-start.5 = (f32[1536,8]{0,1:T(8,128)S(1)}, f32[1536,8]{0,1:T(8,128)S(1)}, u32[]{:S(2)}, u32[]{:S(2)}) collective-permute-start(f32[1536,8]{0,1:T(8,128)S(1)} %pad_maximum_fusion), channel_id=1, source_target_pairs={{0,16},{16,0},{1,17},{17,1},{2,18},{18,2},{3,19},{19,3},{4,20},{20... | collective-permute-start | bytes 147464 | tf_op jit(solution)/shard_map/ppermute | solution.py:565
  23.4 2.0 %collective-permute-done.5 = f32[1536,8]{0,1:T(8,128)S(1)} collective-permute-done((f32[1536,8]{0,1:T(8,128)S(1)}, f32[1536,8]{0,1:T(8,128)S(1)}, u32[]{:S(2)}, u32[]{:S(2)}) %collective-permute-start.5) | collective-permute-done | bytes 49184 | tf_op jit(solution)/shard_map/ppermute | solution.py:565
  25.4 0.3 copy.11.strip_ref
  25.7 3.9 %filter.1 = (f32[8,128,256]{2,1,0:T(8,128)S(1)}, f32[32,128]{1,0:T(8,128)S(1)}, f32[32,128]{1,0:T(8,128)S(1)}) custom-call(f32[4,128,128]{2,1,0:T(8,128)S(1)} %copy-done, f32[4,128,128]{2,1,0:T(8,128)S(1)} %collective-permute-done.3.da_ref, f32[4,128,128]{2,1,0:T(8,128)S(1)} %collective-permute-done.4.db_ref, f32[1536,8]{1,0:T(8,128)S(1)} %copy.11.strip_ref), custom_call_target="tpu_custom_call" | custom-call | flops 30000000 | bytes 4000000 | tf_op jit(solution)/shard_map/filter/pallas_call | solution.py:576
  29.5 0.3 all-to-all-done.rf_ref
  29.8 5.3 %first.1 = (f32[1584,128]{1,0:T(8,128)S(1)}, f32[1584,128]{1,0:T(8,128)S(1)}, f32[1584,128]{1,0:T(8,128)S(1)}, f32[528,128]{1,0:T(8,128)S(1)}, f32[528,128]{1,0:T(8,128)S(1)}, /*index=5*/f32[32,128]{1,0:T(8,128)S(1)}) custom-call(f32[4,312,128]{2,1,0:T(8,128)S(1)} %all-to-all-done.rf_ref, f32[32,128]{1,0:T(8,128)S(1)} %get-tuple-element.41.factor_ref, ...), custom_call_target="tpu_custom_call" | custom-call | tf_op jit(solution)/shard_map/first/pallas_call | solution.py:584
  35.2 1.0 %collective-permute-start.6 = (f32[528,128]{1,0:T(8,128)S(1)}, f32[528,128]{1,0:T(8,128)S(1)}, u32[]{:S(2)}, u32[]{:S(2)}) collective-permute-start(f32[528,128]{1,0:T(8,128)S(1)} %get-tuple-element.46), channel_id=1, source_target_pairs={{0,1},{1,0},{2,3},{3,2},{4,5},{5,4},{6,7},{7,6},{8,9},{9,8},{10,11... | collective-permute-start | bytes 811016 | tf_op jit(solution)/shard_map/ppermute | solution.py:536
  36.2 4.3 %collective-permute-start.7 = (f32[528,128]{1,0:T(8,128)S(1)}, f32[528,128]{1,0:T(8,128)S(1)}, u32[]{:S(2)}, u32[]{:S(2)}) collective-permute-start(f32[528,128]{1,0:T(8,128)S(1)} %get-tuple-element.47), channel_id=1, source_target_pairs={{1,2},{2,1},{3,4},{4,3},{5,6},{6,5},{7,8},{8,7},{9,10},{10,9},{11,... | collective-permute-start | bytes 811016 | tf_op jit(solution)/shard_map/ppermute | solution.py:536
  40.5 4.5 %collective-permute-done.7.from_b = f32[528,128]{1,0:T(8,128)S(1)} collective-permute-done((f32[528,128]{1,0:T(8,128)S(1)}, f32[528,128]{1,0:T(8,128)S(1)}, u32[]{:S(2)}, u32[]{:S(2)}) %collective-permute-start.7) | collective-permute-done | bytes 270368 | tf_op jit(solution)/shard_map/ppermute | solution.py:536
  45.0 4.6 %second.1 = (f32[1584,128]{1,0:T(8,128)S(1)}, f32[1584,128]{1,0:T(8,128)S(1)}, f32[528,128]{1,0:T(8,128)S(1)}, f32[528,128]{1,0:T(8,128)S(1)}, f32[32,128]{1,0:T(8,128)S(1)}, /*index=5*/f32[32,128]{1,0:T(8,128)S(1)}) custom-call(f32[1584,128]{1,0:T(8,128)S(1)} %get-tuple-element.43.prev_ref.v0_ref, f32[1584,128]{1,0:T(8,128)S(1)} %get-tuple-element.44.free_ref, ...), custom_call_target="tpu_custom_call" | custom-call | tf_op jit(solution)/shard_map/second/pallas_call | solution.py:592
  49.6 2.0 %collective-permute-start.8 = (f32[528,128]{1,0:T(8,128)S(1)}, f32[528,128]{1,0:T(8,128)S(1)}, u32[]{:S(2)}, u32[]{:S(2)}) collective-permute-start(f32[528,128]{1,0:T(8,128)S(1)} %get-tuple-element.50), channel_id=1, source_target_pairs={{0,1},{1,0},{2,3},{3,2},{4,5},{5,4},{6,7},{7,6},{8,9},{9,8},{10,11... | collective-permute-start | bytes 811016 | tf_op jit(solution)/shard_map/ppermute | solution.py:536
  51.6 4.7 %collective-permute-start.9 = (f32[528,128]{1,0:T(8,128)S(1)}, f32[528,128]{1,0:T(8,128)S(1)}, u32[]{:S(2)}, u32[]{:S(2)}) collective-permute-start(f32[528,128]{1,0:T(8,128)S(1)} %get-tuple-element.51), channel_id=1, source_target_pairs={{1,2},{2,1},{3,4},{4,3},{5,6},{6,5},{7,8},{8,7},{9,10},{10,9},{11,... | collective-permute-start | bytes 811016 | tf_op jit(solution)/shard_map/ppermute | solution.py:536
  56.3 4.2 %collective-permute-done.9.from_b = f32[528,128]{1,0:T(8,128)S(1)} collective-permute-done((f32[528,128]{1,0:T(8,128)S(1)}, f32[528,128]{1,0:T(8,128)S(1)}, u32[]{:S(2)}, u32[]{:S(2)}) %collective-permute-start.9) | collective-permute-done | bytes 270368 | tf_op jit(solution)/shard_map/ppermute | solution.py:536
  60.5 4.2 %third.1 = (f32[1584,128]{1,0:T(8,128)S(1)}, f32[32,128]{1,0:T(8,128)S(1)}, f32[32,128]{1,0:T(8,128)S(1)}, f32[32,128]{1,0:T(8,128)S(1)}, f32[32,128]{1,0:T(8,128)S(1)}) custom-call(f32[1584,128]{1,0:T(8,128)S(1)} %get-tuple-element.43.prev_ref.v0_ref, f32[1584,128]{1,0:T(8,128)S(1)} %get-tuple-element.48.v1_ref, ...), custom_call_target="tpu_custom_call" | custom-call | tf_op jit(solution)/shard_map/third/pallas_call | solution.py:600
  64.8 12.4 %all_to_all.21 = f32[32,1,128]{2,1,0:T(1,128)S(1)} all-to-all(f32[32,1,128]{2,1,0:T(1,128)S(1)} %bitcast.10), channel_id=1, replica_groups=mesh['role'=2,'gx'=4,'gy'=4] {'role','gx','gy'}, dimensions={0} | all-to-all | bytes 32768 | tf_op jit(solution)/shard_map/all_to_all | solution.py:607
  77.2 1.4 %combine.1 = (f32[32,128]{1,0:T(8,128)S(1)}, f32[4,3,2,16,128]{4,3,2,1,0:T(8,128)}) custom-call(f32[32,128]{1,0:T(8,128)S(1)} %bitcast.9, f32[1584,128]{1,0:T(8,128)S(1)} %get-tuple-element.43.prev_ref.v0_ref, f32[1584,128]{1,0:T(8,128)S(1)} %get-tuple-element.48.v1_ref, f32[1584,128]{1,0:T(8,128)S(1)} %get-tuple-element.56.v2_ref, ...), custom_call_target="tpu_custom_call" | custom-call | tf_op jit(solution)/shard_map/combine/pallas_call | solution.py:608
  78.5 5.1 %all-to-all-start.2 = ((f32[4,3,2,16,128]{4,3,2,1,0:T(8,128)}), f32[4,3,2,16,128]{4,3,2,1,0:T(8,128)S(1)}, u32[]{:S(2)}, u32[]{:S(2)}) async-start(f32[4,3,2,16,128]{4,3,2,1,0:T(8,128)} %get-tuple-element.63), calls=%async_computation.2 | async-start | bytes 393216 | tf_op jit(solution)/shard_map/all_to_all | solution.py:623
  83.6 1.9 %collective-permute-start.11 = (f32[32,128]{1,0:T(8,128)S(1)}, f32[32,128]{1,0:T(8,128)S(1)}, u32[]{:S(2)}, u32[]{:S(2)}) collective-permute-start(f32[32,128]{1,0:T(8,128)S(1)} %get-tuple-element.61.grad_ref), channel_id=1, source_target_pairs={{1,2},{2,1},{3,4},{4,3},{5,6},{6,5},{7,8},{8,7},{9,10},{10,9},{11,... | collective-permute-start | bytes 49160 | tf_op jit(solution)/shard_map/ppermute | solution.py:536
  85.5 0.6 collective-permute-start.10
  86.1 3.5 %collective-permute-done.11.gb_ref = f32[32,128]{1,0:T(8,128)S(1)} collective-permute-done((f32[32,128]{1,0:T(8,128)S(1)}, f32[32,128]{1,0:T(8,128)S(1)}, u32[]{:S(2)}, u32[]{:S(2)}) %collective-permute-start.11) | collective-permute-done | bytes 16416 | tf_op jit(solution)/shard_map/ppermute | solution.py:536
  89.5 2.5 %last.1 = f32[4,128,128]{2,1,0:T(8,128)} custom-call(f32[32,128]{1,0:T(8,128)S(1)} %get-tuple-element.61.grad_ref, f32[32,128]{1,0:T(8,128)S(1)} %collective-permute-done.10.ga_ref, f32[32,128]{1,0:T(8,128)S(1)} %collective-permute-done.11.gb_ref, f32[8,128,256]{2,1,0:T(8,128)S(1)} %get-tuple-element.62.sw_ref), custom_call_target="tpu_custom_call" | custom-call | tf_op jit(solution)/shard_map/last/pallas_call | solution.py:616
  92.0 0.0 all-to-all-done.2
  92.0 0.7 copy.13
  (12 shorter events, 0.0 us)
Async XLA Ops:
  0.6 2.2 %copy-start = (f32[4,128,128]{2,1,0:T(8,128)S(1)}, f32[4,128,128]{2,1,0:T(8,128)}, u32[]{:S(2)}) copy-start(f32[4,128,128]{2,1,0:T(8,128)} %design_ref) | copy-start | bytes 786436
  0.6 1.0 %copy-start.1 = (f32[3,8,16,128]{3,2,1,0:T(8,128)S(1)}, f32[3,8,16,128]{3,2,1,0:T(8,128)}, u32[]{:S(2)}) copy-start(f32[3,8,16,128]{3,2,1,0:T(8,128)} %force_ref.3) | copy-start | bytes 589828
  1.6 0.9 copy-start.3
  2.8 18.8 %collective-permute-start.4 = (f32[4,128,128]{2,1,0:T(8,128)S(1)}, f32[4,128,128]{2,1,0:T(8,128)S(1)}, u32[]{:S(2)}, u32[]{:S(2)}) collective-permute-start(f32[4,128,128]{2,1,0:T(8,128)S(1)} %copy-done), channel_id=1, source_target_pairs={{1,2},{2,1},{3,4},{4,3},{5,6},{6,5},{7,8},{8,7},{9,10},{10,9},{11,... | collective-permute-start | bytes 786440 | tf_op jit(solution)/shard_map/ppermute | solution.py:536
  6.6 15.3 %collective-permute-start.3 = (f32[4,128,128]{2,1,0:T(8,128)S(1)}, f32[4,128,128]{2,1,0:T(8,128)S(1)}, u32[]{:S(2)}, u32[]{:S(2)}) collective-permute-start(f32[4,128,128]{2,1,0:T(8,128)S(1)} %copy-done), channel_id=1, source_target_pairs={{0,1},{1,0},{2,3},{3,2},{4,5},{5,4},{6,7},{7,6},{8,9},{9,8},{10,11... | collective-permute-start | bytes 786440 | tf_op jit(solution)/shard_map/ppermute | solution.py:536
  6.7 5.3 %collective-permute-start.2 = (f32[8,128]{1,0:T(8,128)S(1)}, f32[8,128]{1,0:T(8,128)S(1)}, u32[]{:S(2)}, u32[]{:S(2)}) collective-permute-start(f32[8,128]{1,0:T(8,128)S(1)} %get-tuple-element.38), channel_id=1, source_target_pairs={{20,0},{24,4},{28,8},{4,16},{8,20},{12,24},{21,1},{25,5},{29,9},{5... | collective-permute-start | bytes 12296 | tf_op jit(solution)/shard_map/ppermute | solution.py:547
  8.0 4.0 %collective-permute-start.1 = (f32[48,128]{1,0:T(8,128)S(1)}, f32[48,128]{1,0:T(8,128)S(1)}, u32[]{:S(2)}, u32[]{:S(2)}) collective-permute-start(f32[48,128]{1,0:T(8,128)S(1)} %get-tuple-element.37), channel_id=1, source_target_pairs={{0,16},{16,0},{1,17},{17,1},{2,18},{18,2},{3,19},{19,3},{4,20},{20... | collective-permute-start | bytes 73736 | tf_op jit(solution)/shard_map/ppermute | solution.py:546
  9.3 5.4 %collective-permute-start = (f32[96,128]{1,0:T(8,128)S(1)}, f32[96,128]{1,0:T(8,128)S(1)}, u32[]{:S(2)}, u32[]{:S(2)}) collective-permute-start(f32[96,128]{1,0:T(8,128)S(1)} %get-tuple-element.36), channel_id=1, source_target_pairs={{4,0},{8,4},{12,8},{5,1},{9,5},{13,9},{6,2},{10,6},{14,10},{7,3},{... | collective-permute-start | bytes 147464 | tf_op jit(solution)/shard_map/ppermute | solution.py:545
  10.6 4.1 %copy-start.4 = (s32[3,8,16,128]{3,2,1,0:T(8,128)S(1)}, s32[3,8,16,128]{3,2,1,0:T(8,128)}, u32[]{:S(2)}) copy-start(s32[3,8,16,128]{3,2,1,0:T(8,128)} %mask_ref.3) | copy-start | bytes 589828
  10.6 4.1 %copy-start.6 = (f32[81,81]{1,0:T(8,128)S(1)}, f32[81,81]{1,0:T(8,128)}, u32[]{:S(2)}) copy-start(f32[81,81]{1,0:T(8,128)} %stiff_ref.1) | copy-start | bytes 78736
  10.7 3.9 %copy-start.2 = (f32[3,8,16,128]{3,2,1,0:T(8,128)S(1)}, f32[3,8,16,128]{3,2,1,0:T(8,128)}, u32[]{:S(2)}) copy-start(f32[3,8,16,128]{3,2,1,0:T(8,128)} %force_ref.3) | copy-start | bytes 589828
  10.7 3.9 %copy-start.5 = (f32[120,81]{1,0:T(8,128)S(1)}, f32[120,81]{1,0:T(8,128)}, u32[]{:S(2)}) copy-start(f32[120,81]{1,0:T(8,128)} %constant.10.clone.place_ref) | copy-start | bytes 116644
  16.2 13.6 %all-to-all-start = ((f32[4,312,128]{2,1,0:T(8,128)}), f32[4,312,128]{2,1,0:T(8,128)S(1)}, u32[]{:S(2)}, u32[]{:S(2)}) async-start(f32[4,312,128]{2,1,0:T(8,128)} %get-tuple-element.39), calls=%async_computation | async-start | bytes 1277952 | tf_op jit(solution)/shard_map/all_to_all | solution.py:557
  22.1 3.3 %collective-permute-start.5 = (f32[1536,8]{0,1:T(8,128)S(1)}, f32[1536,8]{0,1:T(8,128)S(1)}, u32[]{:S(2)}, u32[]{:S(2)}) collective-permute-start(f32[1536,8]{0,1:T(8,128)S(1)} %pad_maximum_fusion), channel_id=1, source_target_pairs={{0,16},{16,0},{1,17},{17,1},{2,18},{18,2},{3,19},{19,3},{4,20},{20... | collective-permute-start | bytes 147464 | tf_op jit(solution)/shard_map/ppermute | solution.py:565
  35.2 5.3 %collective-permute-start.6 = (f32[528,128]{1,0:T(8,128)S(1)}, f32[528,128]{1,0:T(8,128)S(1)}, u32[]{:S(2)}, u32[]{:S(2)}) collective-permute-start(f32[528,128]{1,0:T(8,128)S(1)} %get-tuple-element.46), channel_id=1, source_target_pairs={{0,1},{1,0},{2,3},{3,2},{4,5},{5,4},{6,7},{7,6},{8,9},{9,8},{10,11... | collective-permute-start | bytes 811016 | tf_op jit(solution)/shard_map/ppermute | solution.py:536
  36.2 8.8 %collective-permute-start.7 = (f32[528,128]{1,0:T(8,128)S(1)}, f32[528,128]{1,0:T(8,128)S(1)}, u32[]{:S(2)}, u32[]{:S(2)}) collective-permute-start(f32[528,128]{1,0:T(8,128)S(1)} %get-tuple-element.47), channel_id=1, source_target_pairs={{1,2},{2,1},{3,4},{4,3},{5,6},{6,5},{7,8},{8,7},{9,10},{10,9},{11,... | collective-permute-start | bytes 811016 | tf_op jit(solution)/shard_map/ppermute | solution.py:536
  49.6 6.7 %collective-permute-start.8 = (f32[528,128]{1,0:T(8,128)S(1)}, f32[528,128]{1,0:T(8,128)S(1)}, u32[]{:S(2)}, u32[]{:S(2)}) collective-permute-start(f32[528,128]{1,0:T(8,128)S(1)} %get-tuple-element.50), channel_id=1, source_target_pairs={{0,1},{1,0},{2,3},{3,2},{4,5},{5,4},{6,7},{7,6},{8,9},{9,8},{10,11... | collective-permute-start | bytes 811016 | tf_op jit(solution)/shard_map/ppermute | solution.py:536
  51.6 9.0 %collective-permute-start.9 = (f32[528,128]{1,0:T(8,128)S(1)}, f32[528,128]{1,0:T(8,128)S(1)}, u32[]{:S(2)}, u32[]{:S(2)}) collective-permute-start(f32[528,128]{1,0:T(8,128)S(1)} %get-tuple-element.51), channel_id=1, source_target_pairs={{1,2},{2,1},{3,4},{4,3},{5,6},{6,5},{7,8},{8,7},{9,10},{10,9},{11,... | collective-permute-start | bytes 811016 | tf_op jit(solution)/shard_map/ppermute | solution.py:536
  78.5 13.5 %all-to-all-start.2 = ((f32[4,3,2,16,128]{4,3,2,1,0:T(8,128)}), f32[4,3,2,16,128]{4,3,2,1,0:T(8,128)S(1)}, u32[]{:S(2)}, u32[]{:S(2)}) async-start(f32[4,3,2,16,128]{4,3,2,1,0:T(8,128)} %get-tuple-element.63), calls=%async_computation.2 | async-start | bytes 393216 | tf_op jit(solution)/shard_map/all_to_all | solution.py:623
  83.6 5.9 %collective-permute-start.11 = (f32[32,128]{1,0:T(8,128)S(1)}, f32[32,128]{1,0:T(8,128)S(1)}, u32[]{:S(2)}, u32[]{:S(2)}) collective-permute-start(f32[32,128]{1,0:T(8,128)S(1)} %get-tuple-element.61.grad_ref), channel_id=1, source_target_pairs={{1,2},{2,1},{3,4},{4,3},{5,6},{6,5},{7,8},{8,7},{9,10},{10,9},{11,... | collective-permute-start | bytes 49160 | tf_op jit(solution)/shard_map/ppermute | solution.py:536
  85.5 4.0 %collective-permute-start.10 = (f32[32,128]{1,0:T(8,128)S(1)}, f32[32,128]{1,0:T(8,128)S(1)}, u32[]{:S(2)}, u32[]{:S(2)}) collective-permute-start(f32[32,128]{1,0:T(8,128)S(1)} %get-tuple-element.61.grad_ref), channel_id=1, source_target_pairs={{0,1},{1,0},{2,3},{3,2},{4,5},{5,4},{6,7},{7,6},{8,9},{9,8},{10,11... | collective-permute-start | bytes 49160 | tf_op jit(solution)/shard_map/ppermute | solution.py:536

commit v4 on v3

--- a/solution.py
+++ b/solution.py
@@ -248,10 +248,10 @@
         return tuple(right[2])
 
     if out_ref is None:
-        lax.fori_loop(0, columns // 2, lambda i, c: body(i, c), 0)
+        lax.fori_loop(0, columns // 2, lambda i, c: body(i, c), 0, unroll=min(16, columns // 2))
     else:
         zero = jnp.zeros((8, LANES), F32)
-        lax.fori_loop(0, columns // 2, body, (zero,) * 5)
+        lax.fori_loop(0, columns // 2, body, (zero,) * 5, unroll=min(16, columns // 2))
         for a in range(3):
             for node in range(2 * columns, tiles):
                 at = (a * tiles + node) * 8

time: 93.2 us -> 83.4 us (0.89)
  Pallas kernels: 23.7 us -> 13.9 us
    pallas_call x1, Pallas kernels: 5.34 us -> 1.78 us  [on_device(): pl.pallas_call(first_kernel, out_shape=(node_set, node_set, node_set, pla...]
    pallas_call x1, Pallas kernels: 4.61 us -> 1.15 us  [on_device(): pl.pallas_call(second_kernel, out_shape=(node_set, node_set, plane, plane...]
    pallas_call x1, Pallas kernels: 4.23 us -> 1.46 us  [on_device(): pl.pallas_call(third_kernel, out_shape=(node_set, element, element, eleme...]
  transfers between devices with their start and end apart: 14 -> 14, of which waited for: 7 -> 7; matrix products, arithmetic and copies ran while one was open for 1% -> 1% of each run, Pallas kernels for 8% -> 9%
where the time goes in v4:
time: 83.4 us; the launch traced here: 82.9 us
  starting transfers between devices  33.9 us (41%)
  waiting for transfers between devices  18.3 us (22%)
  Pallas kernels  13.9 us (17%)
  blocking collectives  12.4 us (15%)
  local copies, waits for them, and re-layouts  3.15 us (4%)
  between operations  0.85 us (1%)
    ppermute x4, starting transfers between devices, beside(): lax.ppermute(to_b, LINE, pairs_b)  14.6 us
    all_to_all x1, blocking collectives, on_device(): moments = lax.all_to_all(moments, ('role', 'gx', 'gy'), 0, 0, tiled=True)  12.4 us
    ppermute x4, waiting for transfers between devices, beside(): lax.ppermute(to_b, LINE, pairs_b)  12.2 us
    all_to_all x1, starting transfers between devices, on_device(): rf = lax.all_to_all(pack, 'gy', 0, 0)  5.45 us
    all_to_all x1, starting transfers between devices, on_device(): u = lax.all_to_all(u, 'gy', 0, 0)  5.07 us
    pallas_call x1, Pallas kernels, on_device(): pl.pallas_call(filter_kernel, out_shape=(shape(planes + 4, fy, 2 * fz), e...  3.85 us
    ppermute x4, starting transfers between devices, beside(): lax.ppermute(to_a, LINE, pairs_a)  3.64 us
    ppermute x1, waiting for transfers between devices, on_device(): next_plane = lax.ppermute(plane0, 'gx', [(i + 1, i) for i in range(gx - 1)])  2.74 us
  transfers between devices with their start and end apart: 14, of which 7 were waited for; matrix products, arithmetic and copies ran while one was open for 1% of the time, Pallas kernels for 9%

profile of v4, /device:TPU:3, one launch (start us, length us, event | category | flops | bytes accessed | tf_op | source)
XLA Modules:
  0.0 82.9 jit_solution(11896760769608971927)
XLA Ops:
  0.6 0.0 copy-start.1
  0.7 1.0 %copy-done.1 = f32[3,8,16,128]{3,2,1,0:T(8,128)S(1)} copy-done((f32[3,8,16,128]{3,2,1,0:T(8,128)S(1)}, f32[3,8,16,128]{3,2,1,0:T(8,128)}, u32[]{:S(2)}) %copy-start.1) | copy-done | bytes 196632
  1.6 0.9 %copy-done.3 = s32[3,8,16,128]{3,2,1,0:T(8,128)S(1)} copy-done((s32[3,8,16,128]{3,2,1,0:T(8,128)S(1)}, s32[3,8,16,128]{3,2,1,0:T(8,128)}, u32[]{:S(2)}) %copy-start.3) | copy-done | bytes 196632
  2.5 0.3 rows.1
  2.8 3.7 %collective-permute-start.4 = (f32[4,128,128]{2,1,0:T(8,128)S(1)}, f32[4,128,128]{2,1,0:T(8,128)S(1)}, u32[]{:S(2)}, u32[]{:S(2)}) collective-permute-start(f32[4,128,128]{2,1,0:T(8,128)S(1)} %copy-done), channel_id=1, source_target_pairs={{1,2},{2,1},{3,4},{4,3},{5,6},{6,5},{7,8},{8,7},{9,10},{10,9},{11,... | collective-permute-start | bytes 786440 | tf_op jit(solution)/shard_map/ppermute | solution.py:536
  6.6 0.1 collective-permute-start.3
  6.7 1.3 %collective-permute-start.2 = (f32[8,128]{1,0:T(8,128)S(1)}, f32[8,128]{1,0:T(8,128)S(1)}, u32[]{:S(2)}, u32[]{:S(2)}) collective-permute-start(f32[8,128]{1,0:T(8,128)S(1)} %get-tuple-element.38), channel_id=1, source_target_pairs={{20,0},{24,4},{28,8},{4,16},{8,20},{12,24},{21,1},{25,5},{29,9},{5... | collective-permute-start | bytes 12296 | tf_op jit(solution)/shard_map/ppermute | solution.py:547
  8.0 1.3 %collective-permute-start.1 = (f32[48,128]{1,0:T(8,128)S(1)}, f32[48,128]{1,0:T(8,128)S(1)}, u32[]{:S(2)}, u32[]{:S(2)}) collective-permute-start(f32[48,128]{1,0:T(8,128)S(1)} %get-tuple-element.37), channel_id=1, source_target_pairs={{0,16},{16,0},{1,17},{17,1},{2,18},{18,2},{3,19},{19,3},{4,20},{20... | collective-permute-start | bytes 73736 | tf_op jit(solution)/shard_map/ppermute | solution.py:546
  9.3 1.3 %collective-permute-start = (f32[96,128]{1,0:T(8,128)S(1)}, f32[96,128]{1,0:T(8,128)S(1)}, u32[]{:S(2)}, u32[]{:S(2)}) collective-permute-start(f32[96,128]{1,0:T(8,128)S(1)} %get-tuple-element.36), channel_id=1, source_target_pairs={{4,0},{8,4},{12,8},{5,1},{9,5},{13,9},{6,2},{10,6},{14,10},{7,3},{... | collective-permute-start | bytes 147464 | tf_op jit(solution)/shard_map/ppermute | solution.py:545
  10.6 0.0 copy-start.4
  10.6 0.0 copy-start.6
  10.6 0.1 slice_select_fusion.2
  10.7 0.0 copy-start.2
  10.7 0.0 copy-start.5
  10.8 0.1 copy.8
  10.8 1.1 %collective-permute-done.2.corner_ref = f32[8,128]{1,0:T(8,128)S(1)} collective-permute-done((f32[8,128]{1,0:T(8,128)S(1)}, f32[8,128]{1,0:T(8,128)S(1)}, u32[]{:S(2)}, u32[]{:S(2)}) %collective-permute-start.2) | collective-permute-done | bytes 4128 | tf_op jit(solution)/shard_map/ppermute | solution.py:547
  11.9 0.0 collective-permute-done.1.strip_ref
  11.9 2.7 %collective-permute-done.plane_ref = f32[96,128]{1,0:T(8,128)S(1)} collective-permute-done((f32[96,128]{1,0:T(8,128)S(1)}, f32[96,128]{1,0:T(8,128)S(1)}, u32[]{:S(2)}, u32[]{:S(2)}) %collective-permute-start) | collective-permute-done | bytes 49184 | tf_op jit(solution)/shard_map/ppermute | solution.py:545
  14.7 1.5 %pack.1 = (f32[4,312,128]{2,1,0:T(8,128)}, bf16[240,240]{1,0:T(8,128)(2,1)S(1)}) custom-call(f32[3,8,16,128]{3,2,1,0:T(8,128)S(1)} %copy-done.2, s32[3,8,16,128]{3,2,1,0:T(8,128)S(1)} %copy-done.4, f32[96,128]{1,0:T(8,128)S(1)} %collective-permute-done.plane_ref, f32[48,128]{1,0:T(8,128)S(1)} %collective-permute-done.1.strip_ref, ...), custom_call_target="tpu_custom_call" | custom-call | tf_op jit(solution)/shard_map/pack/pallas_call | solution.py:551
  16.2 5.4 %all-to-all-start = ((f32[4,312,128]{2,1,0:T(8,128)}), f32[4,312,128]{2,1,0:T(8,128)S(1)}, u32[]{:S(2)}, u32[]{:S(2)}) async-start(f32[4,312,128]{2,1,0:T(8,128)} %get-tuple-element.39), calls=%async_computation | async-start | bytes 1277952 | tf_op jit(solution)/shard_map/all_to_all | solution.py:557
  21.6 0.0 collective-permute-done.4.db_ref
  21.6 0.1 slice_select_fusion
  21.8 0.1 copy.10
  21.9 0.1 slice_select_fusion.1
  22.0 0.1 copy.9
  22.1 1.3 %collective-permute-start.5 = (f32[1536,8]{0,1:T(8,128)S(1)}, f32[1536,8]{0,1:T(8,128)S(1)}, u32[]{:S(2)}, u32[]{:S(2)}) collective-permute-start(f32[1536,8]{0,1:T(8,128)S(1)} %pad_maximum_fusion), channel_id=1, source_target_pairs={{0,16},{16,0},{1,17},{17,1},{2,18},{18,2},{3,19},{19,3},{4,20},{20... | collective-permute-start | bytes 147464 | tf_op jit(solution)/shard_map/ppermute | solution.py:565
  23.4 2.0 %collective-permute-done.5 = f32[1536,8]{0,1:T(8,128)S(1)} collective-permute-done((f32[1536,8]{0,1:T(8,128)S(1)}, f32[1536,8]{0,1:T(8,128)S(1)}, u32[]{:S(2)}, u32[]{:S(2)}) %collective-permute-start.5) | collective-permute-done | bytes 49184 | tf_op jit(solution)/shard_map/ppermute | solution.py:565
  25.4 0.3 copy.11.strip_ref
  25.7 3.9 %filter.1 = (f32[8,128,256]{2,1,0:T(8,128)S(1)}, f32[32,128]{1,0:T(8,128)S(1)}, f32[32,128]{1,0:T(8,128)S(1)}) custom-call(f32[4,128,128]{2,1,0:T(8,128)S(1)} %copy-done, f32[4,128,128]{2,1,0:T(8,128)S(1)} %collective-permute-done.3.da_ref, f32[4,128,128]{2,1,0:T(8,128)S(1)} %collective-permute-done.4.db_ref, f32[1536,8]{1,0:T(8,128)S(1)} %copy.11.strip_ref), custom_call_target="tpu_custom_call" | custom-call | flops 30000000 | bytes 4000000 | tf_op jit(solution)/shard_map/filter/pallas_call | solution.py:576
  29.5 0.3 all-to-all-done.rf_ref
  29.8 1.8 %first.1 = (f32[1584,128]{1,0:T(8,128)S(1)}, f32[1584,128]{1,0:T(8,128)S(1)}, f32[1584,128]{1,0:T(8,128)S(1)}, f32[528,128]{1,0:T(8,128)S(1)}, f32[528,128]{1,0:T(8,128)S(1)}, /*index=5*/f32[32,128]{1,0:T(8,128)S(1)}) custom-call(f32[4,312,128]{2,1,0:T(8,128)S(1)} %all-to-all-done.rf_ref, f32[32,128]{1,0:T(8,128)S(1)} %get-tuple-element.41.factor_ref, ...), custom_call_target="tpu_custom_call" | custom-call | tf_op jit(solution)/shard_map/first/pallas_call | solution.py:584
  31.6 1.0 %collective-permute-start.6 = (f32[528,128]{1,0:T(8,128)S(1)}, f32[528,128]{1,0:T(8,128)S(1)}, u32[]{:S(2)}, u32[]{:S(2)}) collective-permute-start(f32[528,128]{1,0:T(8,128)S(1)} %get-tuple-element.46), channel_id=1, source_target_pairs={{0,1},{1,0},{2,3},{3,2},{4,5},{5,4},{6,7},{7,6},{8,9},{9,8},{10,11... | collective-permute-start | bytes 811016 | tf_op jit(solution)/shard_map/ppermute | solution.py:536
  32.6 4.3 %collective-permute-start.7 = (f32[528,128]{1,0:T(8,128)S(1)}, f32[528,128]{1,0:T(8,128)S(1)}, u32[]{:S(2)}, u32[]{:S(2)}) collective-permute-start(f32[528,128]{1,0:T(8,128)S(1)} %get-tuple-element.47), channel_id=1, source_target_pairs={{1,2},{2,1},{3,4},{4,3},{5,6},{6,5},{7,8},{8,7},{9,10},{10,9},{11,... | collective-permute-start | bytes 811016 | tf_op jit(solution)/shard_map/ppermute | solution.py:536
  36.9 0.0 collective-permute-done.6.from_a
  36.9 4.5 %collective-permute-done.7.from_b = f32[528,128]{1,0:T(8,128)S(1)} collective-permute-done((f32[528,128]{1,0:T(8,128)S(1)}, f32[528,128]{1,0:T(8,128)S(1)}, u32[]{:S(2)}, u32[]{:S(2)}) %collective-permute-start.7) | collective-permute-done | bytes 270368 | tf_op jit(solution)/shard_map/ppermute | solution.py:536
  41.4 1.1 %second.1 = (f32[1584,128]{1,0:T(8,128)S(1)}, f32[1584,128]{1,0:T(8,128)S(1)}, f32[528,128]{1,0:T(8,128)S(1)}, f32[528,128]{1,0:T(8,128)S(1)}, f32[32,128]{1,0:T(8,128)S(1)}, /*index=5*/f32[32,128]{1,0:T(8,128)S(1)}) custom-call(f32[1584,128]{1,0:T(8,128)S(1)} %get-tuple-element.43.prev_ref.v0_ref, f32[1584,128]{1,0:T(8,128)S(1)} %get-tuple-element.44.free_ref, ...), custom_call_target="tpu_custom_call" | custom-call | tf_op jit(solution)/shard_map/second/pallas_call | solution.py:592
  42.6 2.0 %collective-permute-start.8 = (f32[528,128]{1,0:T(8,128)S(1)}, f32[528,128]{1,0:T(8,128)S(1)}, u32[]{:S(2)}, u32[]{:S(2)}) collective-permute-start(f32[528,128]{1,0:T(8,128)S(1)} %get-tuple-element.50), channel_id=1, source_target_pairs={{0,1},{1,0},{2,3},{3,2},{4,5},{5,4},{6,7},{7,6},{8,9},{9,8},{10,11... | collective-permute-start | bytes 811016 | tf_op jit(solution)/shard_map/ppermute | solution.py:536
  44.6 4.7 %collective-permute-start.9 = (f32[528,128]{1,0:T(8,128)S(1)}, f32[528,128]{1,0:T(8,128)S(1)}, u32[]{:S(2)}, u32[]{:S(2)}) collective-permute-start(f32[528,128]{1,0:T(8,128)S(1)} %get-tuple-element.51), channel_id=1, source_target_pairs={{1,2},{2,1},{3,4},{4,3},{5,6},{6,5},{7,8},{8,7},{9,10},{10,9},{11,... | collective-permute-start | bytes 811016 | tf_op jit(solution)/shard_map/ppermute | solution.py:536
  49.3 4.2 %collective-permute-done.9.from_b = f32[528,128]{1,0:T(8,128)S(1)} collective-permute-done((f32[528,128]{1,0:T(8,128)S(1)}, f32[528,128]{1,0:T(8,128)S(1)}, u32[]{:S(2)}, u32[]{:S(2)}) %collective-permute-start.9) | collective-permute-done | bytes 270368 | tf_op jit(solution)/shard_map/ppermute | solution.py:536
  53.5 1.5 %third.1 = (f32[1584,128]{1,0:T(8,128)S(1)}, f32[32,128]{1,0:T(8,128)S(1)}, f32[32,128]{1,0:T(8,128)S(1)}, f32[32,128]{1,0:T(8,128)S(1)}, f32[32,128]{1,0:T(8,128)S(1)}) custom-call(f32[1584,128]{1,0:T(8,128)S(1)} %get-tuple-element.43.prev_ref.v0_ref, f32[1584,128]{1,0:T(8,128)S(1)} %get-tuple-element.48.v1_ref, ...), custom_call_target="tpu_custom_call" | custom-call | tf_op jit(solution)/shard_map/third/pallas_call | solution.py:600
  55.0 12.4 %all_to_all.21 = f32[32,1,128]{2,1,0:T(1,128)S(1)} all-to-all(f32[32,1,128]{2,1,0:T(1,128)S(1)} %bitcast.10), channel_id=1, replica_groups=mesh['role'=2,'gx'=4,'gy'=4] {'role','gx','gy'}, dimensions={0} | all-to-all | bytes 32768 | tf_op jit(solution)/shard_map/all_to_all | solution.py:607
  67.4 1.4 %combine.1 = (f32[32,128]{1,0:T(8,128)S(1)}, f32[4,3,2,16,128]{4,3,2,1,0:T(8,128)}) custom-call(f32[32,128]{1,0:T(8,128)S(1)} %bitcast.9, f32[1584,128]{1,0:T(8,128)S(1)} %get-tuple-element.43.prev_ref.v0_ref, f32[1584,128]{1,0:T(8,128)S(1)} %get-tuple-element.48.v1_ref, f32[1584,128]{1,0:T(8,128)S(1)} %get-tuple-element.56.v2_ref, ...), custom_call_target="tpu_custom_call" | custom-call | tf_op jit(solution)/shard_map/combine/pallas_call | solution.py:608
  68.7 5.1 %all-to-all-start.2 = ((f32[4,3,2,16,128]{4,3,2,1,0:T(8,128)}), f32[4,3,2,16,128]{4,3,2,1,0:T(8,128)S(1)}, u32[]{:S(2)}, u32[]{:S(2)}) async-start(f32[4,3,2,16,128]{4,3,2,1,0:T(8,128)} %get-tuple-element.63), calls=%async_computation.2 | async-start | bytes 393216 | tf_op jit(solution)/shard_map/all_to_all | solution.py:623
  73.8 1.9 %collective-permute-start.11 = (f32[32,128]{1,0:T(8,128)S(1)}, f32[32,128]{1,0:T(8,128)S(1)}, u32[]{:S(2)}, u32[]{:S(2)}) collective-permute-start(f32[32,128]{1,0:T(8,128)S(1)} %get-tuple-element.61.grad_ref), channel_id=1, source_target_pairs={{1,2},{2,1},{3,4},{4,3},{5,6},{6,5},{7,8},{8,7},{9,10},{10,9},{11,... | collective-permute-start | bytes 49160 | tf_op jit(solution)/shard_map/ppermute | solution.py:536
  75.7 0.6 collective-permute-start.10
  76.3 3.5 %collective-permute-done.11.gb_ref = f32[32,128]{1,0:T(8,128)S(1)} collective-permute-done((f32[32,128]{1,0:T(8,128)S(1)}, f32[32,128]{1,0:T(8,128)S(1)}, u32[]{:S(2)}, u32[]{:S(2)}) %collective-permute-start.11) | collective-permute-done | bytes 16416 | tf_op jit(solution)/shard_map/ppermute | solution.py:536
  79.8 2.5 %last.1 = f32[4,128,128]{2,1,0:T(8,128)} custom-call(f32[32,128]{1,0:T(8,128)S(1)} %get-tuple-element.61.grad_ref, f32[32,128]{1,0:T(8,128)S(1)} %collective-permute-done.10.ga_ref, f32[32,128]{1,0:T(8,128)S(1)} %collective-permute-done.11.gb_ref, f32[8,128,256]{2,1,0:T(8,128)S(1)} %get-tuple-element.62.sw_ref), custom_call_target="tpu_custom_call" | custom-call | tf_op jit(solution)/shard_map/last/pallas_call | solution.py:616
  82.2 0.7 copy.13
  (12 shorter events, 0.0 us)
Async XLA Ops:
  0.6 2.2 %copy-start = (f32[4,128,128]{2,1,0:T(8,128)S(1)}, f32[4,128,128]{2,1,0:T(8,128)}, u32[]{:S(2)}) copy-start(f32[4,128,128]{2,1,0:T(8,128)} %design_ref) | copy-start | bytes 786436
  0.6 1.0 %copy-start.1 = (f32[3,8,16,128]{3,2,1,0:T(8,128)S(1)}, f32[3,8,16,128]{3,2,1,0:T(8,128)}, u32[]{:S(2)}) copy-start(f32[3,8,16,128]{3,2,1,0:T(8,128)} %force_ref.3) | copy-start | bytes 589828
  1.6 0.9 %copy-start.3 = (s32[3,8,16,128]{3,2,1,0:T(8,128)S(1)}, s32[3,8,16,128]{3,2,1,0:T(8,128)}, u32[]{:S(2)}) copy-start(s32[3,8,16,128]{3,2,1,0:T(8,128)} %mask_ref.3) | copy-start | bytes 589828
  2.8 18.8 %collective-permute-start.4 = (f32[4,128,128]{2,1,0:T(8,128)S(1)}, f32[4,128,128]{2,1,0:T(8,128)S(1)}, u32[]{:S(2)}, u32[]{:S(2)}) collective-permute-start(f32[4,128,128]{2,1,0:T(8,128)S(1)} %copy-done), channel_id=1, source_target_pairs={{1,2},{2,1},{3,4},{4,3},{5,6},{6,5},{7,8},{8,7},{9,10},{10,9},{11,... | collective-permute-start | bytes 786440 | tf_op jit(solution)/shard_map/ppermute | solution.py:536
  6.6 15.3 %collective-permute-start.3 = (f32[4,128,128]{2,1,0:T(8,128)S(1)}, f32[4,128,128]{2,1,0:T(8,128)S(1)}, u32[]{:S(2)}, u32[]{:S(2)}) collective-permute-start(f32[4,128,128]{2,1,0:T(8,128)S(1)} %copy-done), channel_id=1, source_target_pairs={{0,1},{1,0},{2,3},{3,2},{4,5},{5,4},{6,7},{7,6},{8,9},{9,8},{10,11... | collective-permute-start | bytes 786440 | tf_op jit(solution)/shard_map/ppermute | solution.py:536
  6.7 5.3 %collective-permute-start.2 = (f32[8,128]{1,0:T(8,128)S(1)}, f32[8,128]{1,0:T(8,128)S(1)}, u32[]{:S(2)}, u32[]{:S(2)}) collective-permute-start(f32[8,128]{1,0:T(8,128)S(1)} %get-tuple-element.38), channel_id=1, source_target_pairs={{20,0},{24,4},{28,8},{4,16},{8,20},{12,24},{21,1},{25,5},{29,9},{5... | collective-permute-start | bytes 12296 | tf_op jit(solution)/shard_map/ppermute | solution.py:547
  8.0 4.0 %collective-permute-start.1 = (f32[48,128]{1,0:T(8,128)S(1)}, f32[48,128]{1,0:T(8,128)S(1)}, u32[]{:S(2)}, u32[]{:S(2)}) collective-permute-start(f32[48,128]{1,0:T(8,128)S(1)} %get-tuple-element.37), channel_id=1, source_target_pairs={{0,16},{16,0},{1,17},{17,1},{2,18},{18,2},{3,19},{19,3},{4,20},{20... | collective-permute-start | bytes 73736 | tf_op jit(solution)/shard_map/ppermute | solution.py:546
  9.3 5.4 %collective-permute-start = (f32[96,128]{1,0:T(8,128)S(1)}, f32[96,128]{1,0:T(8,128)S(1)}, u32[]{:S(2)}, u32[]{:S(2)}) collective-permute-start(f32[96,128]{1,0:T(8,128)S(1)} %get-tuple-element.36), channel_id=1, source_target_pairs={{4,0},{8,4},{12,8},{5,1},{9,5},{13,9},{6,2},{10,6},{14,10},{7,3},{... | collective-permute-start | bytes 147464 | tf_op jit(solution)/shard_map/ppermute | solution.py:545
  10.6 4.1 %copy-start.4 = (s32[3,8,16,128]{3,2,1,0:T(8,128)S(1)}, s32[3,8,16,128]{3,2,1,0:T(8,128)}, u32[]{:S(2)}) copy-start(s32[3,8,16,128]{3,2,1,0:T(8,128)} %mask_ref.3) | copy-start | bytes 589828
  10.6 4.1 %copy-start.6 = (f32[81,81]{1,0:T(8,128)S(1)}, f32[81,81]{1,0:T(8,128)}, u32[]{:S(2)}) copy-start(f32[81,81]{1,0:T(8,128)} %stiff_ref.1) | copy-start | bytes 78736
  10.7 3.9 %copy-start.2 = (f32[3,8,16,128]{3,2,1,0:T(8,128)S(1)}, f32[3,8,16,128]{3,2,1,0:T(8,128)}, u32[]{:S(2)}) copy-start(f32[3,8,16,128]{3,2,1,0:T(8,128)} %force_ref.3) | copy-start | bytes 589828
  10.7 3.9 %copy-start.5 = (f32[120,81]{1,0:T(8,128)S(1)}, f32[120,81]{1,0:T(8,128)}, u32[]{:S(2)}) copy-start(f32[120,81]{1,0:T(8,128)} %constant.10.clone.place_ref) | copy-start | bytes 116644
  16.2 13.6 %all-to-all-start = ((f32[4,312,128]{2,1,0:T(8,128)}), f32[4,312,128]{2,1,0:T(8,128)S(1)}, u32[]{:S(2)}, u32[]{:S(2)}) async-start(f32[4,312,128]{2,1,0:T(8,128)} %get-tuple-element.39), calls=%async_computation | async-start | bytes 1277952 | tf_op jit(solution)/shard_map/all_to_all | solution.py:557
  22.1 3.3 %collective-permute-start.5 = (f32[1536,8]{0,1:T(8,128)S(1)}, f32[1536,8]{0,1:T(8,128)S(1)}, u32[]{:S(2)}, u32[]{:S(2)}) collective-permute-start(f32[1536,8]{0,1:T(8,128)S(1)} %pad_maximum_fusion), channel_id=1, source_target_pairs={{0,16},{16,0},{1,17},{17,1},{2,18},{18,2},{3,19},{19,3},{4,20},{20... | collective-permute-start | bytes 147464 | tf_op jit(solution)/shard_map/ppermute | solution.py:565
  31.6 5.3 %collective-permute-start.6 = (f32[528,128]{1,0:T(8,128)S(1)}, f32[528,128]{1,0:T(8,128)S(1)}, u32[]{:S(2)}, u32[]{:S(2)}) collective-permute-start(f32[528,128]{1,0:T(8,128)S(1)} %get-tuple-element.46), channel_id=1, source_target_pairs={{0,1},{1,0},{2,3},{3,2},{4,5},{5,4},{6,7},{7,6},{8,9},{9,8},{10,11... | collective-permute-start | bytes 811016 | tf_op jit(solution)/shard_map/ppermute | solution.py:536
  32.6 8.8 %collective-permute-start.7 = (f32[528,128]{1,0:T(8,128)S(1)}, f32[528,128]{1,0:T(8,128)S(1)}, u32[]{:S(2)}, u32[]{:S(2)}) collective-permute-start(f32[528,128]{1,0:T(8,128)S(1)} %get-tuple-element.47), channel_id=1, source_target_pairs={{1,2},{2,1},{3,4},{4,3},{5,6},{6,5},{7,8},{8,7},{9,10},{10,9},{11,... | collective-permute-start | bytes 811016 | tf_op jit(solution)/shard_map/ppermute | solution.py:536
  42.6 6.7 %collective-permute-start.8 = (f32[528,128]{1,0:T(8,128)S(1)}, f32[528,128]{1,0:T(8,128)S(1)}, u32[]{:S(2)}, u32[]{:S(2)}) collective-permute-start(f32[528,128]{1,0:T(8,128)S(1)} %get-tuple-element.50), channel_id=1, source_target_pairs={{0,1},{1,0},{2,3},{3,2},{4,5},{5,4},{6,7},{7,6},{8,9},{9,8},{10,11... | collective-permute-start | bytes 811016 | tf_op jit(solution)/shard_map/ppermute | solution.py:536
  44.6 9.0 %collective-permute-start.9 = (f32[528,128]{1,0:T(8,128)S(1)}, f32[528,128]{1,0:T(8,128)S(1)}, u32[]{:S(2)}, u32[]{:S(2)}) collective-permute-start(f32[528,128]{1,0:T(8,128)S(1)} %get-tuple-element.51), channel_id=1, source_target_pairs={{1,2},{2,1},{3,4},{4,3},{5,6},{6,5},{7,8},{8,7},{9,10},{10,9},{11,... | collective-permute-start | bytes 811016 | tf_op jit(solution)/shard_map/ppermute | solution.py:536
  68.7 13.5 %all-to-all-start.2 = ((f32[4,3,2,16,128]{4,3,2,1,0:T(8,128)}), f32[4,3,2,16,128]{4,3,2,1,0:T(8,128)S(1)}, u32[]{:S(2)}, u32[]{:S(2)}) async-start(f32[4,3,2,16,128]{4,3,2,1,0:T(8,128)} %get-tuple-element.63), calls=%async_computation.2 | async-start | bytes 393216 | tf_op jit(solution)/shard_map/all_to_all | solution.py:623
  73.8 5.9 %collective-permute-start.11 = (f32[32,128]{1,0:T(8,128)S(1)}, f32[32,128]{1,0:T(8,128)S(1)}, u32[]{:S(2)}, u32[]{:S(2)}) collective-permute-start(f32[32,128]{1,0:T(8,128)S(1)} %get-tuple-element.61.grad_ref), channel_id=1, source_target_pairs={{1,2},{2,1},{3,4},{4,3},{5,6},{6,5},{7,8},{8,7},{9,10},{10,9},{11,... | collective-permute-start | bytes 49160 | tf_op jit(solution)/shard_map/ppermute | solution.py:536
  75.7 4.0 %collective-permute-start.10 = (f32[32,128]{1,0:T(8,128)S(1)}, f32[32,128]{1,0:T(8,128)S(1)}, u32[]{:S(2)}, u32[]{:S(2)}) collective-permute-start(f32[32,128]{1,0:T(8,128)S(1)} %get-tuple-element.61.grad_ref), channel_id=1, source_target_pairs={{0,1},{1,0},{2,3},{3,2},{4,5},{5,4},{6,7},{7,6},{8,9},{9,8},{10,11... | collective-permute-start | bytes 49160 | tf_op jit(solution)/shard_map/ppermute | solution.py:536

commit v5 on v4

--- a/solution.py
+++ b/solution.py
@@ -5,6 +5,7 @@
 from jax.experimental import pallas as pl
 from jax.experimental.pallas import tpu as pltpu
 from jax.sharding import PartitionSpec as P
+
 
 SHARPNESS = 4.0
 THRESHOLD = 0.5
@@ -100,7 +101,15 @@
     return x[:rows]
 
 
-def strip_rows_kernel(force_ref, mask_ref, plane_ref, strip_ref, corner_ref):
+def strip_rows_kernel(force_hbm, mask_hbm, plane_ref, strip_ref, corner_ref, force_ref, mask_ref, sems):
+    copies = (
+        pltpu.make_async_copy(force_hbm, force_ref, sems.at[0]),
+        pltpu.make_async_copy(mask_hbm, mask_ref, sems.at[1]),
+    )
+    for copy in copies:
+        copy.start()
+    for copy in copies:
+        copy.wait()
     _, bx, by, fz = force_ref.shape
     role, _ = where_am_i()
     first = jnp.where(role == 0, fz - STRIP, 0)
@@ -258,23 +267,80 @@
                 out_ref[at : at + 8, :] = zero
 
 
+def pack_pair(x, y):
+    lane = iota((8, LANES), 1)
+    row = iota((8, LANES), 0)
+    half = LANES // 2
+    even = jnp.where(row < 4, x, pltpu.roll(y, 4, 0))
+    odd = jnp.where(row < 4, pltpu.roll(x, 4, 0), y)
+    main = jnp.where(lane < half, even, pltpu.roll(odd, half, 1))
+    edge = jnp.zeros((8, LANES), F32)
+    for tile, first in ((x, 0), (y, 28)):
+        moved = pltpu.roll(tile, half + first, 1, stride=4, stride_axis=0)
+        at = lane - first - 4 * row
+        edge = jnp.where(((at >= 0) & (at < 4)) | ((at >= 60) & (at < 64)), moved, edge)
+    for shift in (4, 2, 1):
+        edge = edge + pltpu.roll(edge, shift, 0)
+    return jnp.where(row == 3, edge, main)
+
+
+def unpack_pair(x):
+    lane = iota((8, LANES), 1)
+    row = iota((8, LANES), 0)
+    half = LANES // 2
+    own_even = (lane < half) & (row < 3)
+    live = (row & 3) < 3
+    own_odd = (lane < half) & (row >= 4) & live
+    rim = (lane // 4 == half // 4) | (lane // 4 == LANES // 4 - 1)
+    swapped = pltpu.roll(x, half, 1)
+    first = jnp.where(own_even, x, jnp.where(own_odd, pltpu.roll(swapped, 4, 0), 0.0))
+    second = jnp.where(own_even, pltpu.roll(x, 4, 0), jnp.where(own_odd, swapped, 0.0))
+    edge = jnp.broadcast_to(x[3:4], (8, LANES))
+    out = []
+    for tile, start in ((first, 0), (second, 28)):
+        for r in (0, 1, 2, 4, 5, 6):
+            tile = jnp.where(rim & (row == r), pltpu.roll(edge, (half - start - 4 * r) % LANES, 1), tile)
+        out.append(tile)
+    return out
+
+
 def send_planes(local_ref, tiles, slab, to_a, to_b):
     count = plane_rows(tiles)
-    low = local_ref[0:count]
-    high = local_ref[2 * count : 3 * count]
+    half = count // 2
     even = slab % 2 == 0
-    to_a[...] = jnp.where(even, high, low)
-    to_b[...] = jnp.where(even, low, high)
+
+    def body(i, _):
+        at = pl.multiple_of(i * 8, 8)
+
+        def tile(start):
+            return local_ref[pl.ds(start + at, 8), :]
+
+        low = pack_pair(tile(0), tile(half))
+        high = pack_pair(tile(2 * count), tile(2 * count + half))
+        to_a[pl.ds(at, 8), :] = jnp.where(even, high, low)
+        to_b[pl.ds(at, 8), :] = jnp.where(even, low, high)
+        return 0
+
+    lax.fori_loop(0, tiles // 2, body, 0, unroll=11)
 
 
 def gather_nodes(local_ref, from_a, from_b, free_ref, tiles, slab, nodes_ref):
     count = plane_rows(tiles)
+    half = count // 2
     even = slab % 2 == 0
-    a = from_a[...]
-    b = from_b[...]
-    nodes_ref[0:count] = free_ref[0:count] * (local_ref[0:count] + jnp.where(even, b, a))
     nodes_ref[count : 2 * count] = free_ref[count : 2 * count] * local_ref[count : 2 * count]
-    nodes_ref[2 * count :] = free_ref[2 * count :] * (local_ref[2 * count :] + jnp.where(even, a, b))
+
+    def body(i, _):
+        at = pl.multiple_of(i * 8, 8)
+        a = from_a[pl.ds(at, 8), :]
+        b = from_b[pl.ds(at, 8), :]
+        for start, packed in ((0, jnp.where(even, b, a)), (2 * count, jnp.where(even, a, b))):
+            for part, tile in enumerate(unpack_pair(packed)):
+                where = pl.ds(start + part * half + at, 8)
+                nodes_ref[where, :] = free_ref[where, :] * (local_ref[where, :] + tile)
+        return 0
+
+    lax.fori_loop(0, tiles // 2, body, 0, unroll=11)
 
 
 def filter_kernel(design_ref, da_ref, db_ref, strip_ref, sw_ref, factor_ref, density_ref, fine_ref, sum_ref):
@@ -385,7 +451,7 @@
     main_ref, shift_ref, shift32_ref, prev32_ref,
 ):
     tiles = main_ref.shape[1]
-    role, slab = where_am_i()
+    _, slab = where_am_i()
     gather_nodes(last_ref, from_a, from_b, free_ref, tiles, slab, nodes_ref)
     for s in range(2):
         prev32_ref[s] = shifted_tiles(prev_ref, tiles, s)
@@ -404,7 +470,7 @@
 ):
     tiles = main_ref.shape[1]
     count = plane_rows(tiles)
-    role, slab = where_am_i()
+    _, slab = where_am_i()
     gather_nodes(last_ref, from_a, from_b, free_ref, tiles, slab, nodes_ref)
     for s in range(2):
         s0_ref[s] = shifted_tiles(v0_ref, tiles, s)
@@ -432,7 +498,7 @@
     moment_ref, v0_ref, v1_ref, v2_ref, e00_ref, e01_ref, e11_ref, e02_ref, e12_ref, e22_ref, density_ref,
     grad_ref, u_ref, nodes_ref,
 ):
-    role, slab = where_am_i()
+    role, _ = where_am_i()
     parts, _, _, deep, fz = u_ref.shape
     half = fz // 2
     count = v0_ref.shape[0] // 3
@@ -490,7 +556,7 @@
 def last_kernel(grad_ref, ga_ref, gb_ref, sw_ref, out_ref, work_ref):
     planes, fy, fz = out_ref.shape
     width = 2 * fz
-    role, slab = where_am_i()
+    _, slab = where_am_i()
     even = slab % 2 == 0
     rows = grad_ref.shape[0]
     pool_y = jnp.where(iota((fy, rows), 0) // 4 == iota((fy, rows), 1), 1.0, 0.0).astype(BF16)
@@ -533,11 +599,17 @@
     pairs_b = [(i, i + 1 if i % 2 else i - 1) for i in range(1, slabs - 1)]
 
     def beside(to_a, to_b):
-        return lax.ppermute(to_a, LINE, pairs_a), lax.ppermute(to_b, LINE, pairs_b)
+        b = lax.ppermute(to_b, LINE, pairs_b)
+        a = lax.ppermute(to_a, LINE, pairs_a)
+        return a, b
 
     plane0, strips, corner = pl.pallas_call(
         strip_rows_kernel,
         out_shape=(shape(6 * by, fz), shape(6 * bx, LANES), shape(8, LANES)),
+        in_specs=[pl.BlockSpec(memory_space=pltpu.HBM)] * 2,
+        scratch_shapes=[
+            pltpu.VMEM(force.shape, F32), pltpu.VMEM(force.shape, jnp.int32), pltpu.SemaphoreType.DMA((2,)),
+        ],
         name="rows",
         compiler_params=KEEP,
     )(force, clamped_dof_mask)
@@ -565,7 +637,7 @@
     fine_strips = lax.ppermute(fine_strips, "role", [(0, 1), (1, 0)])
 
     node_set = shape(3 * count, LANES)
-    plane = shape(count, LANES)
+    plane = shape(count // 2, LANES)
     element = shape(columns, LANES)
     tile_scratch = [
         pltpu.VMEM((3, tiles, 16, LANES), BF16),
@@ -632,6 +704,7 @@
         P(None, "gx", "gy", "role"),
         P(),
     )
+
     return jax.shard_map(
         on_device,
         mesh=mesh,

time: 83.4 us -> 80.8 us (0.969)
  Pallas kernels: 13.9 us -> 17.2 us
  waiting for transfers between devices: 18.3 us -> 15.2 us
  blocking collectives: 12.4 us -> 11 us
  starting transfers between devices: 33.9 us -> 32.6 us
    ppermute x8, waiting for transfers between devices: 12.2 us -> 9.1 us  [the longest x4 9.09 us: beside(): b = lax.ppermute(to_b, LINE, pairs_b)]
    pallas_call x1, Pallas kernels: 1.15 us -> 2.63 us  [on_device(): pl.pallas_call(second_kernel, out_shape=(node_set, node_set, plane, plane...]
    all_to_all x1, blocking collectives: 12.4 us -> 11 us  [on_device(): moments = lax.all_to_all(moments, ('role', 'gx', 'gy'), 0, 0, tiled=True)]
    ppermute x8, starting transfers between devices: 18.3 us -> 16.9 us  [the longest x4 15.2 us: beside(): b = lax.ppermute(to_b, LINE, pairs_b)]
    pallas_call x1, Pallas kernels: 1.46 us -> 2.42 us  [on_device(): pl.pallas_call(third_kernel, out_shape=(node_set, element, element, eleme...]
  transfers between devices with their start and end apart: 14 -> 14, of which waited for: 7 -> 7; matrix products, arithmetic and copies ran while one was open for 1% -> 1% of each run, Pallas kernels for 9% -> 10%
where the time goes in v5:
time: 80.8 us; the launch traced here: 80.4 us
  starting transfers between devices  32.6 us (40%)
  Pallas kernels  17.2 us (21%)
  waiting for transfers between devices  15.2 us (19%)
  blocking collectives  11 us (14%)
  local copies, waits for them, and re-layouts  3.15 us (4%)
  between operations  0.86 us (1%)
    ppermute x4, starting transfers between devices, beside(): b = lax.ppermute(to_b, LINE, pairs_b)  15.2 us
    all_to_all x1, blocking collectives, on_device(): moments = lax.all_to_all(moments, ('role', 'gx', 'gy'), 0, 0, tiled=True)  11 us
    ppermute x4, waiting for transfers between devices, beside(): b = lax.ppermute(to_b, LINE, pairs_b)  9.09 us
    all_to_all x1, starting transfers between devices, on_device(): rf = lax.all_to_all(pack, 'gy', 0, 0)  5.45 us
    all_to_all x1, starting transfers between devices, on_device(): u = lax.all_to_all(u, 'gy', 0, 0)  5.07 us
    pallas_call x1, Pallas kernels, on_device(): pl.pallas_call(filter_kernel, out_shape=(shape(planes + 4, fy, 2 * fz), e...  3.85 us
    ppermute x1, waiting for transfers between devices, on_device(): next_plane = lax.ppermute(plane0, 'gx', [(i + 1, i) for i in range(gx - 1)])  2.74 us
    pallas_call x1, Pallas kernels, on_device(): pl.pallas_call(second_kernel, out_shape=(node_set, node_set, plane, plane...  2.63 us
  transfers between devices with their start and end apart: 14, of which 7 were waited for; matrix products, arithmetic and copies ran while one was open for 1% of the time, Pallas kernels for 10%

profile of v5, /device:TPU:3, one launch (start us, length us, event | category | flops | bytes accessed | tf_op | source)
XLA Modules:
  0.0 80.4 jit_solution(15716137550679479171)
XLA Ops:
  0.6 0.0 copy-start.1
  0.7 1.0 %copy-done.1 = f32[3,8,16,128]{3,2,1,0:T(8,128)S(1)} copy-done((f32[3,8,16,128]{3,2,1,0:T(8,128)S(1)}, f32[3,8,16,128]{3,2,1,0:T(8,128)}, u32[]{:S(2)}) %copy-start.1) | copy-done | bytes 196632
  1.6 0.9 %copy-done.3 = s32[3,8,16,128]{3,2,1,0:T(8,128)S(1)} copy-done((s32[3,8,16,128]{3,2,1,0:T(8,128)S(1)}, s32[3,8,16,128]{3,2,1,0:T(8,128)}, u32[]{:S(2)}) %copy-start.3) | copy-done | bytes 196632
  2.5 0.8 rows.1
  3.3 3.7 %collective-permute-start.4 = (f32[4,128,128]{2,1,0:T(8,128)S(1)}, f32[4,128,128]{2,1,0:T(8,128)S(1)}, u32[]{:S(2)}, u32[]{:S(2)}) collective-permute-start(f32[4,128,128]{2,1,0:T(8,128)S(1)} %copy-done), channel_id=1, source_target_pairs={{1,2},{2,1},{3,4},{4,3},{5,6},{6,5},{7,8},{8,7},{9,10},{10,9},{11,... | collective-permute-start | bytes 786440 | tf_op jit(solution)/shard_map/ppermute | solution.py:602
  7.1 0.1 collective-permute-start.3
  7.2 1.3 %collective-permute-start.2 = (f32[8,128]{1,0:T(8,128)S(1)}, f32[8,128]{1,0:T(8,128)S(1)}, u32[]{:S(2)}, u32[]{:S(2)}) collective-permute-start(f32[8,128]{1,0:T(8,128)S(1)} %get-tuple-element.38), channel_id=1, source_target_pairs={{20,0},{24,4},{28,8},{4,16},{8,20},{12,24},{21,1},{25,5},{29,9},{5... | collective-permute-start | bytes 12296 | tf_op jit(solution)/shard_map/ppermute | solution.py:619
  8.5 1.3 %collective-permute-start.1 = (f32[48,128]{1,0:T(8,128)S(1)}, f32[48,128]{1,0:T(8,128)S(1)}, u32[]{:S(2)}, u32[]{:S(2)}) collective-permute-start(f32[48,128]{1,0:T(8,128)S(1)} %get-tuple-element.37), channel_id=1, source_target_pairs={{0,16},{16,0},{1,17},{17,1},{2,18},{18,2},{3,19},{19,3},{4,20},{20... | collective-permute-start | bytes 73736 | tf_op jit(solution)/shard_map/ppermute | solution.py:618
  9.8 1.3 %collective-permute-start = (f32[96,128]{1,0:T(8,128)S(1)}, f32[96,128]{1,0:T(8,128)S(1)}, u32[]{:S(2)}, u32[]{:S(2)}) collective-permute-start(f32[96,128]{1,0:T(8,128)S(1)} %get-tuple-element.36), channel_id=1, source_target_pairs={{4,0},{8,4},{12,8},{5,1},{9,5},{13,9},{6,2},{10,6},{14,10},{7,3},{... | collective-permute-start | bytes 147464 | tf_op jit(solution)/shard_map/ppermute | solution.py:617
  11.1 0.0 copy-start.4
  11.1 0.0 copy-start.6
  11.1 0.1 slice_select_fusion.2
  11.2 0.0 copy-start.2
  11.2 0.0 copy-start.5
  11.2 0.1 copy.8
  11.3 1.1 %collective-permute-done.2.corner_ref = f32[8,128]{1,0:T(8,128)S(1)} collective-permute-done((f32[8,128]{1,0:T(8,128)S(1)}, f32[8,128]{1,0:T(8,128)S(1)}, u32[]{:S(2)}, u32[]{:S(2)}) %collective-permute-start.2) | collective-permute-done | bytes 4128 | tf_op jit(solution)/shard_map/ppermute | solution.py:619
  12.4 2.7 %collective-permute-done.plane_ref = f32[96,128]{1,0:T(8,128)S(1)} collective-permute-done((f32[96,128]{1,0:T(8,128)S(1)}, f32[96,128]{1,0:T(8,128)S(1)}, u32[]{:S(2)}, u32[]{:S(2)}) %collective-permute-start) | collective-permute-done | bytes 49184 | tf_op jit(solution)/shard_map/ppermute | solution.py:617
  15.2 1.5 %pack.1 = (f32[4,312,128]{2,1,0:T(8,128)}, bf16[240,240]{1,0:T(8,128)(2,1)S(1)}) custom-call(f32[3,8,16,128]{3,2,1,0:T(8,128)S(1)} %copy-done.2, s32[3,8,16,128]{3,2,1,0:T(8,128)S(1)} %copy-done.4, f32[96,128]{1,0:T(8,128)S(1)} %collective-permute-done.plane_ref, f32[48,128]{1,0:T(8,128)S(1)} %collective-permute-done.1.strip_ref, ...), custom_call_target="tpu_custom_call" | custom-call | tf_op jit(solution)/shard_map/pack/pallas_call | solution.py:623
  16.7 5.4 %all-to-all-start = ((f32[4,312,128]{2,1,0:T(8,128)}), f32[4,312,128]{2,1,0:T(8,128)S(1)}, u32[]{:S(2)}, u32[]{:S(2)}) async-start(f32[4,312,128]{2,1,0:T(8,128)} %get-tuple-element.39), calls=%async_computation | async-start | bytes 1277952 | tf_op jit(solution)/shard_map/all_to_all | solution.py:629
  22.1 0.0 collective-permute-done.4.db_ref
  22.1 0.1 slice_select_fusion
  22.3 0.1 copy.10
  22.4 0.1 slice_select_fusion.1
  22.5 0.1 copy.9
  22.6 1.3 %collective-permute-start.5 = (f32[1536,8]{0,1:T(8,128)S(1)}, f32[1536,8]{0,1:T(8,128)S(1)}, u32[]{:S(2)}, u32[]{:S(2)}) collective-permute-start(f32[1536,8]{0,1:T(8,128)S(1)} %pad_maximum_fusion), channel_id=1, source_target_pairs={{0,16},{16,0},{1,17},{17,1},{2,18},{18,2},{3,19},{19,3},{4,20},{20... | collective-permute-start | bytes 147464 | tf_op jit(solution)/shard_map/ppermute | solution.py:637
  23.9 2.0 %collective-permute-done.5 = f32[1536,8]{0,1:T(8,128)S(1)} collective-permute-done((f32[1536,8]{0,1:T(8,128)S(1)}, f32[1536,8]{0,1:T(8,128)S(1)}, u32[]{:S(2)}, u32[]{:S(2)}) %collective-permute-start.5) | collective-permute-done | bytes 49184 | tf_op jit(solution)/shard_map/ppermute | solution.py:637
  25.9 0.3 copy.11.strip_ref
  26.2 3.9 %filter.1 = (f32[8,128,256]{2,1,0:T(8,128)S(1)}, f32[32,128]{1,0:T(8,128)S(1)}, f32[32,128]{1,0:T(8,128)S(1)}) custom-call(f32[4,128,128]{2,1,0:T(8,128)S(1)} %copy-done, f32[4,128,128]{2,1,0:T(8,128)S(1)} %collective-permute-done.3.da_ref, f32[4,128,128]{2,1,0:T(8,128)S(1)} %collective-permute-done.4.db_ref, f32[1536,8]{1,0:T(8,128)S(1)} %copy.11.strip_ref), custom_call_target="tpu_custom_call" | custom-call | flops 30000000 | bytes 4000000 | tf_op jit(solution)/shard_map/filter/pallas_call | solution.py:648
  30.0 0.3 all-to-all-done.rf_ref
  30.3 2.2 %first.1 = (f32[1584,128]{1,0:T(8,128)S(1)}, f32[1584,128]{1,0:T(8,128)S(1)}, f32[1584,128]{1,0:T(8,128)S(1)}, f32[264,128]{1,0:T(8,128)S(1)}, f32[264,128]{1,0:T(8,128)S(1)}, /*index=5*/f32[32,128]{1,0:T(8,128)S(1)}) custom-call(f32[4,312,128]{2,1,0:T(8,128)S(1)} %all-to-all-done.rf_ref, f32[32,128]{1,0:T(8,128)S(1)} %get-tuple-element.41.factor_ref, ...), custom_call_target="tpu_custom_call" | custom-call | tf_op jit(solution)/shard_map/first/pallas_call | solution.py:656
  32.5 1.0 %collective-permute-start.6 = (f32[264,128]{1,0:T(8,128)S(1)}, f32[264,128]{1,0:T(8,128)S(1)}, u32[]{:S(2)}, u32[]{:S(2)}) collective-permute-start(f32[264,128]{1,0:T(8,128)S(1)} %get-tuple-element.46), channel_id=1, source_target_pairs={{0,1},{1,0},{2,3},{3,2},{4,5},{5,4},{6,7},{7,6},{8,9},{9,8},{10,11... | collective-permute-start | bytes 405512 | tf_op jit(solution)/shard_map/ppermute | solution.py:603
  33.5 4.3 %collective-permute-start.7 = (f32[264,128]{1,0:T(8,128)S(1)}, f32[264,128]{1,0:T(8,128)S(1)}, u32[]{:S(2)}, u32[]{:S(2)}) collective-permute-start(f32[264,128]{1,0:T(8,128)S(1)} %get-tuple-element.47), channel_id=1, source_target_pairs={{1,2},{2,1},{3,4},{4,3},{5,6},{6,5},{7,8},{8,7},{9,10},{10,9},{11,... | collective-permute-start | bytes 405512 | tf_op jit(solution)/shard_map/ppermute | solution.py:602
  37.8 2.9 %collective-permute-done.7.from_b = f32[264,128]{1,0:T(8,128)S(1)} collective-permute-done((f32[264,128]{1,0:T(8,128)S(1)}, f32[264,128]{1,0:T(8,128)S(1)}, u32[]{:S(2)}, u32[]{:S(2)}) %collective-permute-start.7) | collective-permute-done | bytes 135200 | tf_op jit(solution)/shard_map/ppermute | solution.py:602
  40.8 2.6 %second.1 = (f32[1584,128]{1,0:T(8,128)S(1)}, f32[1584,128]{1,0:T(8,128)S(1)}, f32[264,128]{1,0:T(8,128)S(1)}, f32[264,128]{1,0:T(8,128)S(1)}, f32[32,128]{1,0:T(8,128)S(1)}, /*index=5*/f32[32,128]{1,0:T(8,128)S(1)}) custom-call(f32[1584,128]{1,0:T(8,128)S(1)} %get-tuple-element.43.prev_ref.v0_ref, f32[1584,128]{1,0:T(8,128)S(1)} %get-tuple-element.44.free_ref, ...), custom_call_target="tpu_custom_call" | custom-call | tf_op jit(solution)/shard_map/second/pallas_call | solution.py:664
  43.4 0.1 collective-permute-start.8
  43.5 5.3 %collective-permute-start.9 = (f32[264,128]{1,0:T(8,128)S(1)}, f32[264,128]{1,0:T(8,128)S(1)}, u32[]{:S(2)}, u32[]{:S(2)}) collective-permute-start(f32[264,128]{1,0:T(8,128)S(1)} %get-tuple-element.51), channel_id=1, source_target_pairs={{1,2},{2,1},{3,4},{4,3},{5,6},{6,5},{7,8},{8,7},{9,10},{10,9},{11,... | collective-permute-start | bytes 405512 | tf_op jit(solution)/shard_map/ppermute | solution.py:602
  48.8 0.0 collective-permute-done.8.from_a
  48.8 2.7 %collective-permute-done.9.from_b = f32[264,128]{1,0:T(8,128)S(1)} collective-permute-done((f32[264,128]{1,0:T(8,128)S(1)}, f32[264,128]{1,0:T(8,128)S(1)}, u32[]{:S(2)}, u32[]{:S(2)}) %collective-permute-start.9) | collective-permute-done | bytes 135200 | tf_op jit(solution)/shard_map/ppermute | solution.py:602
  51.4 2.4 %third.1 = (f32[1584,128]{1,0:T(8,128)S(1)}, f32[32,128]{1,0:T(8,128)S(1)}, f32[32,128]{1,0:T(8,128)S(1)}, f32[32,128]{1,0:T(8,128)S(1)}, f32[32,128]{1,0:T(8,128)S(1)}) custom-call(f32[1584,128]{1,0:T(8,128)S(1)} %get-tuple-element.43.prev_ref.v0_ref, f32[1584,128]{1,0:T(8,128)S(1)} %get-tuple-element.48.v1_ref, ...), custom_call_target="tpu_custom_call" | custom-call | tf_op jit(solution)/shard_map/third/pallas_call | solution.py:672
  53.9 11.0 %all_to_all.21 = f32[32,1,128]{2,1,0:T(1,128)S(1)} all-to-all(f32[32,1,128]{2,1,0:T(1,128)S(1)} %bitcast.10), channel_id=1, replica_groups=mesh['role'=2,'gx'=4,'gy'=4] {'role','gx','gy'}, dimensions={0} | all-to-all | bytes 32768 | tf_op jit(solution)/shard_map/all_to_all | solution.py:679
  64.8 1.3 %combine.1 = (f32[32,128]{1,0:T(8,128)S(1)}, f32[4,3,2,16,128]{4,3,2,1,0:T(8,128)}) custom-call(f32[32,128]{1,0:T(8,128)S(1)} %bitcast.9, f32[1584,128]{1,0:T(8,128)S(1)} %get-tuple-element.43.prev_ref.v0_ref, f32[1584,128]{1,0:T(8,128)S(1)} %get-tuple-element.48.v1_ref, f32[1584,128]{1,0:T(8,128)S(1)} %get-tuple-element.56.v2_ref, ...), custom_call_target="tpu_custom_call" | custom-call | tf_op jit(solution)/shard_map/combine/pallas_call | solution.py:680
  66.2 5.1 %all-to-all-start.2 = ((f32[4,3,2,16,128]{4,3,2,1,0:T(8,128)}), f32[4,3,2,16,128]{4,3,2,1,0:T(8,128)S(1)}, u32[]{:S(2)}, u32[]{:S(2)}) async-start(f32[4,3,2,16,128]{4,3,2,1,0:T(8,128)} %get-tuple-element.63), calls=%async_computation.2 | async-start | bytes 393216 | tf_op jit(solution)/shard_map/all_to_all | solution.py:695
  71.3 1.9 %collective-permute-start.11 = (f32[32,128]{1,0:T(8,128)S(1)}, f32[32,128]{1,0:T(8,128)S(1)}, u32[]{:S(2)}, u32[]{:S(2)}) collective-permute-start(f32[32,128]{1,0:T(8,128)S(1)} %get-tuple-element.61.grad_ref), channel_id=1, source_target_pairs={{1,2},{2,1},{3,4},{4,3},{5,6},{6,5},{7,8},{8,7},{9,10},{10,9},{11,... | collective-permute-start | bytes 49160 | tf_op jit(solution)/shard_map/ppermute | solution.py:602
  73.2 0.6 collective-permute-start.10
  73.7 3.5 %collective-permute-done.11.gb_ref = f32[32,128]{1,0:T(8,128)S(1)} collective-permute-done((f32[32,128]{1,0:T(8,128)S(1)}, f32[32,128]{1,0:T(8,128)S(1)}, u32[]{:S(2)}, u32[]{:S(2)}) %collective-permute-start.11) | collective-permute-done | bytes 16416 | tf_op jit(solution)/shard_map/ppermute | solution.py:602
  77.2 2.5 %last.1 = f32[4,128,128]{2,1,0:T(8,128)} custom-call(f32[32,128]{1,0:T(8,128)S(1)} %get-tuple-element.61.grad_ref, f32[32,128]{1,0:T(8,128)S(1)} %collective-permute-done.10.ga_ref, f32[32,128]{1,0:T(8,128)S(1)} %collective-permute-done.11.gb_ref, f32[8,128,256]{2,1,0:T(8,128)S(1)} %get-tuple-element.62.sw_ref), custom_call_target="tpu_custom_call" | custom-call | tf_op jit(solution)/shard_map/last/pallas_call | solution.py:688
  79.7 0.0 all-to-all-done.2
  79.7 0.7 copy.13
  (12 shorter events, 0.0 us)
Async XLA Ops:
  0.6 2.7 %copy-start = (f32[4,128,128]{2,1,0:T(8,128)S(1)}, f32[4,128,128]{2,1,0:T(8,128)}, u32[]{:S(2)}) copy-start(f32[4,128,128]{2,1,0:T(8,128)} %design_ref) | copy-start | bytes 786436
  0.6 1.0 %copy-start.1 = (f32[3,8,16,128]{3,2,1,0:T(8,128)S(1)}, f32[3,8,16,128]{3,2,1,0:T(8,128)}, u32[]{:S(2)}) copy-start(f32[3,8,16,128]{3,2,1,0:T(8,128)} %force_ref.1) | copy-start | bytes 589828
  1.6 0.9 %copy-start.3 = (s32[3,8,16,128]{3,2,1,0:T(8,128)S(1)}, s32[3,8,16,128]{3,2,1,0:T(8,128)}, u32[]{:S(2)}) copy-start(s32[3,8,16,128]{3,2,1,0:T(8,128)} %mask_ref.1) | copy-start | bytes 589828
  3.3 18.8 %collective-permute-start.4 = (f32[4,128,128]{2,1,0:T(8,128)S(1)}, f32[4,128,128]{2,1,0:T(8,128)S(1)}, u32[]{:S(2)}, u32[]{:S(2)}) collective-permute-start(f32[4,128,128]{2,1,0:T(8,128)S(1)} %copy-done), channel_id=1, source_target_pairs={{1,2},{2,1},{3,4},{4,3},{5,6},{6,5},{7,8},{8,7},{9,10},{10,9},{11,... | collective-permute-start | bytes 786440 | tf_op jit(solution)/shard_map/ppermute | solution.py:602
  7.1 15.3 %collective-permute-start.3 = (f32[4,128,128]{2,1,0:T(8,128)S(1)}, f32[4,128,128]{2,1,0:T(8,128)S(1)}, u32[]{:S(2)}, u32[]{:S(2)}) collective-permute-start(f32[4,128,128]{2,1,0:T(8,128)S(1)} %copy-done), channel_id=1, source_target_pairs={{0,1},{1,0},{2,3},{3,2},{4,5},{5,4},{6,7},{7,6},{8,9},{9,8},{10,11... | collective-permute-start | bytes 786440 | tf_op jit(solution)/shard_map/ppermute | solution.py:603
  7.2 5.3 %collective-permute-start.2 = (f32[8,128]{1,0:T(8,128)S(1)}, f32[8,128]{1,0:T(8,128)S(1)}, u32[]{:S(2)}, u32[]{:S(2)}) collective-permute-start(f32[8,128]{1,0:T(8,128)S(1)} %get-tuple-element.38), channel_id=1, source_target_pairs={{20,0},{24,4},{28,8},{4,16},{8,20},{12,24},{21,1},{25,5},{29,9},{5... | collective-permute-start | bytes 12296 | tf_op jit(solution)/shard_map/ppermute | solution.py:619
  8.5 4.0 %collective-permute-start.1 = (f32[48,128]{1,0:T(8,128)S(1)}, f32[48,128]{1,0:T(8,128)S(1)}, u32[]{:S(2)}, u32[]{:S(2)}) collective-permute-start(f32[48,128]{1,0:T(8,128)S(1)} %get-tuple-element.37), channel_id=1, source_target_pairs={{0,16},{16,0},{1,17},{17,1},{2,18},{18,2},{3,19},{19,3},{4,20},{20... | collective-permute-start | bytes 73736 | tf_op jit(solution)/shard_map/ppermute | solution.py:618
  9.8 5.4 %collective-permute-start = (f32[96,128]{1,0:T(8,128)S(1)}, f32[96,128]{1,0:T(8,128)S(1)}, u32[]{:S(2)}, u32[]{:S(2)}) collective-permute-start(f32[96,128]{1,0:T(8,128)S(1)} %get-tuple-element.36), channel_id=1, source_target_pairs={{4,0},{8,4},{12,8},{5,1},{9,5},{13,9},{6,2},{10,6},{14,10},{7,3},{... | collective-permute-start | bytes 147464 | tf_op jit(solution)/shard_map/ppermute | solution.py:617
  11.1 4.1 %copy-start.4 = (s32[3,8,16,128]{3,2,1,0:T(8,128)S(1)}, s32[3,8,16,128]{3,2,1,0:T(8,128)}, u32[]{:S(2)}) copy-start(s32[3,8,16,128]{3,2,1,0:T(8,128)} %mask_ref.1) | copy-start | bytes 589828
  11.1 4.1 %copy-start.6 = (f32[81,81]{1,0:T(8,128)S(1)}, f32[81,81]{1,0:T(8,128)}, u32[]{:S(2)}) copy-start(f32[81,81]{1,0:T(8,128)} %stiff_ref.1) | copy-start | bytes 78736
  11.2 3.9 %copy-start.2 = (f32[3,8,16,128]{3,2,1,0:T(8,128)S(1)}, f32[3,8,16,128]{3,2,1,0:T(8,128)}, u32[]{:S(2)}) copy-start(f32[3,8,16,128]{3,2,1,0:T(8,128)} %force_ref.1) | copy-start | bytes 589828
  11.2 3.9 %copy-start.5 = (f32[120,81]{1,0:T(8,128)S(1)}, f32[120,81]{1,0:T(8,128)}, u32[]{:S(2)}) copy-start(f32[120,81]{1,0:T(8,128)} %constant.10.clone.place_ref) | copy-start | bytes 116644
  16.7 13.6 %all-to-all-start = ((f32[4,312,128]{2,1,0:T(8,128)}), f32[4,312,128]{2,1,0:T(8,128)S(1)}, u32[]{:S(2)}, u32[]{:S(2)}) async-start(f32[4,312,128]{2,1,0:T(8,128)} %get-tuple-element.39), calls=%async_computation | async-start | bytes 1277952 | tf_op jit(solution)/shard_map/all_to_all | solution.py:629
  22.6 3.3 %collective-permute-start.5 = (f32[1536,8]{0,1:T(8,128)S(1)}, f32[1536,8]{0,1:T(8,128)S(1)}, u32[]{:S(2)}, u32[]{:S(2)}) collective-permute-start(f32[1536,8]{0,1:T(8,128)S(1)} %pad_maximum_fusion), channel_id=1, source_target_pairs={{0,16},{16,0},{1,17},{17,1},{2,18},{18,2},{3,19},{19,3},{4,20},{20... | collective-permute-start | bytes 147464 | tf_op jit(solution)/shard_map/ppermute | solution.py:637
  32.5 5.3 %collective-permute-start.6 = (f32[264,128]{1,0:T(8,128)S(1)}, f32[264,128]{1,0:T(8,128)S(1)}, u32[]{:S(2)}, u32[]{:S(2)}) collective-permute-start(f32[264,128]{1,0:T(8,128)S(1)} %get-tuple-element.46), channel_id=1, source_target_pairs={{0,1},{1,0},{2,3},{3,2},{4,5},{5,4},{6,7},{7,6},{8,9},{9,8},{10,11... | collective-permute-start | bytes 405512 | tf_op jit(solution)/shard_map/ppermute | solution.py:603
  33.5 7.2 %collective-permute-start.7 = (f32[264,128]{1,0:T(8,128)S(1)}, f32[264,128]{1,0:T(8,128)S(1)}, u32[]{:S(2)}, u32[]{:S(2)}) collective-permute-start(f32[264,128]{1,0:T(8,128)S(1)} %get-tuple-element.47), channel_id=1, source_target_pairs={{1,2},{2,1},{3,4},{4,3},{5,6},{6,5},{7,8},{8,7},{9,10},{10,9},{11,... | collective-permute-start | bytes 405512 | tf_op jit(solution)/shard_map/ppermute | solution.py:602
  43.4 5.4 %collective-permute-start.8 = (f32[264,128]{1,0:T(8,128)S(1)}, f32[264,128]{1,0:T(8,128)S(1)}, u32[]{:S(2)}, u32[]{:S(2)}) collective-permute-start(f32[264,128]{1,0:T(8,128)S(1)} %get-tuple-element.50), channel_id=1, source_target_pairs={{0,1},{1,0},{2,3},{3,2},{4,5},{5,4},{6,7},{7,6},{8,9},{9,8},{10,11... | collective-permute-start | bytes 405512 | tf_op jit(solution)/shard_map/ppermute | solution.py:603
  43.5 8.0 %collective-permute-start.9 = (f32[264,128]{1,0:T(8,128)S(1)}, f32[264,128]{1,0:T(8,128)S(1)}, u32[]{:S(2)}, u32[]{:S(2)}) collective-permute-start(f32[264,128]{1,0:T(8,128)S(1)} %get-tuple-element.51), channel_id=1, source_target_pairs={{1,2},{2,1},{3,4},{4,3},{5,6},{6,5},{7,8},{8,7},{9,10},{10,9},{11,... | collective-permute-start | bytes 405512 | tf_op jit(solution)/shard_map/ppermute | solution.py:602
  66.2 13.5 %all-to-all-start.2 = ((f32[4,3,2,16,128]{4,3,2,1,0:T(8,128)}), f32[4,3,2,16,128]{4,3,2,1,0:T(8,128)S(1)}, u32[]{:S(2)}, u32[]{:S(2)}) async-start(f32[4,3,2,16,128]{4,3,2,1,0:T(8,128)} %get-tuple-element.63), calls=%async_computation.2 | async-start | bytes 393216 | tf_op jit(solution)/shard_map/all_to_all | solution.py:695
  71.3 5.9 %collective-permute-start.11 = (f32[32,128]{1,0:T(8,128)S(1)}, f32[32,128]{1,0:T(8,128)S(1)}, u32[]{:S(2)}, u32[]{:S(2)}) collective-permute-start(f32[32,128]{1,0:T(8,128)S(1)} %get-tuple-element.61.grad_ref), channel_id=1, source_target_pairs={{1,2},{2,1},{3,4},{4,3},{5,6},{6,5},{7,8},{8,7},{9,10},{10,9},{11,... | collective-permute-start | bytes 49160 | tf_op jit(solution)/shard_map/ppermute | solution.py:602
  73.2 4.0 %collective-permute-start.10 = (f32[32,128]{1,0:T(8,128)S(1)}, f32[32,128]{1,0:T(8,128)S(1)}, u32[]{:S(2)}, u32[]{:S(2)}) collective-permute-start(f32[32,128]{1,0:T(8,128)S(1)} %get-tuple-element.61.grad_ref), channel_id=1, source_target_pairs={{0,1},{1,0},{2,3},{3,2},{4,5},{5,4},{6,7},{7,6},{8,9},{9,8},{10,11... | collective-permute-start | bytes 49160 | tf_op jit(solution)/shard_map/ppermute | solution.py:603

commit v6 on v5

--- a/solution.py
+++ b/solution.py
@@ -128,7 +128,7 @@
             corner_ref[row : row + 1] = x[0:1]
 
 
-def pack_kernel(force_ref, mask_ref, plane_ref, strip_ref, corner_ref, stiff_ref, place_ref, pack_ref, table_ref):
+def pack_kernel(force_ref, mask_ref, plane_ref, strip_ref, corner_ref, pack_ref):
     _, bx, by, _ = force_ref.shape
     parts = pack_ref.shape[0]
     tail = 18 * by
@@ -146,6 +146,9 @@
                     pack_ref[j, at * by : (at + 1) * by] = val[x] if inner else plane_ref[row * by : (row + 1) * by]
                     edge = strip_ref[row * bx + x : row * bx + x + 1] if inner else corner_ref[row : row + 1]
                     pack_ref[j, tail + at : tail + at + 1] = edge
+
+
+def table_kernel(stiff_ref, place_ref, table_ref):
     place = place_ref[...]
     half_way = jnp.dot(place, stiff_ref[...], precision=lax.Precision.HIGHEST, preferred_element_type=F32)
     spread = lax.dot_general(
@@ -291,16 +294,15 @@
     own_even = (lane < half) & (row < 3)
     live = (row & 3) < 3
     own_odd = (lane < half) & (row >= 4) & live
-    rim = (lane // 4 == half // 4) | (lane // 4 == LANES // 4 - 1)
+    rim = live & ((lane // 4 == half // 4) | (lane // 4 == LANES // 4 - 1))
     swapped = pltpu.roll(x, half, 1)
     first = jnp.where(own_even, x, jnp.where(own_odd, pltpu.roll(swapped, 4, 0), 0.0))
     second = jnp.where(own_even, pltpu.roll(x, 4, 0), jnp.where(own_odd, swapped, 0.0))
     edge = jnp.broadcast_to(x[3:4], (8, LANES))
     out = []
     for tile, start in ((first, 0), (second, 28)):
-        for r in (0, 1, 2, 4, 5, 6):
-            tile = jnp.where(rim & (row == r), pltpu.roll(edge, (half - start - 4 * r) % LANES, 1), tile)
-        out.append(tile)
+        moved = jnp.take_along_axis(edge, (lane - half + start + 4 * row) & (LANES - 1), axis=1)
+        out.append(jnp.where(rim, moved, tile))
     return out
 
 
@@ -572,10 +574,10 @@
 
     def body(p, _):
         x = work_ref[p] + work_ref[p + 4] + 2.0 * (work_ref[p + 1] + work_ref[p + 3]) + 3.0 * work_ref[p + 2]
-        out_ref[p] = smooth_y(smooth_z(x))[:, :fz]
+        out_ref[p] = smooth_y(smooth_z(x)[:, :fz])
         return 0
 
-    lax.fori_loop(0, planes, body, 0)
+    lax.fori_loop(0, planes, body, 0, unroll=True)
 
 
 def shape(*dims, dtype=F32):
@@ -612,7 +614,7 @@
         ],
         name="rows",
         compiler_params=KEEP,
-    )(force, clamped_dof_mask)
+    )(pltpu.with_memory_space_constraint(force, pltpu.HBM), pltpu.with_memory_space_constraint(clamped_dof_mask, pltpu.HBM))
     plane0, strips, corner, design = lax.optimization_barrier((plane0, strips, corner, design))
     next_plane = lax.ppermute(plane0, "gx", [(i + 1, i) for i in range(gx - 1)])
     strips = lax.ppermute(strips, "role", [(0, 1), (1, 0)])
@@ -620,12 +622,18 @@
         corner, ("role", "gx"), [((1 - r) * gx + i + 1, r * gx + i) for r in range(2) for i in range(gx - 1)]
     )
     design_a, design_b = beside(design, design)
-    pack, table = pl.pallas_call(
+    pack = pl.pallas_call(
         pack_kernel,
-        out_shape=(shape(gy, 18 * by + 24, fz), shape(2 * ROWS, 2 * ROWS, dtype=BF16)),
+        out_shape=shape(gy, 18 * by + 24, fz),
         name="pack",
         compiler_params=KEEP,
-    )(force, clamped_dof_mask, next_plane, strips, corner, stiffness, jnp.asarray(place_table()))
+    )(force, clamped_dof_mask, next_plane, strips, corner)
+    table = pl.pallas_call(
+        table_kernel,
+        out_shape=shape(2 * ROWS, 2 * ROWS, dtype=BF16),
+        name="table",
+        compiler_params=KEEP,
+    )(stiffness, jnp.asarray(place_table()))
     rf = lax.all_to_all(pack, "gy", 0, 0)
 
     role = lax.axis_index("role")

time: 80.8 us -> 77.3 us (0.957)
  local copies, waits for them, and re-layouts: 3.15 us -> 1.25 us
  Pallas kernels: 17.2 us -> 16.3 us
    unnamed x14 -> x10, local copies, waits for them, and re-layouts: 1.92 us -> 0.03 us
    pallas_call x1 -> x2, Pallas kernels: 1.5 us -> 1.64 us  [the longest x1 0.91 us: on_device(): pl.pallas_call(pack_kernel, out_shape=shape(gy, 18 * by + 24, fz), name='...]
where the time goes in v6:
time: 77.3 us; the launch traced here: 76.9 us
  starting transfers between devices  32.6 us (42%)
  Pallas kernels  16.3 us (21%)
  waiting for transfers between devices  14.5 us (19%)
  blocking collectives  11 us (14%)
  local copies, waits for them, and re-layouts  1.25 us (2%)
  between operations  0.84 us (1%)
    ppermute x4, starting transfers between devices, beside(): b = lax.ppermute(to_b, LINE, pairs_b)  15.1 us
    all_to_all x1, blocking collectives, on_device(): moments = lax.all_to_all(moments, ('role', 'gx', 'gy'), 0, 0, tiled=True)  11 us
    ppermute x4, waiting for transfers between devices, beside(): b = lax.ppermute(to_b, LINE, pairs_b)  9.11 us
    all_to_all x1, starting transfers between devices, on_device(): rf = lax.all_to_all(pack, 'gy', 0, 0)  5.45 us
    all_to_all x1, starting transfers between devices, on_device(): u = lax.all_to_all(u, 'gy', 0, 0)  5.07 us
    pallas_call x1, Pallas kernels, on_device(): pl.pallas_call(filter_kernel, out_shape=(shape(planes + 4, fy, 2 * fz), e...  3.85 us
    ppermute x1, waiting for transfers between devices, on_device(): next_plane = lax.ppermute(plane0, 'gx', [(i + 1, i) for i in range(gx - 1)])  2.74 us
    pallas_call x1, Pallas kernels, on_device(): pl.pallas_call(first_kernel, out_shape=(node_set, node_set, node_set, pla...  2.19 us
  transfers between devices with their start and end apart: 14, of which 7 were waited for; matrix products, arithmetic and copies ran while one was open for 1% of the time, Pallas kernels for 10%

profile of v6, /device:TPU:3, one launch (start us, length us, event | category | flops | bytes accessed | tf_op | source)
XLA Modules:
  0.0 76.9 jit_solution(17184588231951233384)
XLA Ops:
  0.6 1.4 %rows.1 = (f32[96,128]{1,0:T(8,128)S(1)}, f32[48,128]{1,0:T(8,128)S(1)}, f32[8,128]{1,0:T(8,128)S(1)}) custom-call(f32[3,8,16,128]{3,2,1,0:T(8,128)} %force_ref.1, s32[3,8,16,128]{3,2,1,0:T(8,128)} %mask_ref.1), custom_call_target="tpu_custom_call" | custom-call | tf_op jit(solution)/shard_map/rows/pallas_call | solution.py:608
  2.0 3.7 %collective-permute-start.4 = (f32[4,128,128]{2,1,0:T(8,128)S(1)}, f32[4,128,128]{2,1,0:T(8,128)S(1)}, u32[]{:S(2)}, u32[]{:S(2)}) collective-permute-start(f32[4,128,128]{2,1,0:T(8,128)S(1)} %copy-done), channel_id=1, source_target_pairs={{1,2},{2,1},{3,4},{4,3},{5,6},{6,5},{7,8},{8,7},{9,10},{10,9},{11,... | collective-permute-start | bytes 786440 | tf_op jit(solution)/shard_map/ppermute | solution.py:604
  5.8 0.1 collective-permute-start.3
  5.8 1.3 %collective-permute-start.2 = (f32[8,128]{1,0:T(8,128)S(1)}, f32[8,128]{1,0:T(8,128)S(1)}, u32[]{:S(2)}, u32[]{:S(2)}) collective-permute-start(f32[8,128]{1,0:T(8,128)S(1)} %get-tuple-element.36), channel_id=1, source_target_pairs={{20,0},{24,4},{28,8},{4,16},{8,20},{12,24},{21,1},{25,5},{29,9},{5... | collective-permute-start | bytes 12296 | tf_op jit(solution)/shard_map/ppermute | solution.py:621
  7.1 1.3 %collective-permute-start.1 = (f32[48,128]{1,0:T(8,128)S(1)}, f32[48,128]{1,0:T(8,128)S(1)}, u32[]{:S(2)}, u32[]{:S(2)}) collective-permute-start(f32[48,128]{1,0:T(8,128)S(1)} %get-tuple-element.35), channel_id=1, source_target_pairs={{0,16},{16,0},{1,17},{17,1},{2,18},{18,2},{3,19},{19,3},{4,20},{20... | collective-permute-start | bytes 73736 | tf_op jit(solution)/shard_map/ppermute | solution.py:620
  8.5 1.3 %collective-permute-start = (f32[96,128]{1,0:T(8,128)S(1)}, f32[96,128]{1,0:T(8,128)S(1)}, u32[]{:S(2)}, u32[]{:S(2)}) collective-permute-start(f32[96,128]{1,0:T(8,128)S(1)} %get-tuple-element.34), channel_id=1, source_target_pairs={{4,0},{8,4},{12,8},{5,1},{9,5},{13,9},{6,2},{10,6},{14,10},{7,3},{... | collective-permute-start | bytes 147464 | tf_op jit(solution)/shard_map/ppermute | solution.py:619
  9.7 0.0 copy-start.2
  9.8 0.1 slice_select_fusion.2
  9.9 0.0 copy-start.1
  9.9 0.1 copy.8
  10.0 1.1 %collective-permute-done.2.corner_ref = f32[8,128]{1,0:T(8,128)S(1)} collective-permute-done((f32[8,128]{1,0:T(8,128)S(1)}, f32[8,128]{1,0:T(8,128)S(1)}, u32[]{:S(2)}, u32[]{:S(2)}) %collective-permute-start.2) | collective-permute-done | bytes 4128 | tf_op jit(solution)/shard_map/ppermute | solution.py:621
  11.1 0.0 collective-permute-done.1.strip_ref
  11.1 2.7 %collective-permute-done.plane_ref = f32[96,128]{1,0:T(8,128)S(1)} collective-permute-done((f32[96,128]{1,0:T(8,128)S(1)}, f32[96,128]{1,0:T(8,128)S(1)}, u32[]{:S(2)}, u32[]{:S(2)}) %collective-permute-start) | collective-permute-done | bytes 49184 | tf_op jit(solution)/shard_map/ppermute | solution.py:619
  13.9 0.9 %pack.1 = f32[4,312,128]{2,1,0:T(8,128)} custom-call(f32[3,8,16,128]{3,2,1,0:T(8,128)S(1)} %copy-done.1, s32[3,8,16,128]{3,2,1,0:T(8,128)S(1)} %copy-done.2, f32[96,128]{1,0:T(8,128)S(1)} %collective-permute-done.plane_ref, f32[48,128]{1,0:T(8,128)S(1)} %collective-permute-done.1.strip_ref, f32[8,128]{1,0:T(8,128)S(1)} %collective-permute-done.2.corner_ref), custom_call_target="tpu_custom_call" | custom-call | tf_op jit(solution)/shard_map/pack/pallas_call | solution.py:625
  14.8 5.5 %all-to-all-start = ((f32[4,312,128]{2,1,0:T(8,128)}), f32[4,312,128]{2,1,0:T(8,128)S(1)}, u32[]{:S(2)}, u32[]{:S(2)}) async-start(f32[4,312,128]{2,1,0:T(8,128)} %pack.1), calls=%async_computation | async-start | bytes 1277952 | tf_op jit(solution)/shard_map/all_to_all | solution.py:637
  20.2 0.0 collective-permute-done.4.db_ref
  20.2 0.1 slice_select_fusion
  20.4 0.1 copy.10
  20.5 0.0 collective-permute-done.3.da_ref
  20.5 0.1 slice_select_fusion.1
  20.6 0.0 copy-start.4
  20.6 0.1 copy.9
  20.7 1.3 %collective-permute-start.5 = (f32[1536,8]{0,1:T(8,128)S(1)}, f32[1536,8]{0,1:T(8,128)S(1)}, u32[]{:S(2)}, u32[]{:S(2)}) collective-permute-start(f32[1536,8]{0,1:T(8,128)S(1)} %pad_maximum_fusion), channel_id=1, source_target_pairs={{0,16},{16,0},{1,17},{17,1},{2,18},{18,2},{3,19},{19,3},{4,20},{20... | collective-permute-start | bytes 147464 | tf_op jit(solution)/shard_map/ppermute | solution.py:645
  22.0 0.7 table.1.table_ref
  22.8 1.3 %collective-permute-done.5 = f32[1536,8]{0,1:T(8,128)S(1)} collective-permute-done((f32[1536,8]{0,1:T(8,128)S(1)}, f32[1536,8]{0,1:T(8,128)S(1)}, u32[]{:S(2)}, u32[]{:S(2)}) %collective-permute-start.5) | collective-permute-done | bytes 49184 | tf_op jit(solution)/shard_map/ppermute | solution.py:645
  24.0 0.3 copy.11.strip_ref
  24.3 3.9 %filter.1 = (f32[8,128,256]{2,1,0:T(8,128)S(1)}, f32[32,128]{1,0:T(8,128)S(1)}, f32[32,128]{1,0:T(8,128)S(1)}) custom-call(f32[4,128,128]{2,1,0:T(8,128)S(1)} %copy-done, f32[4,128,128]{2,1,0:T(8,128)S(1)} %collective-permute-done.3.da_ref, f32[4,128,128]{2,1,0:T(8,128)S(1)} %collective-permute-done.4.db_ref, f32[1536,8]{1,0:T(8,128)S(1)} %copy.11.strip_ref), custom_call_target="tpu_custom_call" | custom-call | flops 30000000 | bytes 4000000 | tf_op jit(solution)/shard_map/filter/pallas_call | solution.py:656
  28.1 0.3 all-to-all-done.rf_ref
  28.4 2.2 %first.1 = (f32[1584,128]{1,0:T(8,128)S(1)}, f32[1584,128]{1,0:T(8,128)S(1)}, f32[1584,128]{1,0:T(8,128)S(1)}, f32[264,128]{1,0:T(8,128)S(1)}, f32[264,128]{1,0:T(8,128)S(1)}, /*index=5*/f32[32,128]{1,0:T(8,128)S(1)}) custom-call(f32[4,312,128]{2,1,0:T(8,128)S(1)} %all-to-all-done.rf_ref, f32[32,128]{1,0:T(8,128)S(1)} %get-tuple-element.38.factor_ref, ...), custom_call_target="tpu_custom_call" | custom-call | tf_op jit(solution)/shard_map/first/pallas_call | solution.py:664
  30.6 1.1 %collective-permute-start.6 = (f32[264,128]{1,0:T(8,128)S(1)}, f32[264,128]{1,0:T(8,128)S(1)}, u32[]{:S(2)}, u32[]{:S(2)}) collective-permute-start(f32[264,128]{1,0:T(8,128)S(1)} %get-tuple-element.42), channel_id=1, source_target_pairs={{0,1},{1,0},{2,3},{3,2},{4,5},{5,4},{6,7},{7,6},{8,9},{9,8},{10,11... | collective-permute-start | bytes 405512 | tf_op jit(solution)/shard_map/ppermute | solution.py:605
  31.7 4.2 %collective-permute-start.7 = (f32[264,128]{1,0:T(8,128)S(1)}, f32[264,128]{1,0:T(8,128)S(1)}, u32[]{:S(2)}, u32[]{:S(2)}) collective-permute-start(f32[264,128]{1,0:T(8,128)S(1)} %get-tuple-element.43), channel_id=1, source_target_pairs={{1,2},{2,1},{3,4},{4,3},{5,6},{6,5},{7,8},{8,7},{9,10},{10,9},{11,... | collective-permute-start | bytes 405512 | tf_op jit(solution)/shard_map/ppermute | solution.py:604
  35.9 0.0 collective-permute-done.6.from_a
  35.9 3.0 %collective-permute-done.7.from_b = f32[264,128]{1,0:T(8,128)S(1)} collective-permute-done((f32[264,128]{1,0:T(8,128)S(1)}, f32[264,128]{1,0:T(8,128)S(1)}, u32[]{:S(2)}, u32[]{:S(2)}) %collective-permute-start.7) | collective-permute-done | bytes 135200 | tf_op jit(solution)/shard_map/ppermute | solution.py:604
  38.9 2.0 %second.1 = (f32[1584,128]{1,0:T(8,128)S(1)}, f32[1584,128]{1,0:T(8,128)S(1)}, f32[264,128]{1,0:T(8,128)S(1)}, f32[264,128]{1,0:T(8,128)S(1)}, f32[32,128]{1,0:T(8,128)S(1)}, /*index=5*/f32[32,128]{1,0:T(8,128)S(1)}) custom-call(f32[1584,128]{1,0:T(8,128)S(1)} %get-tuple-element.39.prev_ref.v0_ref, f32[1584,128]{1,0:T(8,128)S(1)} %get-tuple-element.40.free_ref, ...), custom_call_target="tpu_custom_call" | custom-call | tf_op jit(solution)/shard_map/second/pallas_call | solution.py:672
  40.9 0.1 collective-permute-start.8
  41.0 5.3 %collective-permute-start.9 = (f32[264,128]{1,0:T(8,128)S(1)}, f32[264,128]{1,0:T(8,128)S(1)}, u32[]{:S(2)}, u32[]{:S(2)}) collective-permute-start(f32[264,128]{1,0:T(8,128)S(1)} %get-tuple-element.47), channel_id=1, source_target_pairs={{1,2},{2,1},{3,4},{4,3},{5,6},{6,5},{7,8},{8,7},{9,10},{10,9},{11,... | collective-permute-start | bytes 405512 | tf_op jit(solution)/shard_map/ppermute | solution.py:604
  46.3 0.0 collective-permute-done.8.from_a
  46.3 2.7 %collective-permute-done.9.from_b = f32[264,128]{1,0:T(8,128)S(1)} collective-permute-done((f32[264,128]{1,0:T(8,128)S(1)}, f32[264,128]{1,0:T(8,128)S(1)}, u32[]{:S(2)}, u32[]{:S(2)}) %collective-permute-start.9) | collective-permute-done | bytes 135200 | tf_op jit(solution)/shard_map/ppermute | solution.py:604
  49.0 1.9 %third.1 = (f32[1584,128]{1,0:T(8,128)S(1)}, f32[32,128]{1,0:T(8,128)S(1)}, f32[32,128]{1,0:T(8,128)S(1)}, f32[32,128]{1,0:T(8,128)S(1)}, f32[32,128]{1,0:T(8,128)S(1)}) custom-call(f32[1584,128]{1,0:T(8,128)S(1)} %get-tuple-element.39.prev_ref.v0_ref, f32[1584,128]{1,0:T(8,128)S(1)} %get-tuple-element.44.v1_ref, ...), custom_call_target="tpu_custom_call" | custom-call | tf_op jit(solution)/shard_map/third/pallas_call | solution.py:680
  50.9 11.0 %all_to_all.21 = f32[32,1,128]{2,1,0:T(1,128)S(1)} all-to-all(f32[32,1,128]{2,1,0:T(1,128)S(1)} %bitcast.10), channel_id=1, replica_groups=mesh['role'=2,'gx'=4,'gy'=4] {'role','gx','gy'}, dimensions={0} | all-to-all | bytes 32768 | tf_op jit(solution)/shard_map/all_to_all | solution.py:687
  61.9 1.4 %combine.1 = (f32[32,128]{1,0:T(8,128)S(1)}, f32[4,3,2,16,128]{4,3,2,1,0:T(8,128)}) custom-call(f32[32,128]{1,0:T(8,128)S(1)} %bitcast.9, f32[1584,128]{1,0:T(8,128)S(1)} %get-tuple-element.39.prev_ref.v0_ref, f32[1584,128]{1,0:T(8,128)S(1)} %get-tuple-element.44.v1_ref, f32[1584,128]{1,0:T(8,128)S(1)} %get-tuple-element.52.v2_ref, ...), custom_call_target="tpu_custom_call" | custom-call | tf_op jit(solution)/shard_map/combine/pallas_call | solution.py:688
  63.2 5.1 %all-to-all-start.2 = ((f32[4,3,2,16,128]{4,3,2,1,0:T(8,128)}), f32[4,3,2,16,128]{4,3,2,1,0:T(8,128)S(1)}, u32[]{:S(2)}, u32[]{:S(2)}) async-start(f32[4,3,2,16,128]{4,3,2,1,0:T(8,128)} %get-tuple-element.59), calls=%async_computation.2 | async-start | bytes 393216 | tf_op jit(solution)/shard_map/all_to_all | solution.py:703
  68.3 1.9 %collective-permute-start.11 = (f32[32,128]{1,0:T(8,128)S(1)}, f32[32,128]{1,0:T(8,128)S(1)}, u32[]{:S(2)}, u32[]{:S(2)}) collective-permute-start(f32[32,128]{1,0:T(8,128)S(1)} %get-tuple-element.57.grad_ref), channel_id=1, source_target_pairs={{1,2},{2,1},{3,4},{4,3},{5,6},{6,5},{7,8},{8,7},{9,10},{10,9},{11,... | collective-permute-start | bytes 49160 | tf_op jit(solution)/shard_map/ppermute | solution.py:604
  70.2 0.6 collective-permute-start.10
  70.8 3.5 %collective-permute-done.11.gb_ref = f32[32,128]{1,0:T(8,128)S(1)} collective-permute-done((f32[32,128]{1,0:T(8,128)S(1)}, f32[32,128]{1,0:T(8,128)S(1)}, u32[]{:S(2)}, u32[]{:S(2)}) %collective-permute-start.11) | collective-permute-done | bytes 16416 | tf_op jit(solution)/shard_map/ppermute | solution.py:604
  74.2 1.9 %last.1 = f32[4,128,128]{2,1,0:T(8,128)} custom-call(f32[32,128]{1,0:T(8,128)S(1)} %get-tuple-element.57.grad_ref, f32[32,128]{1,0:T(8,128)S(1)} %collective-permute-done.10.ga_ref, f32[32,128]{1,0:T(8,128)S(1)} %collective-permute-done.11.gb_ref, f32[8,128,256]{2,1,0:T(8,128)S(1)} %get-tuple-element.58.sw_ref), custom_call_target="tpu_custom_call" | custom-call | tf_op jit(solution)/shard_map/last/pallas_call | solution.py:696
  76.2 0.0 all-to-all-done.2
  76.2 0.7 copy.13
  (9 shorter events, 0.0 us)
Async XLA Ops:
  0.6 1.4 %copy-start = (f32[4,128,128]{2,1,0:T(8,128)S(1)}, f32[4,128,128]{2,1,0:T(8,128)}, u32[]{:S(2)}) copy-start(f32[4,128,128]{2,1,0:T(8,128)} %design_ref) | copy-start | bytes 786436
  2.0 18.2 %collective-permute-start.4 = (f32[4,128,128]{2,1,0:T(8,128)S(1)}, f32[4,128,128]{2,1,0:T(8,128)S(1)}, u32[]{:S(2)}, u32[]{:S(2)}) collective-permute-start(f32[4,128,128]{2,1,0:T(8,128)S(1)} %copy-done), channel_id=1, source_target_pairs={{1,2},{2,1},{3,4},{4,3},{5,6},{6,5},{7,8},{8,7},{9,10},{10,9},{11,... | collective-permute-start | bytes 786440 | tf_op jit(solution)/shard_map/ppermute | solution.py:604
  5.8 14.7 %collective-permute-start.3 = (f32[4,128,128]{2,1,0:T(8,128)S(1)}, f32[4,128,128]{2,1,0:T(8,128)S(1)}, u32[]{:S(2)}, u32[]{:S(2)}) collective-permute-start(f32[4,128,128]{2,1,0:T(8,128)S(1)} %copy-done), channel_id=1, source_target_pairs={{0,1},{1,0},{2,3},{3,2},{4,5},{5,4},{6,7},{7,6},{8,9},{9,8},{10,11... | collective-permute-start | bytes 786440 | tf_op jit(solution)/shard_map/ppermute | solution.py:605
  5.8 5.3 %collective-permute-start.2 = (f32[8,128]{1,0:T(8,128)S(1)}, f32[8,128]{1,0:T(8,128)S(1)}, u32[]{:S(2)}, u32[]{:S(2)}) collective-permute-start(f32[8,128]{1,0:T(8,128)S(1)} %get-tuple-element.36), channel_id=1, source_target_pairs={{20,0},{24,4},{28,8},{4,16},{8,20},{12,24},{21,1},{25,5},{29,9},{5... | collective-permute-start | bytes 12296 | tf_op jit(solution)/shard_map/ppermute | solution.py:621
  7.1 4.0 %collective-permute-start.1 = (f32[48,128]{1,0:T(8,128)S(1)}, f32[48,128]{1,0:T(8,128)S(1)}, u32[]{:S(2)}, u32[]{:S(2)}) collective-permute-start(f32[48,128]{1,0:T(8,128)S(1)} %get-tuple-element.35), channel_id=1, source_target_pairs={{0,16},{16,0},{1,17},{17,1},{2,18},{18,2},{3,19},{19,3},{4,20},{20... | collective-permute-start | bytes 73736 | tf_op jit(solution)/shard_map/ppermute | solution.py:620
  8.5 5.4 %collective-permute-start = (f32[96,128]{1,0:T(8,128)S(1)}, f32[96,128]{1,0:T(8,128)S(1)}, u32[]{:S(2)}, u32[]{:S(2)}) collective-permute-start(f32[96,128]{1,0:T(8,128)S(1)} %get-tuple-element.34), channel_id=1, source_target_pairs={{4,0},{8,4},{12,8},{5,1},{9,5},{13,9},{6,2},{10,6},{14,10},{7,3},{... | collective-permute-start | bytes 147464 | tf_op jit(solution)/shard_map/ppermute | solution.py:619
  9.7 4.1 %copy-start.2 = (s32[3,8,16,128]{3,2,1,0:T(8,128)S(1)}, s32[3,8,16,128]{3,2,1,0:T(8,128)}, u32[]{:S(2)}) copy-start(s32[3,8,16,128]{3,2,1,0:T(8,128)} %mask_ref.1) | copy-start | bytes 589828
  9.9 4.0 %copy-start.1 = (f32[3,8,16,128]{3,2,1,0:T(8,128)S(1)}, f32[3,8,16,128]{3,2,1,0:T(8,128)}, u32[]{:S(2)}) copy-start(f32[3,8,16,128]{3,2,1,0:T(8,128)} %force_ref.1) | copy-start | bytes 589828
  14.8 13.7 %all-to-all-start = ((f32[4,312,128]{2,1,0:T(8,128)}), f32[4,312,128]{2,1,0:T(8,128)S(1)}, u32[]{:S(2)}, u32[]{:S(2)}) async-start(f32[4,312,128]{2,1,0:T(8,128)} %pack.1), calls=%async_computation | async-start | bytes 1277952 | tf_op jit(solution)/shard_map/all_to_all | solution.py:637
  20.6 1.4 %copy-start.4 = (f32[81,81]{1,0:T(8,128)S(1)}, f32[81,81]{1,0:T(8,128)}, u32[]{:S(2)}) copy-start(f32[81,81]{1,0:T(8,128)} %stiff_ref.1) | copy-start | bytes 78736
  20.7 1.3 %copy-start.3 = (f32[120,81]{1,0:T(8,128)S(1)}, f32[120,81]{1,0:T(8,128)}, u32[]{:S(2)}) copy-start(f32[120,81]{1,0:T(8,128)} %constant.10.clone.place_ref) | copy-start | bytes 116644
  20.7 3.3 %collective-permute-start.5 = (f32[1536,8]{0,1:T(8,128)S(1)}, f32[1536,8]{0,1:T(8,128)S(1)}, u32[]{:S(2)}, u32[]{:S(2)}) collective-permute-start(f32[1536,8]{0,1:T(8,128)S(1)} %pad_maximum_fusion), channel_id=1, source_target_pairs={{0,16},{16,0},{1,17},{17,1},{2,18},{18,2},{3,19},{19,3},{4,20},{20... | collective-permute-start | bytes 147464 | tf_op jit(solution)/shard_map/ppermute | solution.py:645
  30.6 5.3 %collective-permute-start.6 = (f32[264,128]{1,0:T(8,128)S(1)}, f32[264,128]{1,0:T(8,128)S(1)}, u32[]{:S(2)}, u32[]{:S(2)}) collective-permute-start(f32[264,128]{1,0:T(8,128)S(1)} %get-tuple-element.42), channel_id=1, source_target_pairs={{0,1},{1,0},{2,3},{3,2},{4,5},{5,4},{6,7},{7,6},{8,9},{9,8},{10,11... | collective-permute-start | bytes 405512 | tf_op jit(solution)/shard_map/ppermute | solution.py:605
  31.7 7.2 %collective-permute-start.7 = (f32[264,128]{1,0:T(8,128)S(1)}, f32[264,128]{1,0:T(8,128)S(1)}, u32[]{:S(2)}, u32[]{:S(2)}) collective-permute-start(f32[264,128]{1,0:T(8,128)S(1)} %get-tuple-element.43), channel_id=1, source_target_pairs={{1,2},{2,1},{3,4},{4,3},{5,6},{6,5},{7,8},{8,7},{9,10},{10,9},{11,... | collective-permute-start | bytes 405512 | tf_op jit(solution)/shard_map/ppermute | solution.py:604
  40.9 5.3 %collective-permute-start.8 = (f32[264,128]{1,0:T(8,128)S(1)}, f32[264,128]{1,0:T(8,128)S(1)}, u32[]{:S(2)}, u32[]{:S(2)}) collective-permute-start(f32[264,128]{1,0:T(8,128)S(1)} %get-tuple-element.46), channel_id=1, source_target_pairs={{0,1},{1,0},{2,3},{3,2},{4,5},{5,4},{6,7},{7,6},{8,9},{9,8},{10,11... | collective-permute-start | bytes 405512 | tf_op jit(solution)/shard_map/ppermute | solution.py:605
  41.0 7.9 %collective-permute-start.9 = (f32[264,128]{1,0:T(8,128)S(1)}, f32[264,128]{1,0:T(8,128)S(1)}, u32[]{:S(2)}, u32[]{:S(2)}) collective-permute-start(f32[264,128]{1,0:T(8,128)S(1)} %get-tuple-element.47), channel_id=1, source_target_pairs={{1,2},{2,1},{3,4},{4,3},{5,6},{6,5},{7,8},{8,7},{9,10},{10,9},{11,... | collective-permute-start | bytes 405512 | tf_op jit(solution)/shard_map/ppermute | solution.py:604
  63.2 13.0 %all-to-all-start.2 = ((f32[4,3,2,16,128]{4,3,2,1,0:T(8,128)}), f32[4,3,2,16,128]{4,3,2,1,0:T(8,128)S(1)}, u32[]{:S(2)}, u32[]{:S(2)}) async-start(f32[4,3,2,16,128]{4,3,2,1,0:T(8,128)} %get-tuple-element.59), calls=%async_computation.2 | async-start | bytes 393216 | tf_op jit(solution)/shard_map/all_to_all | solution.py:703
  68.3 5.9 %collective-permute-start.11 = (f32[32,128]{1,0:T(8,128)S(1)}, f32[32,128]{1,0:T(8,128)S(1)}, u32[]{:S(2)}, u32[]{:S(2)}) collective-permute-start(f32[32,128]{1,0:T(8,128)S(1)} %get-tuple-element.57.grad_ref), channel_id=1, source_target_pairs={{1,2},{2,1},{3,4},{4,3},{5,6},{6,5},{7,8},{8,7},{9,10},{10,9},{11,... | collective-permute-start | bytes 49160 | tf_op jit(solution)/shard_map/ppermute | solution.py:604
  70.2 4.0 %collective-permute-start.10 = (f32[32,128]{1,0:T(8,128)S(1)}, f32[32,128]{1,0:T(8,128)S(1)}, u32[]{:S(2)}, u32[]{:S(2)}) collective-permute-start(f32[32,128]{1,0:T(8,128)S(1)} %get-tuple-element.57.grad_ref), channel_id=1, source_target_pairs={{0,1},{1,0},{2,3},{3,2},{4,5},{5,4},{6,7},{7,6},{8,9},{9,8},{10,11... | collective-permute-start | bytes 49160 | tf_op jit(solution)/shard_map/ppermute | solution.py:605
